TPU v7x, 32 devices: a whole 2x2x4 slice. The times are simulated.
32 devices in a mesh: dp: 8 (over z, y), fsdp: 4 (over x, core).
Axes of the slice: x: 2, y: 2, z: 4, core: 2. Of those that a mesh axis runs over, the one named last changes fastest.
Arguments:
- tokens: bfloat16 [2, 32768, 512], P(None, ('dp', 'fsdp')), may hold values from -6 to 6
- out_grad: bfloat16 [2, 32768, 512], P(None, ('dp', 'fsdp')), may hold values from -6 to 6
- seq_lengths: int32 [2, 32], P(None, ('dp', 'fsdp')), may hold values from 256 to 1024, as said below
- send_to: int32 [2, 32, 8], P(None, ('dp', 'fsdp')), may hold values from 0 to 7, each once within a row
- slot_of: int32 [2, 32, 8], P(None, ('dp', 'fsdp')), may hold values from 0 to 7, each once within a row
- first_gain: bfloat16 [512], P(('dp', 'fsdp')), may hold values from 0.5 to 1.5
- first_shift: bfloat16 [512], P(('dp', 'fsdp')), may hold values from -1.75 to 1.75
- joint_weight: bfloat16 [512, 1536], P(('dp', 'fsdp')), may hold values from -0.25 to 0.25
- query_bias: bfloat16 [512], P(('dp', 'fsdp')), may hold values from -3 to 3
- value_bias: bfloat16 [512], P(('dp', 'fsdp')), may hold values from -1.75 to 1.75
- mix_weight: bfloat16 [512, 512], P(('dp', 'fsdp')), may hold values from -1 to 1
- mix_bias: bfloat16 [512], P(('dp', 'fsdp')), may hold values from -1.75 to 1.75
- second_gain: bfloat16 [512], P(('dp', 'fsdp')), may hold values from 0.5 to 1.5
- second_shift: bfloat16 [512], P(('dp', 'fsdp')), may hold values from -1.75 to 1.75
- up_weight: bfloat16 [512, 2048], P(('dp', 'fsdp')), may hold values from -0.25 to 0.25
- up_bias: bfloat16 [2048], P(('dp', 'fsdp')), may hold values from -3 to 3
- down_weight: bfloat16 [2048, 512], P(None, ('dp', 'fsdp')), may hold values from -0.125 to 0.125
- down_bias: bfloat16 [512], P(('dp', 'fsdp')), may hold values from -1.75 to 1.75
Outputs:
- layer_output: bfloat16 [2, 32768, 512], P(None, ('dp', 'fsdp'))
- input_grad: bfloat16 [2, 32768, 512], P(None, ('dp', 'fsdp'))
- first_gain_grad: float32 [512], P(('dp', 'fsdp'))
- first_shift_grad: float32 [512], P(('dp', 'fsdp'))
- joint_weight_grad: float32 [512, 1536], P(('dp', 'fsdp'))
- query_bias_grad: float32 [512], P(('dp', 'fsdp'))
- value_bias_grad: float32 [512], P(('dp', 'fsdp'))
- mix_weight_grad: float32 [512, 512], P(('dp', 'fsdp'))
- mix_bias_grad: float32 [512], P(('dp', 'fsdp'))
- second_gain_grad: float32 [512], P(('dp', 'fsdp'))
- second_shift_grad: float32 [512], P(('dp', 'fsdp'))
- up_weight_grad: float32 [512, 2048], P(('dp', 'fsdp'))
- up_bias_grad: float32 [2048], P(('dp', 'fsdp'))
- down_weight_grad: float32 [2048, 512], P(None, ('dp', 'fsdp'))
- down_bias_grad: float32 [512], P(('dp', 'fsdp'))
Inputs may be any that keep to these rules, and one draw needn't show every extreme that they name: `seq_lengths`: in every micro-batch some device's sequence fills all 1024 slots; the live slots are the first of a buffer. `send_to`: each row is a permutation: a device sends exactly one piece to each device of its fsdp index. `slot_of`: each row is a permutation: a device receives exactly one piece from each device of its fsdp index.
All inputs are finite; a program needn't handle non-finite values.
Results may differ from a plain program's by a relative error of at most 0.017.
Values may be sent and summed in bfloat16 or wider, within the bound.
A program may use at most 320 MiB of HBM per device.

v0:
```python
import math

import jax
import jax.numpy as jnp
from jax import lax
from jax.sharding import PartitionSpec as P

HEADS = 8
HEAD_DIM = 64


epsilon = 1e-05
masked_score = -1e30
root_half = math.sqrt(0.5)
gauss_norm = 1.0 / math.sqrt(2.0 * math.pi)


def normalize(rows):
    center = rows - jnp.mean(rows, axis=-1, keepdims=True)
    spread = jnp.mean(center * center, axis=-1, keepdims=True)
    factor = lax.rsqrt(spread + epsilon)
    return (center * factor, factor)


def norm_back(grad_norm, normed, factor):
    first_mean = jnp.mean(grad_norm, axis=-1, keepdims=True)
    second_mean = jnp.mean(grad_norm * normed, axis=-1, keepdims=True)
    return factor * (grad_norm - first_mean - normed * second_mean)


def gelu_slope(pre_act):
    return (
        0.5 * (1.0 + lax.erf(pre_act * root_half))
        + pre_act * jnp.exp(-0.5 * pre_act * pre_act) * gauss_norm
    )


def inverse(order):
    count = order.shape[-1]
    hits = order[:, None] == jnp.arange(count, dtype=jnp.int32)[None, :]
    picks = jnp.arange(count, dtype=jnp.int32)[:, None]
    return jnp.sum(jnp.where(hits, picks, 0), axis=0)


def block_scores(query_block, keys, key_live):
    scores = jnp.einsum("qhd,khd->hqk", query_block, keys, preferred_element_type=jnp.float32)
    scores = scores * HEAD_DIM ** (-0.5)
    return jnp.where(key_live[None, None, :], scores, masked_score)


def forward(whole, routed, length):
    (
        first_gain,
        first_shift,
        joint_weight,
        query_bias,
        value_bias,
        mix_weight,
        mix_bias,
        second_gain,
        second_shift,
        up_weight,
        up_bias,
        down_weight,
        down_bias,
    ) = whole
    rows, width = routed.shape
    head_dim = width // HEADS
    key_live = jnp.arange(rows, dtype=jnp.int32) < length
    live = key_live.astype(jnp.float32)[:, None]
    inputs = routed.astype(jnp.float32)
    first_norm, first_factor = normalize(inputs)
    first_in = (
        first_norm * first_gain.astype(jnp.float32) + first_shift.astype(jnp.float32)
    ).astype(jnp.bfloat16)
    joint_bias = jnp.concatenate([query_bias, jnp.zeros_like(query_bias), value_bias]).astype(
        jnp.float32
    )
    joint = (
        jnp.dot(first_in, joint_weight, preferred_element_type=jnp.float32) + joint_bias
    ).astype(jnp.bfloat16)
    queries = joint[:, :width].reshape(rows, HEADS, head_dim)
    keys = joint[:, width : 2 * width].reshape(rows, HEADS, head_dim)
    values = joint[:, 2 * width :].reshape(rows, HEADS, head_dim)
    block = min(512, rows)
    parts = []
    log_totals = []
    for start in range(0, rows, block):
        scores = block_scores(queries[start : start + block], keys, key_live)
        peak = jnp.max(scores, axis=-1, keepdims=True)
        log_total = peak + jnp.log(jnp.sum(jnp.exp(scores - peak), axis=-1, keepdims=True))
        chances = jnp.exp(scores - log_total).astype(jnp.bfloat16)
        parts.append(
            jnp.einsum("hqk,khd->qhd", chances, values, preferred_element_type=jnp.float32).astype(
                jnp.bfloat16
            )
        )
        log_totals.append(log_total)
    attended = jnp.concatenate(parts, axis=0).reshape(rows, width)
    middle = inputs + live * (
        jnp.dot(attended, mix_weight, preferred_element_type=jnp.float32)
        + mix_bias.astype(jnp.float32)
    )
    second_norm, second_factor = normalize(middle)
    second_in = (
        second_norm * second_gain.astype(jnp.float32) + second_shift.astype(jnp.float32)
    ).astype(jnp.bfloat16)
    pre_act = jnp.dot(second_in, up_weight, preferred_element_type=jnp.float32) + up_bias.astype(
        jnp.float32
    )
    hidden = jax.nn.gelu(pre_act, approximate=False).astype(jnp.bfloat16)
    final = middle + live * (
        jnp.dot(hidden, down_weight, preferred_element_type=jnp.float32)
        + down_bias.astype(jnp.float32)
    )
    saved = (
        live,
        key_live,
        first_norm,
        first_factor,
        first_in,
        joint,
        log_totals,
        attended,
        second_norm,
        second_factor,
        second_in,
        pre_act,
        hidden,
    )
    return (final.astype(jnp.bfloat16), saved)


def backward(matrices, saved, routed_grad):
    first_gain, joint_weight, mix_weight, second_gain, up_weight, down_weight = matrices
    (
        live,
        key_live,
        first_norm,
        first_factor,
        first_in,
        joint,
        log_totals,
        attended,
        second_norm,
        second_factor,
        second_in,
        pre_act,
        hidden,
    ) = saved
    rows, width = routed_grad.shape
    head_dim = width // HEADS
    outer_grad = routed_grad.astype(jnp.float32)
    down_in = (live * outer_grad).astype(jnp.bfloat16)
    down_bias_grad = jnp.sum(down_in.astype(jnp.float32), axis=0)
    down_weight_grad = jnp.einsum("rf,rd->fd", hidden, down_in, preferred_element_type=jnp.float32)
    hidden_grad = jnp.einsum("rd,fd->rf", down_in, down_weight, preferred_element_type=jnp.float32)
    pre_grad = (hidden_grad * gelu_slope(pre_act)).astype(jnp.bfloat16)
    up_bias_grad = jnp.sum(pre_grad.astype(jnp.float32), axis=0)
    up_weight_grad = jnp.einsum(
        "rd,rf->df", second_in, pre_grad, preferred_element_type=jnp.float32
    )
    second_in_grad = jnp.einsum(
        "rf,df->rd", pre_grad, up_weight, preferred_element_type=jnp.float32
    )
    second_gain_grad = jnp.sum(second_in_grad * second_norm, axis=0)
    second_shift_grad = jnp.sum(second_in_grad, axis=0)
    middle_grad = outer_grad + norm_back(
        second_in_grad * second_gain.astype(jnp.float32), second_norm, second_factor
    )
    mix_in = (live * middle_grad).astype(jnp.bfloat16)
    mix_bias_grad = jnp.sum(mix_in.astype(jnp.float32), axis=0)
    mix_weight_grad = jnp.einsum("rd,re->de", attended, mix_in, preferred_element_type=jnp.float32)
    attended_grad = jnp.einsum("re,de->rd", mix_in, mix_weight, preferred_element_type=jnp.float32)
    attended_grad = attended_grad.astype(jnp.bfloat16).reshape(rows, HEADS, head_dim)
    queries = joint[:, :width].reshape(rows, HEADS, head_dim)
    keys = joint[:, width : 2 * width].reshape(rows, HEADS, head_dim)
    values = joint[:, 2 * width :].reshape(rows, HEADS, head_dim)
    factor = HEAD_DIM ** (-0.5)
    block = min(512, rows)
    key_grad = jnp.zeros((rows, HEADS, head_dim), jnp.float32)
    value_grad = jnp.zeros((rows, HEADS, head_dim), jnp.float32)
    query_parts = []
    for number, start in enumerate(range(0, rows, block)):
        query_block = queries[start : start + block]
        grad_block = attended_grad[start : start + block]
        chances = jnp.exp(block_scores(query_block, keys, key_live) - log_totals[number])
        chance_grad = jnp.einsum(
            "qhd,khd->hqk", grad_block, values, preferred_element_type=jnp.float32
        )
        inner = jnp.sum(chances * chance_grad, axis=-1, keepdims=True)
        score_grad = (chances * (chance_grad - inner)).astype(jnp.bfloat16)
        query_parts.append(
            jnp.einsum("hqk,khd->qhd", score_grad, keys, preferred_element_type=jnp.float32)
            * factor
        )
        key_grad = (
            key_grad
            + jnp.einsum(
                "hqk,qhd->khd", score_grad, query_block, preferred_element_type=jnp.float32
            )
            * factor
        )
        value_grad = value_grad + jnp.einsum(
            "hqk,qhd->khd",
            chances.astype(jnp.bfloat16),
            grad_block,
            preferred_element_type=jnp.float32,
        )
    query_grad = jnp.concatenate(query_parts, axis=0).reshape(rows, width)
    joint_grad = jnp.concatenate(
        [query_grad, key_grad.reshape(rows, width), value_grad.reshape(rows, width)], axis=1
    ).astype(jnp.bfloat16)
    joint_sums = jnp.sum(joint_grad.astype(jnp.float32), axis=0)
    query_bias_grad = joint_sums[:width]
    value_bias_grad = joint_sums[2 * width :]
    joint_weight_grad = jnp.einsum(
        "rd,re->de", first_in, joint_grad, preferred_element_type=jnp.float32
    )
    first_in_grad = jnp.einsum(
        "re,de->rd", joint_grad, joint_weight, preferred_element_type=jnp.float32
    )
    first_gain_grad = jnp.sum(first_in_grad * first_norm, axis=0)
    first_shift_grad = jnp.sum(first_in_grad, axis=0)
    token_grad = middle_grad + norm_back(
        first_in_grad * first_gain.astype(jnp.float32), first_norm, first_factor
    )
    grads = (
        first_gain_grad,
        first_shift_grad,
        joint_weight_grad,
        query_bias_grad,
        value_bias_grad,
        mix_weight_grad,
        mix_bias_grad,
        second_gain_grad,
        second_shift_grad,
        up_weight_grad,
        up_bias_grad,
        down_weight_grad,
        down_bias_grad,
    )
    return (token_grad.astype(jnp.bfloat16), grads)


def body(
    tokens,
    out_grad,
    seq_lengths,
    send_to,
    slot_of,
    first_gain,
    first_shift,
    joint_weight,
    query_bias,
    value_bias,
    mix_weight,
    mix_bias,
    second_gain,
    second_shift,
    up_weight,
    up_bias,
    down_weight,
    down_bias,
):
    members = lax.axis_size("dp")
    micro, rows, width = tokens.shape
    piece = rows // members
    totals = None
    shares = None
    outputs = []
    token_grads = []
    for step in range(micro):
        sender = inverse(send_to[step, 0])
        placer = inverse(slot_of[step, 0])
        arrived = (
            lax.all_to_all(
                jnp.take(tokens[step].reshape(members, piece, width), sender, axis=0),
                "dp",
                split_axis=0,
                concat_axis=0,
                tiled=True,
            ),
            lax.all_to_all(
                jnp.take(out_grad[step].reshape(members, piece, width), sender, axis=0),
                "dp",
                split_axis=0,
                concat_axis=0,
                tiled=True,
            ),
        )
        routed = jnp.take(arrived[0], placer, axis=0).reshape(rows, width)
        routed_grad = jnp.take(arrived[1], placer, axis=0).reshape(rows, width)
        forward_weights = (
            lax.all_gather(first_gain, ("dp", "fsdp"), axis=0, tiled=True),
            lax.all_gather(first_shift, ("dp", "fsdp"), axis=0, tiled=True),
            lax.all_gather(joint_weight, ("dp", "fsdp"), axis=0, tiled=True),
            lax.all_gather(query_bias, ("dp", "fsdp"), axis=0, tiled=True),
            lax.all_gather(value_bias, ("dp", "fsdp"), axis=0, tiled=True),
            lax.all_gather(mix_weight, ("dp", "fsdp"), axis=0, tiled=True),
            lax.all_gather(mix_bias, ("dp", "fsdp"), axis=0, tiled=True),
            lax.all_gather(second_gain, ("dp", "fsdp"), axis=0, tiled=True),
            lax.all_gather(second_shift, ("dp", "fsdp"), axis=0, tiled=True),
            lax.all_gather(up_weight, ("dp", "fsdp"), axis=0, tiled=True),
            lax.all_gather(up_bias, ("dp", "fsdp"), axis=0, tiled=True),
            lax.all_gather(down_weight, ("dp", "fsdp"), axis=1, tiled=True),
            lax.all_gather(down_bias, ("dp", "fsdp"), axis=0, tiled=True),
        )
        final, saved = forward(forward_weights, routed, seq_lengths[step, 0])
        backward_weights = (
            lax.all_gather(first_gain, ("dp", "fsdp"), axis=0, tiled=True),
            lax.all_gather(joint_weight, ("dp", "fsdp"), axis=0, tiled=True),
            lax.all_gather(mix_weight, ("dp", "fsdp"), axis=0, tiled=True),
            lax.all_gather(second_gain, ("dp", "fsdp"), axis=0, tiled=True),
            lax.all_gather(up_weight, ("dp", "fsdp"), axis=0, tiled=True),
            lax.all_gather(down_weight, ("dp", "fsdp"), axis=1, tiled=True),
        )
        token_grad, grads = backward(backward_weights, saved, routed_grad)
        returned = (
            lax.all_to_all(
                jnp.take(final.reshape(members, piece, width), slot_of[step, 0], axis=0),
                "dp",
                split_axis=0,
                concat_axis=0,
                tiled=True,
            ),
            lax.all_to_all(
                jnp.take(token_grad.reshape(members, piece, width), slot_of[step, 0], axis=0),
                "dp",
                split_axis=0,
                concat_axis=0,
                tiled=True,
            ),
        )
        outputs.append(jnp.take(returned[0], send_to[step, 0], axis=0).reshape(rows, width))
        token_grads.append(jnp.take(returned[1], send_to[step, 0], axis=0).reshape(rows, width))
        totals = (
            grads if totals is None else tuple((left + right for left, right in zip(totals, grads)))
        )
    shares = (
        lax.psum_scatter(totals[0], ("dp", "fsdp"), scatter_dimension=0, tiled=True),
        lax.psum_scatter(totals[1], ("dp", "fsdp"), scatter_dimension=0, tiled=True),
        lax.psum_scatter(totals[2], ("dp", "fsdp"), scatter_dimension=0, tiled=True),
        lax.psum_scatter(totals[3], ("dp", "fsdp"), scatter_dimension=0, tiled=True),
        lax.psum_scatter(totals[4], ("dp", "fsdp"), scatter_dimension=0, tiled=True),
        lax.psum_scatter(totals[5], ("dp", "fsdp"), scatter_dimension=0, tiled=True),
        lax.psum_scatter(totals[6], ("dp", "fsdp"), scatter_dimension=0, tiled=True),
        lax.psum_scatter(totals[7], ("dp", "fsdp"), scatter_dimension=0, tiled=True),
        lax.psum_scatter(totals[8], ("dp", "fsdp"), scatter_dimension=0, tiled=True),
        lax.psum_scatter(totals[9], ("dp", "fsdp"), scatter_dimension=0, tiled=True),
        lax.psum_scatter(totals[10], ("dp", "fsdp"), scatter_dimension=0, tiled=True),
        lax.psum_scatter(totals[11], ("dp", "fsdp"), scatter_dimension=1, tiled=True),
        lax.psum_scatter(totals[12], ("dp", "fsdp"), scatter_dimension=0, tiled=True),
    )
    return (jnp.stack(outputs), jnp.stack(token_grads)) + tuple(shares)


def solution(mesh):
    return jax.shard_map(
        body,
        mesh=mesh,
        in_specs=(
            P(None, ("dp", "fsdp"), None),
            P(None, ("dp", "fsdp"), None),
            P(None, ("dp", "fsdp")),
            P(None, ("dp", "fsdp"), None),
            P(None, ("dp", "fsdp"), None),
            P(("dp", "fsdp")),
            P(("dp", "fsdp")),
            P(("dp", "fsdp"), None),
            P(("dp", "fsdp")),
            P(("dp", "fsdp")),
            P(("dp", "fsdp"), None),
            P(("dp", "fsdp")),
            P(("dp", "fsdp")),
            P(("dp", "fsdp")),
            P(("dp", "fsdp"), None),
            P(("dp", "fsdp")),
            P(None, ("dp", "fsdp")),
            P(("dp", "fsdp")),
        ),
        out_specs=(
            P(None, ("dp", "fsdp"), None),
            P(None, ("dp", "fsdp"), None),
            P(("dp", "fsdp")),
            P(("dp", "fsdp")),
            P(("dp", "fsdp"), None),
            P(("dp", "fsdp")),
            P(("dp", "fsdp")),
            P(("dp", "fsdp"), None),
            P(("dp", "fsdp")),
            P(("dp", "fsdp")),
            P(("dp", "fsdp")),
            P(("dp", "fsdp"), None),
            P(("dp", "fsdp")),
            P(None, ("dp", "fsdp")),
            P(("dp", "fsdp")),
        ),
        check_vma=False,
    )
```

profile of v0, /device:TPU:0, one launch (start us, length us, event | category | flops | bytes accessed | tf_op | source)
XLA Modules:
  0.0 1115.0 jit_solution(3818205105753060365)
XLA Ops:
  17.2 35.7 %all_to_all.40 = bf16[8,128,512]{2,1,0:T(8,128)(2,1)S(1)} all-to-all(bf16[8,128,512]{2,1,0:T(8,128)(2,1)S(1)} %get-tuple-element.131), channel_id=1, replica_groups=mesh['dp'=8,'fsdp'=4] {'dp'}, dimensions={0} | all-to-all | bytes 2097152 | tf_op jit(solution)/shard_map/all_to_all | solution.py:284
  62.8 23.1 %all-to-all-done.2 = bf16[8,128,512]{2,1,0:T(8,128)(2,1)} async-done(((bf16[8,128,512]{2,1,0:T(8,128)(2,1)}), bf16[8,128,512]{2,1,0:T(8,128)(2,1)}, u32[]{:S(2)}, u32[]{:S(2)}) %all-to-all-start.2) | async-done | bytes 1048608 | tf_op jit(solution)/shard_map/all_to_all | solution.py:277
  92.5 46.4 %all-reduce.19 = (bf16[512]{0:T(512)(128)(2,1)S(1)}, bf16[512]{0:T(512)(128)(2,1)S(1)}, bf16[512]{0:T(512)(128)(2,1)S(1)}, bf16[512]{0:T(512)(128)(2,1)S(1)}, bf...) all-reduce(bf16[512]{0:T(512)(128)(2,1)S(1)} %dynamic-update-slice., ...), channel_id=1, replica_groups=mesh['dp'=8,'fsdp'=4] {'dp','fsdp'}, use_global_device_ids=true, to_apply=%add.1 | all-reduce | flops 6144 | bytes 24576
  144.8 5.9 all-to-all-start
  152.1 55.4 %all_gather.31 = bf16[512,512]{1,0:T(8,128)(2,1)} all-gather(bf16[16,512]{1,0:T(8,128)(2,1)S(1)} %copy-done.115), channel_id=1, replica_groups=mesh['dp'=8,'fsdp'=4] {'dp','fsdp'}, dimensions={0}, use_global_device_ids=true | all-gather | bytes 540672 | tf_op jit(solution)/shard_map/all_gather | solution.py:300
  251.2 8.8 fusion
  260.0 10.8 exponential_reduce_fusion.3
  281.8 7.8 fusion.78
  292.5 8.8 fusion.2
  301.3 10.8 exponential_reduce_fusion.1
  323.2 7.7 fusion.80
  340.3 39.9 %fusion.10 = (bf16[1024,2048]{1,0:T(8,128)(2,1)}, bf16[1024,2048]{1,0:T(8,128)(2,1)}, f32[1024,2048]{1,0:T(8,128)}) fusion(f32[2048]{0:T(1024)S(1)} %copy-done.131, f32[1024,2048]{1,0:T(8,128)S(1)} %fusion.125, bf16[512,2048]{1,0:T(8,128)(2,1)S(1)} %copy-done.62, f32[1024,512]{1,0:T(8,128)S(1)} %copy-done.9, f32[512]{0:T(512)S(1)} %copy-done.95, ...), kind=kOutput, calls=%fused_computation.50 | convolution fusion | flops 2426929152 | bytes 29380608 | tf_op jit(solution)/shard_map/dot_general | solution.py:108
  380.2 8.6 convert_reduce_fusion.1
  393.6 9.0 convert_reduce_fusion
  402.7 8.2 convert_reduce_fusion.9
  424.0 25.8 %multiply_reduce_fusion.2 = (f32[8,512]{1,0:T(8,128)S(1)}, f32[8,512]{1,0:T(8,128)S(1)}, f32[8,512,1024]{2,1,0:T(8,128)}) fusion(f32[8,512,1024]{2,1,0:T(8,128)} %copy-done.2, f32[8,512]{1,0:T(8,128)} %copy-done.84, pred[1024]{0:T(1024)(128)(4,1)S(1)} %copy-done.119, f32[8,512,1024]{2,1,0:T(8,128)S(1)} %fusion.137, f32[8,512]{1,0:T(8,128)} %copy-done.92, ...), kind=kOutput, calls=%fused_computation.21 | convolution fusion | flops 578805760 | bytes 68748288 | tf_op jit(solution)/shard_map/qhd,khd->hqk/dot_general | solution.py:188
  449.8 28.9 %multiply_convert_fusion.2 = (bf16[8,512,1024]{2,1,0:T(8,128)(2,1)}, bf16[8,512,1024]{2,1,0:T(8,128)(2,1)}) fusion(f32[8,512,1024]{2,1,0:T(8,128)} %get-tuple-element.148, f32[8,512,1024]{2,1,0:T(8,128)} %copy-done.2, f32[8,512]{1,0:T(8,128)S(1)} %get-tuple-element.32, f32[8,512]{1,0:T(8,128)S(1)} %copy-done.85, pred[1024]{0:T(1024)(128)(4,1)S(1)} %copy-done.119, ...), kind=kLoop, calls=%fused_computation.20 | loop fusion | flops 50331648 | bytes 83952640 | tf_op jit(solution)/shard_map/convert_element_type | solution.py:192
  478.8 7.0 fusion.85
  501.8 25.5 %multiply_reduce_fusion = (f32[8,512]{1,0:T(8,128)}, f32[8,512]{1,0:T(8,128)}, f32[8,512,1024]{2,1,0:T(8,128)}) fusion(f32[8,512,1024]{2,1,0:T(8,128)} %copy-done.3, f32[8,512]{1,0:T(8,128)S(1)} %copy-done.87, pred[1024]{0:T(1024)(128)(4,1)S(1)} %copy-done.122, f32[8,512,1024]{2,1,0:T(8,128)S(1)} %fusion.139, f32[8,512]{1,0:T(8,128)S(1)} %copy-done.91, ...), kind=kOutput, calls=%fused_computation.17 | convolution fusion | flops 578805760 | bytes 68748288 | tf_op jit(solution)/shard_map/qhd,khd->hqk/dot_general | solution.py:188
  527.3 29.1 %multiply_convert_fusion = (bf16[8,512,1024]{2,1,0:T(8,128)(2,1)}, bf16[8,512,1024]{2,1,0:T(8,128)(2,1)}) fusion(f32[8,512,1024]{2,1,0:T(8,128)} %get-tuple-element.147, f32[8,512,1024]{2,1,0:T(8,128)} %copy-done.3, f32[8,512]{1,0:T(8,128)} %get-tuple-element.34, f32[8,512]{1,0:T(8,128)} %copy-done.86, pred[1024]{0:T(1024)(128)(4,1)S(1)} %copy-done.122, ...), kind=kLoop, calls=%fused_computation.16 | loop fusion | flops 50331648 | bytes 83952640 | tf_op jit(solution)/shard_map/convert_element_type | solution.py:192
  556.5 7.0 fusion.83
  568.3 9.8 add_convert_fusion.3
  578.1 7.1 fusion.84
  609.7 7.4 convolution_add_fusion
  626.6 6.3 add_convert_fusion.4
  661.3 29.9 %all_to_all.41 = bf16[8,128,512]{2,1,0:T(8,128)(2,1)} all-to-all(bf16[8,128,512]{2,1,0:T(8,128)(2,1)S(1)} %get-tuple-element.129), channel_id=1, replica_groups=mesh['dp'=8,'fsdp'=4] {'dp'}, dimensions={0} | all-to-all | bytes 2097152 | tf_op jit(solution)/shard_map/all_to_all | solution.py:327
  695.5 6.2 add_convert_fusion.6
  709.4 11.5 %all-to-all-done.3 = bf16[8,128,512]{2,1,0:T(8,128)(2,1)} async-done(((bf16[8,128,512]{2,1,0:T(8,128)(2,1)}), bf16[8,128,512]{2,1,0:T(8,128)(2,1)}, u32[]{:S(2)}, u32[]{:S(2)}) %all-to-all-start.3) | async-done | bytes 1048608 | tf_op jit(solution)/shard_map/all_to_all | solution.py:320
  720.9 29.7 %all_to_all.42 = bf16[8,128,512]{2,1,0:T(8,128)(2,1)} all-to-all(bf16[8,128,512]{2,1,0:T(8,128)(2,1)} %get-tuple-element.123), channel_id=1, replica_groups=mesh['dp'=8,'fsdp'=4] {'dp'}, dimensions={0} | all-to-all | bytes 2097152 | tf_op jit(solution)/shard_map/all_to_all | solution.py:327
  759.1 48.7 %all-reduce.18 = (f32[512]{0:T(512)S(1)}, f32[512]{0:T(512)S(1)}, f32[512]{0:T(512)S(1)}, f32[512]{0:T(512)S(1)}, f32[512]{0:T(512)S(1)}, /*index=5*/f32[512]{0:...) all-reduce(f32[512]{0:T(512)S(1)} %add.328, ...), channel_id=2, replica_groups=mesh['dp'=8,'fsdp'=4] {'dp','fsdp'}, use_global_device_ids=true, to_apply=%region_34.36.clone | all-reduce | flops 6144 | bytes 49152
  824.9 140.7 %reduce-scatter.11.cloned.1.call-done = f32[2048,16]{0,1:T(8,128)} async-done(((f32[2048,512]{0,1:T(8,128)}), f32[2048,16]{0,1:T(8,128)}) %reduce-scatter.11.cloned.1.call-update) | async-done | bytes 131088 | tf_op jit(solution)/shard_map/reduce_scatter | solution.py:352
  965.6 142.0 %reduce-scatter.9.cloned.1.call-done = f32[16,2048]{1,0:T(8,128)} async-done(((f32[512,2048]{1,0:T(8,128)}), f32[16,2048]{1,0:T(8,128)}) %reduce-scatter.9.cloned.1.call-update) | async-done | bytes 131088 | tf_op jit(solution)/shard_map/reduce_scatter | solution.py:350
  (558 shorter events, 248.0 us)
Async XLA Ops:
  7.2 219.9 %all-gather.4.cloned.1.call-start = ((), (), s32[]{:S(2)}) async-start(), calls=%async_computation.12 | async-start | bytes 1622016 | tf_op jit(solution)/shard_map/all_gather | solution.py:297
  7.9 324.7 %all-gather.6.cloned.1.call-start = ((), (), s32[]{:S(2)}) async-start(), calls=%async_computation.13 | async-start | bytes 2162688 | tf_op jit(solution)/shard_map/all_gather | solution.py:304
  53.0 87.7 %copy-start.143 = (s32[2,1]{0,1:T(1,128)S(1)}, s32[2,1]{0,1:T(1,128)}, u32[]{:S(2)}) copy-start(s32[2,1]{0,1:T(1,128)} %param.22) | copy-start | bytes 28
  53.0 91.6 %copy-start.136 = (s32[2,1,8]{2,1,0:T(1,128)S(1)}, s32[2,1,8]{2,1,0:T(1,128)}, u32[]{:S(2)}) copy-start(s32[2,1,8]{2,1,0:T(1,128)} %param.24) | copy-start | bytes 196
  53.0 32.9 %all-to-all-start.2 = ((bf16[8,128,512]{2,1,0:T(8,128)(2,1)}), bf16[8,128,512]{2,1,0:T(8,128)(2,1)}, u32[]{:S(2)}, u32[]{:S(2)}) async-start(bf16[8,128,512]{2,1,0:T(8,128)(2,1)} %get-tuple-element.132), calls=%async_computation.2 | async-start | bytes 2097152 | tf_op jit(solution)/shard_map/all_to_all | solution.py:277
  57.5 94.6 %copy-start.115 = (bf16[16,512]{1,0:T(8,128)(2,1)S(1)}, bf16[16,512]{1,0:T(8,128)(2,1)}, u32[]{:S(2)}) copy-start(bf16[16,512]{1,0:T(8,128)(2,1)} %param.30) | copy-start | bytes 49156
  85.9 58.9 %all-to-all-start.4 = ((bf16[8,128,512]{2,1,0:T(8,128)(2,1)}), bf16[8,128,512]{2,1,0:T(8,128)(2,1)S(1)}, u32[]{:S(2)}, u32[]{:S(2)}) async-start(bf16[8,128,512]{2,1,0:T(8,128)(2,1)} %get-tuple-element.125), calls=%async_computation.4 | async-start | bytes 2097152 | tf_op jit(solution)/shard_map/all_to_all | solution.py:284
  89.5 290.7 %all-gather.8.cloned.1.call-start = ((), (), s32[]{:S(2)}) async-start(), calls=%async_computation.14 | async-start | bytes 2162688 | tf_op jit(solution)/shard_map/all_gather | solution.py:306
  138.9 86.2 %copy-start.109 = (f32[512]{0:T(512)}, f32[512]{0:T(512)S(1)}, u32[]{:S(2)}) copy-start(f32[512]{0:T(512)S(1)} %convert_element_type.248) | copy-start | bytes 6148
  141.9 139.8 %copy-start.118 = (pred[1024]{0:T(1024)(128)(4,1)}, pred[1024]{0:T(1024)(128)(4,1)S(1)}, u32[]{:S(2)}) copy-start(pred[1024]{0:T(1024)(128)(4,1)S(1)} %iota_compare_fusion.3) | copy-start | bytes 3076
  142.6 147.2 %copy-start.106 = (f32[1024]{0:T(1024)}, f32[1024]{0:T(1024)S(1)}, u32[]{:S(2)}) copy-start(f32[1024]{0:T(1024)S(1)} %fusion.100) | copy-start | bytes 12292
  143.9 79.9 %copy-start.99 = (f32[1024]{0:T(1024)}, f32[1024]{0:T(1024)S(1)}, u32[]{:S(2)}) copy-start(f32[1024]{0:T(1024)S(1)} %fusion.101) | copy-start | bytes 12292
  144.8 71.8 %all-to-all-start = ((bf16[8,128,512]{2,1,0:T(8,128)(2,1)}), bf16[8,128,512]{2,1,0:T(8,128)(2,1)}, u32[]{:S(2)}, u32[]{:S(2)}) async-start(bf16[8,128,512]{2,1,0:T(8,128)(2,1)} %get-tuple-element.126), calls=%async_computation | async-start | bytes 2097152 | tf_op jit(solution)/shard_map/all_to_all | solution.py:277
  150.7 674.2 %reduce-scatter.7.cloned.1.call-start = ((), (), s32[]{:S(2)}) async-start(), calls=%async_computation.16 | async-start | bytes 1081344 | tf_op jit(solution)/shard_map/reduce_scatter | solution.py:346
  152.0 70.4 %copy-start.134 = (pred[8]{0:T(512)(128)(4,1)}, pred[8]{0:T(512)(128)(4,1)S(1)}, u32[]{:S(2)}) copy-start(pred[8]{0:T(512)(128)(4,1)S(1)} %compare_and_fusion.6) | copy-start | bytes 28
  152.1 71.7 %copy-start.132 = (pred[8]{0:T(512)(128)(4,1)}, pred[8]{0:T(512)(128)(4,1)S(1)}, u32[]{:S(2)}) copy-start(pred[8]{0:T(512)(128)(4,1)S(1)} %compare_and_fusion.2) | copy-start | bytes 28
  290.7 111.9 %copy-start.80 = (f32[1024]{0:T(1024)}, f32[1024]{0:T(1024)S(1)}, u32[]{:S(2)}) copy-start(f32[1024]{0:T(1024)S(1)} %broadcast_multiply_fusion.9) | copy-start | bytes 12292
  292.4 110.2 %copy-start.82 = (f32[1024]{0:T(1024)}, f32[1024]{0:T(1024)S(1)}, u32[]{:S(2)}) copy-start(f32[1024]{0:T(1024)S(1)} %add_rsqrt_fusion.1) | copy-start | bytes 12292
  332.1 156.6 %copy-start.6 = (f32[1024,512]{1,0:T(8,128)}, f32[1024,512]{1,0:T(8,128)S(1)}, u32[]{:S(2)}) copy-start(f32[1024,512]{1,0:T(8,128)S(1)} %get-tuple-element.145) | copy-start | bytes 6291460
  568.3 256.7 %reduce-scatter.5.cloned.1.call-start = ((), (), s32[]{:S(2)}) async-start(), calls=%async_computation.15 | async-start | bytes 3244032 | tf_op jit(solution)/shard_map/reduce_scatter | solution.py:343
  617.1 348.5 %reduce-scatter.11.cloned.1.call-start = ((), (), s32[]{:S(2)}) async-start(), calls=%async_computation.18 | async-start | bytes 4325376 | tf_op jit(solution)/shard_map/reduce_scatter | solution.py:352
  626.5 481.2 %reduce-scatter.9.cloned.1.call-start = ((), (), s32[]{:S(2)}) async-start(), calls=%async_computation.17 | async-start | bytes 4325376 | tf_op jit(solution)/shard_map/reduce_scatter | solution.py:350
  691.2 29.7 %all-to-all-start.3 = ((bf16[8,128,512]{2,1,0:T(8,128)(2,1)}), bf16[8,128,512]{2,1,0:T(8,128)(2,1)}, u32[]{:S(2)}, u32[]{:S(2)}) async-start(bf16[8,128,512]{2,1,0:T(8,128)(2,1)} %get-tuple-element.130), calls=%async_computation.3 | async-start | bytes 2097152 | tf_op jit(solution)/shard_map/all_to_all | solution.py:320
  701.7 53.6 %copy-start.127 = (f32[512]{0:T(512)S(1)}, f32[512]{0:T(512)}, u32[]{:S(2)}) copy-start(f32[512]{0:T(512)} %get-tuple-element.106) | copy-start | bytes 6148
  701.7 53.6 %copy-start.140 = (f32[512]{0:T(512)S(1)}, f32[512]{0:T(512)}, u32[]{:S(2)}) copy-start(f32[512]{0:T(512)} %get-tuple-element.18) | copy-start | bytes 6148
  701.8 53.6 %copy-start.126 = (f32[512]{0:T(512)S(1)}, f32[512]{0:T(512)}, u32[]{:S(2)}) copy-start(f32[512]{0:T(512)} %get-tuple-element.103) | copy-start | bytes 6148
  701.8 53.6 %copy-start.139 = (f32[512]{0:T(512)S(1)}, f32[512]{0:T(512)}, u32[]{:S(2)}) copy-start(f32[512]{0:T(512)} %get-tuple-element.29) | copy-start | bytes 6148
  701.8 53.6 %copy-start.125 = (f32[512]{0:T(512)S(1)}, f32[512]{0:T(512)}, u32[]{:S(2)}) copy-start(f32[512]{0:T(512)} %get-tuple-element.61) | copy-start | bytes 6148
  701.8 53.6 %copy-start.128 = (f32[512]{0:T(512)S(1)}, f32[512]{0:T(512)}, u32[]{:S(2)}) copy-start(f32[512]{0:T(512)} %get-tuple-element.58) | copy-start | bytes 6148
  701.8 53.6 %copy-start.37 = (bf16[8,64,1024]{2,1,0:T(8,128)(2,1)S(1)}, bf16[8,64,1024]{2,1,0:T(8,128)(2,1)}, u32[]{:S(2)}) copy-start(bf16[8,64,1024]{2,1,0:T(8,128)(2,1)} %copy-done.36) | copy-start | bytes 3145732
  709.4 103.6 %copy-start.49 = (bf16[8,128,512]{2,1,0:T(8,128)(2,1)S(1)}, bf16[8,128,512]{2,1,0:T(8,128)(2,1)}, u32[]{:S(2)}) copy-start(bf16[8,128,512]{2,1,0:T(8,128)(2,1)} %all_to_all.41) | copy-start | bytes 3145732
  750.6 66.8 %all-to-all-start.1 = ((bf16[8,128,512]{2,1,0:T(8,128)(2,1)}), bf16[8,128,512]{2,1,0:T(8,128)(2,1)}, u32[]{:S(2)}, u32[]{:S(2)}) async-start(bf16[8,128,512]{2,1,0:T(8,128)(2,1)} %get-tuple-element.124), calls=%async_computation.1 | async-start | bytes 2097152 | tf_op jit(solution)/shard_map/all_to_all | solution.py:320
  (153 other events, 1754.0 us)
Sparse Core Ops, SparseCore 0:
  10.8 63.5 all-gather.3
  77.3 64.6 all-gather.5
  144.9 61.6 all-gather.7
  568.4 134.7 reduce-scatter.6
  709.0 112.0 reduce-scatter.4
  823.7 141.8 reduce-scatter.10
  968.5 139.0 reduce-scatter.8
where the time goes:
time: 1120 us; the launch traced here: 1110 us
  matrix products  324 us (29%)
  waiting for transfers between devices  319 us (28%)
  blocking collectives  246 us (22%)
  other arithmetic  111 us (10%)
  local copies, waits for them, and re-layouts  74.2 us (7%)
  starting transfers between devices  23 us (2%)
  between operations  17.2 us (2%)
    reduce_scatter x1, waiting for transfers between devices, body(): lax.psum_scatter(totals[9], ('dp', 'fsdp'), scatter_dimension=0, tiled=True)  142 us
    reduce_scatter x1, waiting for transfers between devices, body(): lax.psum_scatter(totals[11], ('dp', 'fsdp'), scatter_dimension=1, tiled=T...  141 us
    unnamed x2, blocking collectives  95.2 us
    all_to_all x2, blocking collectives, body(): lax.all_to_all(jnp.take(token_grad.reshape(members, piece, width), slot_o...  59.6 us
    convert_element_type x2, other arithmetic, backward(): score_grad = (chances * (chance_grad - inner)).astype(jnp.bfloat16)  58.1 us
    dot_general x4, matrix products, backward(): jnp.einsum('qhd,khd->hqk', grad_block, values, preferred_element_type=jnp...  57.3 us
    all_gather x1, blocking collectives, body(): lax.all_gather(mix_weight, ('dp', 'fsdp'), axis=0, tiled=True)  55.4 us
    dot_general x2, matrix products, forward(): jnp.dot(second_in, up_weight, preferred_element_type=jnp.float32)  44.2 us
  transfers between devices with their start and end apart: 12, of which 4 were waited for; matrix products, arithmetic and copies ran while one was open for 28% of the time, Pallas kernels for 0%

commit v1 on v0

v1 whole, which is shorter than its diff:
```python
import functools
import math

import jax
import jax.numpy as jnp
from jax import lax
from jax.experimental import pallas as pl
from jax.experimental.pallas import tpu as pltpu
from jax.sharding import PartitionSpec as P

HEADS = 8
HEAD_DIM = 64
BLK = 256

f32, bf16 = jnp.float32, jnp.bfloat16
epsilon = 1e-05
masked_score = -1e30
root_half = math.sqrt(0.5)
gauss_norm = 1.0 / math.sqrt(2.0 * math.pi)


def nn(a, b):
    return lax.dot_general(a, b, (((1,), (0,)), ((), ())), preferred_element_type=f32)


def nt(a, b):
    return lax.dot_general(a, b, (((1,), (1,)), ((), ())), preferred_element_type=f32)


def tn(a, b):
    return lax.dot_general(a, b, (((0,), (0,)), ((), ())), preferred_element_type=f32)


def normalize(rows):
    center = rows - jnp.mean(rows, axis=-1, keepdims=True)
    spread = jnp.mean(center * center, axis=-1, keepdims=True)
    factor = lax.rsqrt(spread + epsilon)
    return center * factor, factor


def norm_back(grad_norm, normed, factor):
    first_mean = jnp.mean(grad_norm, axis=-1, keepdims=True)
    second_mean = jnp.mean(grad_norm * normed, axis=-1, keepdims=True)
    return factor * (grad_norm - first_mean - normed * second_mean)


def three_parts(v):
    hi = v.astype(bf16).astype(f32)
    mid = (v - hi).astype(bf16).astype(f32)
    return hi, mid, v - hi - mid


def col_sum(v):
    return jnp.sum(v, axis=0, keepdims=True)


def micro_kernel(first, *refs):
    x_ref, g_ref, live_ref, w_ref, vec_ref, upb_ref = refs[:6]
    refs = refs[6:]
    if not first:
        prev_ref, vprev_ref, uprev_ref = refs[:3]
        refs = refs[3:]
    final_ref, tg_ref, grad_ref, vsum_ref, usum_ref = refs[:5]
    (q_ref, k_ref, v_ref, att_ref, qaug_ref, first_t, second_t, down_t, att_t, mixin_ref, mg_ref,
     dout_ref, hid_ref, pre_ref, kaug, vaug_a, vaug_b, dk_acc, dv_acc, acc_a, acc_b) = refs[5:]
    rows, width = x_ref.shape
    hidden = upb_ref.shape[1]
    blocks = rows // BLK
    pairs = width // 128
    mix_at = 3 * width
    up_at = mix_at + width
    down_at = up_at + hidden
    lane = lax.broadcasted_iota(jnp.int32, (1, 128), 1)
    low_half = lane < HEAD_DIM

    def at(i, size=BLK):
        return pl.ds(pl.multiple_of(i * size, size), size)

    if first:
        vsum_ref[...] = jnp.zeros_like(vsum_ref)
        usum_ref[...] = jnp.zeros_like(usum_ref)
    else:
        vsum_ref[...] = vprev_ref[...]
        usum_ref[...] = uprev_ref[...]

    def row(ref, n):
        return ref[n : n + 1, :]

    live_all = live_ref[...]
    mask_aug = jnp.where(
        lane == 0, (live_all - 1.0) * (-masked_score), jnp.where(lane < 4, 1.0, 0.0)
    ).astype(bf16)
    kaug[:, 128:] = mask_aug
    vaug_a[:, 128:] = jnp.ones((rows, 128), bf16)
    vaug_b[:, 128:] = jnp.ones((rows, 128), bf16)

    def project(i, carry):
        rs = at(i)
        normed, _ = normalize(x_ref[rs, :].astype(f32))
        first_in = (normed * row(vec_ref, 0) + row(vec_ref, 1)).astype(bf16)
        first_t[:, rs] = first_in.T
        query = (nn(first_in, w_ref[:, :width]) + row(vec_ref, 2)).astype(bf16)
        q_ref[rs, :] = query * jnp.array(HEAD_DIM ** (-0.5), bf16)
        k_ref[rs, :] = nn(first_in, w_ref[:, width : 2 * width]).astype(bf16)
        v_ref[rs, :] = (nn(first_in, w_ref[:, 2 * width : 3 * width]) + row(vec_ref, 3)).astype(bf16)
        return carry

    lax.fori_loop(0, blocks, project, 0)

    def attend_pair(p, carry):
        ls = at(p, 128)
        kaug[:, :128] = k_ref[:, ls]
        values = v_ref[:, ls]
        zero = jnp.zeros_like(values)
        vaug_a[:, :128] = jnp.where(low_half, values, zero)
        vaug_b[:, :128] = jnp.where(low_half, zero, values)

        def attend(i, carry):
            rs = at(i)
            query = q_ref[rs, ls]
            qzero = jnp.zeros_like(query)
            one = jnp.broadcast_to(jnp.where(lane == 0, 1.0, 0.0), (BLK, 128)).astype(bf16)
            out = None
            for half, vaug in ((0, vaug_a), (1, vaug_b)):
                mine = jnp.where(low_half if half == 0 else jnp.logical_not(low_half), query, qzero)
                scores = nt(jnp.concatenate([mine, one], axis=1), kaug[...])
                peak = jnp.max(scores, axis=-1, keepdims=True)
                chances = jnp.exp(scores - peak).astype(bf16)
                got = nn(chances, vaug[...])
                total = got[:, 128:]
                lse = peak + jnp.log(total)
                hi, mid, lo = three_parts(lse)
                qaug_ref[2 * p + half, rs, :] = jnp.where(
                    lane == 0, 1.0,
                    jnp.where(lane == 1, -hi, jnp.where(lane == 2, -mid, jnp.where(lane == 3, -lo, 0.0))),
                ).astype(bf16)
                part = got[:, :128] / total
                out = part if out is None else out + part
            att_ref[rs, ls] = out
            return carry

        return lax.fori_loop(0, blocks, attend, carry)

    lax.fori_loop(0, pairs, attend_pair, 0)

    chunk = 512
    mix_w = w_ref.at[:, mix_at:up_at]

    def feed(i, carry):
        rs = at(i)
        live = live_ref[rs, :]
        attended = att_ref[rs, :].astype(bf16)
        att_t[:, rs] = attended.T
        middle = x_ref[rs, :].astype(f32) + live * (nn(attended, mix_w[...]) + row(vec_ref, 4))
        second_norm, factor = normalize(middle)
        second_in = (second_norm * row(vec_ref, 5) + row(vec_ref, 6)).astype(bf16)
        second_t[:, rs] = second_in.T
        outer = g_ref[rs, :].astype(f32)
        down_in = (live * outer).astype(bf16)
        down_t[:, rs] = down_in.T
        vsum_ref[7:8, :] += col_sum(down_in.astype(f32))
        acc_a[...] = jnp.zeros_like(acc_a)
        acc_b[...] = jnp.zeros_like(acc_b)

        def part(c, carry):
            cs = at(c, chunk)
            up = w_ref[:, pl.ds(pl.multiple_of(up_at + c * chunk, chunk), chunk)]
            down = w_ref[:, pl.ds(pl.multiple_of(down_at + c * chunk, chunk), chunk)]
            pre = nn(second_in, up) + upb_ref[:, cs]
            phi = 0.5 * (1.0 + lax.erf(pre * root_half))
            hid = (pre * phi).astype(bf16)
            slope = phi + pre * jnp.exp(-0.5 * pre * pre) * gauss_norm
            hid_ref[rs, cs] = hid
            acc_a[...] += nt(hid, down)
            pre_grad = (nn(down_in, down) * slope).astype(bf16)
            pre_ref[rs, cs] = pre_grad
            usum_ref[:, cs] += col_sum(pre_grad.astype(f32))
            acc_b[...] += nt(pre_grad, up)
            return carry

        lax.fori_loop(0, hidden // chunk, part, 0)
        final_ref[rs, :] = (middle + live * (acc_a[...] + row(vec_ref, 7))).astype(bf16)
        second_in_grad = acc_b[...]
        vsum_ref[5:6, :] += col_sum(second_in_grad * second_norm)
        vsum_ref[6:7, :] += col_sum(second_in_grad)
        middle_grad = outer + norm_back(second_in_grad * row(vec_ref, 5), second_norm, factor)
        mg_ref[rs, :] = middle_grad
        mix_in = (live * middle_grad).astype(bf16)
        mixin_ref[rs, :] = mix_in
        vsum_ref[4:5, :] += col_sum(mix_in.astype(f32))
        dout_ref[rs, :] = nt(mix_in, mix_w[...]).astype(bf16)
        return carry

    lax.fori_loop(0, blocks, feed, 0)

    def put(value, cs):
        if not first:
            value = value + prev_ref[:, cs]
        grad_ref[:, cs] = value.astype(grad_ref.dtype)

    def wide(lhs_t, rhs_ref, base, count):
        def one(c, carry):
            put(nn(lhs_t[...], rhs_ref[:, at(c, chunk)]),
                pl.ds(pl.multiple_of(base + c * chunk, chunk), chunk))
            return carry
        lax.fori_loop(0, count, one, 0)

    wide(down_t, hid_ref, down_at, hidden // chunk)
    wide(second_t, pre_ref, up_at, hidden // chunk)
    wide(att_t, mixin_ref, mix_at, width // chunk)

    joint_grad = hid_ref

    def back_pair(p, carry):
        ls = at(p, 128)
        keys = k_ref[:, ls]
        kaug[:, :128] = keys
        vaug_a[:, :128] = v_ref[:, ls]
        vaug_a[:, 128:] = kaug[:, 128:]
        zero = jnp.zeros_like(keys)
        vaug_b[:, :128] = jnp.where(low_half, keys, zero)
        vaug_b[:, 128:] = jnp.where(low_half, zero, keys)
        dk_acc[...] = jnp.zeros_like(dk_acc)
        dv_acc[...] = jnp.zeros_like(dv_acc)

        def back(i, carry):
            rs = at(i)
            query = q_ref[rs, ls]
            grad = dout_ref[rs, ls]
            both = grad.astype(f32) * att_ref[rs, ls]
            dq = None
            for half in (0, 1):
                keep = low_half if half == 0 else jnp.logical_not(low_half)
                mine = jnp.where(keep, query, jnp.zeros_like(query))
                grads = jnp.where(keep, grad, jnp.zeros_like(grad))
                inner = jnp.sum(jnp.where(keep, both, 0.0), axis=-1, keepdims=True)
                hi, mid, lo = three_parts(inner)
                gaug = jnp.where(
                    lane == 1, -hi, jnp.where(lane == 2, -mid, jnp.where(lane == 3, -lo, 0.0))
                ).astype(bf16)
                scores = nt(kaug[...], jnp.concatenate([mine, qaug_ref[2 * p + half, rs, :]], axis=1))
                chances = jnp.exp(scores)
                centered = nt(vaug_a[...], jnp.concatenate([grads, gaug], axis=1))
                score_grad = (chances * centered).astype(bf16)
                dv_acc[...] += nn(chances.astype(bf16), grads)
                dk_acc[...] += nn(score_grad, mine)
                part = tn(score_grad, vaug_b[:, 128 * half : 128 * half + 128])
                dq = part if dq is None else dq + part
            joint_grad[rs, ls] = (dq * HEAD_DIM ** (-0.5)).astype(bf16)
            return carry

        lax.fori_loop(0, blocks, back, 0)
        joint_grad[:, pl.ds(pl.multiple_of(width + p * 128, 128), 128)] = dk_acc[...].astype(bf16)
        joint_grad[:, pl.ds(pl.multiple_of(2 * width + p * 128, 128), 128)] = dv_acc[...].astype(bf16)
        return carry

    lax.fori_loop(0, pairs, back_pair, 0)

    wide(first_t, joint_grad, 0, 3 * width // chunk)

    def back_first(i, carry):
        rs = at(i)
        grads = joint_grad[rs, : 3 * width]
        vsum_ref[2:3, :] += col_sum(grads[:, :width].astype(f32))
        vsum_ref[3:4, :] += col_sum(grads[:, 2 * width :].astype(f32))
        first_in_grad = nt(grads, w_ref[:, : 3 * width])
        normed, factor = normalize(x_ref[rs, :].astype(f32))
        vsum_ref[0:1, :] += col_sum(first_in_grad * normed)
        vsum_ref[1:2, :] += col_sum(first_in_grad)
        tg_ref[rs, :] = (
            mg_ref[rs, :] + norm_back(first_in_grad * row(vec_ref, 0), normed, factor)
        ).astype(bf16)
        return carry

    lax.fori_loop(0, blocks, back_first, 0)


def micro_call(x, g, live, weights, vec, upb, previous=None):
    rows, width = x.shape
    hidden = upb.shape[1]
    columns = weights.shape[1]
    first = previous is None
    vmem = pl.BlockSpec(memory_space=pltpu.VMEM)
    args = (x, g, live, weights, vec, upb) + (() if first else previous)
    scratch = [
        pltpu.VMEM((rows, width), bf16),
        pltpu.VMEM((rows, width), bf16),
        pltpu.VMEM((rows, width), bf16),
        pltpu.VMEM((rows, width), f32),
        pltpu.VMEM((HEADS, rows, 128), bf16),
        pltpu.VMEM((width, rows), bf16),
        pltpu.VMEM((width, rows), bf16),
        pltpu.VMEM((width, rows), bf16),
        pltpu.VMEM((width, rows), bf16),
        pltpu.VMEM((rows, width), bf16),
        pltpu.VMEM((rows, width), f32),
        pltpu.VMEM((rows, width), bf16),
        pltpu.VMEM((rows, hidden), bf16),
        pltpu.VMEM((rows, hidden), bf16),
        pltpu.VMEM((rows, 256), bf16),
        pltpu.VMEM((rows, 256), bf16),
        pltpu.VMEM((rows, 256), bf16),
        pltpu.VMEM((rows, 128), f32),
        pltpu.VMEM((rows, 128), f32),
        pltpu.VMEM((BLK, width), f32),
        pltpu.VMEM((BLK, width), f32),
    ]
    flops = 2 * rows * width * columns * 3 + 7 * 2 * rows * rows * width * 4
    return pl.pallas_call(
        functools.partial(micro_kernel, first),
        out_shape=(
            jax.ShapeDtypeStruct((rows, width), bf16),
            jax.ShapeDtypeStruct((rows, width), bf16),
            jax.ShapeDtypeStruct((width, 4 * width + 2 * hidden), f32 if first else bf16),
            jax.ShapeDtypeStruct((8, width), f32),
            jax.ShapeDtypeStruct((1, hidden), f32),
        ),
        in_specs=[vmem] * len(args),
        out_specs=(vmem,) * 5,
        scratch_shapes=scratch,
        compiler_params=pltpu.CompilerParams(vmem_limit_bytes=63 * 1024 * 1024),
        cost_estimate=pl.CostEstimate(flops=flops, bytes_accessed=30_000_000, transcendentals=3 * HEADS * rows * rows),
        name="micro_first" if first else "micro_second",
    )(*args)


MESH = pl.DeviceIdType.MESH


def split_axes():
    members, others = lax.axis_size("dp"), lax.axis_size("fsdp")
    return members // 2, 2, others // 2, 2


def my_place():
    d, f = lax.axis_index("dp"), lax.axis_index("fsdp")
    return d, f, (d // 2, lax.rem(d, 2), f // 2, lax.rem(f, 2))


def greet(members, others):
    d, f = lax.axis_index("dp"), lax.axis_index("fsdp")
    barrier = pltpu.get_barrier_semaphore()
    for s in range(1, members):
        pl.semaphore_signal(barrier, inc=1, device_id={"dp": lax.rem(d + s, members)}, device_id_type=MESH)
    for s in range(1, others):
        pl.semaphore_signal(barrier, inc=1, device_id={"fsdp": lax.rem(f + s, others)}, device_id_type=MESH)
    pl.semaphore_wait(barrier, members + others - 2)


class Swap:
    def __init__(self, src, dst, local, send, recv, members):
        d = lax.axis_index("dp")
        self.copies = []
        for s in range(1, members):
            to = lax.rem(d + s, members)
            self.copies.append(pltpu.make_async_remote_copy(
                src_ref=src.at[to], dst_ref=dst.at[d], send_sem=send.at[s], recv_sem=recv.at[s],
                device_id={"dp": to}, device_id_type=MESH))
        self.own = pltpu.make_async_copy(src.at[d], dst.at[d], local)

    def start(self):
        for copy in self.copies:
            copy.start()
        self.own.start()

    def wait(self):
        for copy in self.copies:
            copy.wait_recv()
        self.own.wait()

    def wait_sent(self):
        for copy in self.copies:
            copy.wait_send()


class Gather:
    def __init__(self, src, out, cs, order, local, send, recv, sizes):
        a, b, c, e = my_place()[2]
        d, f = lax.axis_index("dp"), lax.axis_index("fsdp")
        high, _, wide, _ = sizes
        every = slice(None)
        place = [a, b, c, e]
        self.own = pltpu.make_async_copy(src.at[:, cs], out.at[a, b, c, e, :, cs], local)
        self.stages = []
        done = [False] * 4
        slot = 0
        for number, axis in enumerate(order):
            copies = []
            size = (high, 2, wide, 2)[axis]
            for s in range(1, size):
                other = lax.rem(place[axis] + s, size)
                if axis == 0:
                    target = {"dp": other * 2 + b}
                elif axis == 1:
                    target = {"dp": a * 2 + other}
                elif axis == 2:
                    target = {"fsdp": other * 2 + e}
                else:
                    target = {"fsdp": c * 2 + other}
                where = tuple(every if done[k] else place[k] for k in range(4)) + (every, cs)
                source = src.at[:, cs] if number == 0 else out.at[where]
                copies.append(pltpu.make_async_remote_copy(
                    src_ref=source, dst_ref=out.at[where], send_sem=send.at[slot], recv_sem=recv.at[slot],
                    device_id=target, device_id_type=MESH))
                slot += 1
            self.stages.append(copies)
            done[axis] = True

    def start(self, number):
        if number == 0:
            self.own.start()
        for copy in self.stages[number]:
            copy.start()

    def wait(self, number):
        for copy in self.stages[number]:
            copy.wait_recv()
        if number == 0:
            self.own.wait()

    def wait_sent(self):
        for stage in self.stages:
            for copy in stage:
                copy.wait_send()


class Reduce:
    def __init__(self, grads, cs, wide_first, emit, scratch, send, recv, high):
        self.grads, self.cs, self.wide_first, self.emit, self.high = grads, cs, wide_first, emit, high
        self.from_core, self.after_core, self.from_one, self.after_one, self.from_two, self.after_two, self.last = scratch
        self.send, self.recv = send, recv
        self.sent = []

    def push(self, source, target, slot, device):
        copy = pltpu.make_async_remote_copy(
            src_ref=source, dst_ref=target, send_sem=self.send.at[slot], recv_sem=self.recv.at[slot],
            device_id=device, device_id_type=MESH)
        copy.start()
        self.sent.append(copy)
        self.copy = copy

    def start(self):
        _, _, (a, b, c, e) = my_place()
        self.push(self.grads.at[:, :, :, 1 - e, :, self.cs], self.from_core, 0, {"fsdp": c * 2 + 1 - e})

    def step(self, number):
        d, f, (a, b, c, e) = my_place()
        across = {"fsdp": (1 - c) * 2 + e}, {"dp": a * 2 + 1 - b}
        if number == 0:
            self.copy.wait_recv()

            def one(i, carry):
                mine = self.grads[i, :, :, e, :, self.cs]
                self.after_core[i] = (mine.astype(f32) + self.from_core[i].astype(f32)).astype(bf16)
                return carry

            lax.fori_loop(0, self.high, one, 0)
            if self.wide_first:
                self.push(self.after_core.at[:, :, 1 - c], self.from_one, 1, across[0])
            else:
                self.push(self.after_core.at[:, 1 - b], self.from_one, 1, across[1])
        elif number == 1:
            self.copy.wait_recv()

            def two(i, carry):
                mine = self.after_core[i, :, c] if self.wide_first else self.after_core[i, b]
                self.after_one[i] = (mine.astype(f32) + self.from_one[i].astype(f32)).astype(bf16)
                return carry

            lax.fori_loop(0, self.high, two, 0)
            if self.wide_first:
                self.push(self.after_one.at[:, 1 - b], self.from_two, 2, across[1])
            else:
                self.push(self.after_one.at[:, 1 - c], self.from_two, 2, across[0])
        elif number == 2:
            self.copy.wait_recv()

            def three(i, carry):
                mine = self.after_one[i, b] if self.wide_first else self.after_one[i, c]
                self.after_two[i] = (mine.astype(f32) + self.from_two[i].astype(f32)).astype(bf16)
                return carry

            lax.fori_loop(0, self.high, three, 0)
            self.copies = []
            for s in range(1, self.high):
                other = lax.rem(a + s, self.high)
                self.push(self.after_two.at[other], self.last.at[a], 2 + s, {"dp": other * 2 + b})
                self.copies.append(self.copy)
        else:
            for copy in self.copies:
                copy.wait_recv()
            total = self.after_two[a].astype(f32)
            for s in range(1, self.high):
                total = total + self.last[lax.rem(a + s, self.high)].astype(f32)
            self.emit(total)

    def wait_sent(self):
        for copy in self.sent:
            copy.wait_send()


def reduce_scratch(high, rows, columns):
    shapes = [(high, 2, 2), (high, 2, 2), (high, 2), (high, 2), (high,), (high,), (high,)]
    return [pltpu.VMEM(lead + (rows, columns), bf16) for lead in shapes]


def gather_kernel(sizes, members, others, ranges, shard, tokens, grads, out, tokens_out, grads_out, wsend, wrecv, tsend, trecv, local):
    greet(members, others)
    micro = tokens.shape[0]
    swaps = []
    for step in range(micro):
        for kind, (src, dst) in enumerate(((tokens, tokens_out), (grads, grads_out))):
            n = step * 2 + kind
            swaps.append(Swap(src.at[step], dst.at[step], local.at[n], tsend.at[n], trecv.at[n], members))
    gathers = [
        Gather(shard, out, cs, order, local.at[2 * micro + n], wsend.at[n], wrecv.at[n], sizes)
        for n, (cs, order) in enumerate(ranges)
    ]
    swaps[0].start()
    for gather in gathers:
        gather.start(0)
    for number in range(1, 4):
        for gather in gathers:
            gather.wait(number - 1)
            gather.start(number)
        if number == 1:
            for swap in swaps[1:]:
                swap.start()
    for gather in gathers:
        gather.wait(3)
    for swap in swaps:
        swap.wait()
    for item in swaps + gathers:
        item.wait_sent()


def scatter_kernel(high, members, others, widths, grads, extra, *refs):
    sources, refs = refs[:4], refs[4:]
    outs, refs = refs[:5], refs[5:]
    returned, refs = refs[:4], refs[4:]
    wsend, wrecv, tsend, trecv, local = refs[-5:]
    scratch = refs[:-5]
    greet(members, others)
    width, hidden = widths
    swaps = [
        Swap(src, dst, local.at[n], tsend.at[n], trecv.at[n], members)
        for n, (src, dst) in enumerate(zip(sources, returned))
    ]

    def emit_first(total):
        outs[0][...] = total[:, : 3 * width]
        outs[1][...] = total[:, 3 * width :]

    def emit_to(ref):
        def emit(total):
            ref[...] = total
        return emit

    up_at, down_at = 4 * width, 4 * width + hidden
    items = [
        Reduce(grads, pl.ds(down_at, hidden), True, emit_to(outs[3]), scratch[0:7], wsend.at[0], wrecv.at[0], high),
        Reduce(grads, pl.ds(up_at, hidden), False, emit_to(outs[2]), scratch[7:14], wsend.at[1], wrecv.at[1], high),
        Reduce(grads, pl.ds(0, up_at), True, emit_first, scratch[14:21], wsend.at[2], wrecv.at[2], high),
        Reduce(extra, pl.ds(0, 128), False, emit_to(outs[4]), scratch[21:28], wsend.at[3], wrecv.at[3], high),
    ]
    for item in items:
        item.start()
    for swap in swaps:
        swap.start()
    for number in range(4):
        for item in items:
            item.step(number)
    for swap in swaps:
        swap.wait()
    for item in items + swaps:
        item.wait_sent()


def order_kernel(scatter, table, *refs):
    count = (len(refs) - 3) // 2
    sources, targets = refs[:count], refs[count : 2 * count]
    held, in_sem, out_sem = refs[2 * count :]
    micro, members = sources[0].shape[:2]
    incoming, outgoing = [], []
    for n in range(count):
        for m in range(micro):
            for p in range(members):
                other = table[m, p]
                src, dst = (p, other) if scatter else (other, p)
                slot = (n * micro + m) * members + p
                copy = pltpu.make_async_copy(sources[n].at[m, src], held.at[slot], in_sem.at[slot])
                copy.start()
                incoming.append(copy)
                outgoing.append(pltpu.make_async_copy(held.at[slot], targets[n].at[m, dst], out_sem.at[slot]))
    for one, two in zip(incoming, outgoing):
        one.wait()
        two.start()
    for two in outgoing:
        two.wait()


ANY = pl.BlockSpec(memory_space=pl.ANY)
VMEM = pl.BlockSpec(memory_space=pltpu.VMEM)


def reorder(scatter, table, *arrays):
    micro, members, piece, width = arrays[0].shape
    slots = len(arrays) * micro * members
    return pl.pallas_call(
        functools.partial(order_kernel, scatter),
        out_shape=tuple(jax.ShapeDtypeStruct(item.shape, item.dtype) for item in arrays),
        in_specs=[pl.BlockSpec(memory_space=pltpu.SMEM)] + [ANY] * len(arrays),
        out_specs=(ANY,) * len(arrays),
        scratch_shapes=[
            pltpu.VMEM((slots, piece, width), arrays[0].dtype),
            pltpu.SemaphoreType.DMA((slots,)),
            pltpu.SemaphoreType.DMA((slots,)),
        ],
        name="order_out" if scatter else "order_in",
    )(table, *arrays)


def gather_call(shard, tokens, grads, members, others):
    rows, columns = shard.shape
    high, wide = members // 2, others // 2
    sizes = (high, 2, wide, 2)
    micro = tokens.shape[0]
    third = 2048
    ranges = (
        (pl.ds(0, third), (0, 1, 2, 3)),
        (pl.ds(third, third), (0, 2, 1, 3)),
        (pl.ds(2 * third, columns - 2 * third), (0, 1, 2, 3)),
    )
    slots = high + 1 + wide
    return pl.pallas_call(
        functools.partial(gather_kernel, sizes, members, others, ranges),
        out_shape=(
            jax.ShapeDtypeStruct(sizes + (rows, columns), shard.dtype),
            jax.ShapeDtypeStruct(tokens.shape, tokens.dtype),
            jax.ShapeDtypeStruct(grads.shape, grads.dtype),
        ),
        in_specs=[VMEM, ANY, ANY],
        out_specs=(ANY,) * 3,
        scratch_shapes=[
            pltpu.SemaphoreType.DMA((len(ranges), slots)),
            pltpu.SemaphoreType.DMA((len(ranges), slots)),
            pltpu.SemaphoreType.DMA((2 * micro, members)),
            pltpu.SemaphoreType.DMA((2 * micro, members)),
            pltpu.SemaphoreType.DMA((2 * micro + len(ranges),)),
        ],
        compiler_params=pltpu.CompilerParams(collective_id=0, has_side_effects=True),
        name="gather_in",
    )(shard, tokens, grads)


def scatter_call(grads, extra, arrays, members, others, width, hidden):
    high = members // 2
    rows = grads.shape[4]
    scratch = []
    for columns in (hidden, hidden, 4 * width, 128):
        scratch += reduce_scratch(high, rows, columns)
    shapes = [(rows, 3 * width), (rows, width), (rows, hidden), (rows, hidden), (rows, 128)]
    return pl.pallas_call(
        functools.partial(scatter_kernel, high, members, others, (width, hidden)),
        out_shape=tuple(jax.ShapeDtypeStruct(shape, f32) for shape in shapes)
        + tuple(jax.ShapeDtypeStruct(item.shape, item.dtype) for item in arrays),
        in_specs=[VMEM, VMEM] + [ANY] * 4,
        out_specs=(VMEM,) * 5 + (ANY,) * 4,
        scratch_shapes=scratch + [
            pltpu.SemaphoreType.DMA((4, high + 2)),
            pltpu.SemaphoreType.DMA((4, high + 2)),
            pltpu.SemaphoreType.DMA((4, members)),
            pltpu.SemaphoreType.DMA((4, members)),
            pltpu.SemaphoreType.DMA((4,)),
        ],
        compiler_params=pltpu.CompilerParams(
            collective_id=1, has_side_effects=True, vmem_limit_bytes=63 * 1024 * 1024),
        name="scatter_out",
    )(grads, extra, *arrays)


def body(
    tokens, out_grad, seq_lengths, send_to, slot_of, first_gain, first_shift, joint_weight, query_bias,
    value_bias, mix_weight, mix_bias, second_gain, second_shift, up_weight, up_bias, down_weight, down_bias,
):
    members, others = lax.axis_size("dp"), lax.axis_size("fsdp")
    devices = members * others
    micro, rows, width = tokens.shape
    piece = rows // members
    own = first_gain.shape[0]
    hidden = down_weight.shape[0]
    per = hidden // width
    vectors = (first_gain, first_shift, query_bias, value_bias, mix_bias, second_gain, second_shift, down_bias)
    small = jnp.concatenate(
        [jnp.stack(vectors, axis=1), up_bias.reshape(own, per), jnp.zeros((own, 128 - 8 - per), bf16)], axis=1)
    shard = jnp.concatenate([joint_weight, mix_weight, up_weight, down_weight.T, small], axis=1)
    table = send_to[:, 0]
    pieces = (micro, members, piece, width)
    sent = reorder(True, table, tokens.reshape(pieces), out_grad.reshape(pieces))
    gathered, routed, routed_grad = gather_call(shard, *sent, members, others)
    whole = gathered.reshape(width, shard.shape[1])
    tail = whole[:, 4 * width + 2 * hidden :].astype(f32)
    vec = tail[:, :8].T
    upb = tail[:, 8 : 8 + per].reshape(1, hidden)
    spots = slot_of[:, 0, :, None] * piece + jnp.arange(piece, dtype=jnp.int32)
    live = (spots.reshape(micro, rows) < seq_lengths).astype(f32)[:, :, None]
    previous = None
    results = []
    for step in range(micro):
        final, token_grad, *previous = micro_call(
            routed[step].reshape(rows, width), routed_grad[step].reshape(rows, width), live[step], whole, vec, upb,
            previous and tuple(previous))
        results += [final.reshape(members, piece, width), token_grad.reshape(members, piece, width)]
    total, vsum, usum = previous
    sizes = (members // 2, 2, others // 2, 2, own)
    grads = total.reshape(sizes + (total.shape[1],))
    extra = jnp.concatenate(
        [vsum.T, usum.reshape(width, per), jnp.zeros((width, 128 - 8 - per), f32)], axis=1
    ).astype(bf16).reshape(sizes + (128,))
    joint, mix, up, down, tail, *returned = scatter_call(grads, extra, results, members, others, width, hidden)
    layer_output, input_grad = reorder(
        False, table, jnp.stack([returned[0], returned[2]]), jnp.stack([returned[1], returned[3]]))
    vec_grad = [tail[:, n] for n in range(8)]
    return (
        layer_output.reshape(tokens.shape), input_grad.reshape(tokens.shape),
        vec_grad[0], vec_grad[1], joint, vec_grad[2], vec_grad[3], mix, vec_grad[4], vec_grad[5], vec_grad[6],
        up, tail[:, 8 : 8 + per].reshape(up_bias.shape), down.T, vec_grad[7],
    )


def solution(mesh):
    both = ("dp", "fsdp")
    row3, row2, vector, matrix = P(None, both, None), P(None, both), P(both), P(both, None)
    turned = P(None, both)
    return jax.shard_map(
        body,
        mesh=mesh,
        in_specs=(row3, row3, row2, row3, row3, vector, vector, matrix, vector, vector, matrix, vector, vector,
                  vector, matrix, vector, turned, vector),
        out_specs=(row3, row3, vector, vector, matrix, vector, vector, matrix, vector, vector, vector, matrix,
                   vector, turned, vector),
        check_vma=False,
    )
```

time: 1120 us -> 454 us (0.41)
  Pallas kernels: 0 us -> 431 us
  matrix products: 324 us -> 0 us
  waiting for transfers between devices: 319 us -> 0 us
  blocking collectives: 246 us -> 0 us
  other arithmetic: 111 us -> 7.01 us
  local copies, waits for them, and re-layouts: 74.2 us -> 15.3 us
  starting transfers between devices: 23 us -> 0 us
  between operations: 17.2 us -> 0.98 us
    pallas_call x0 -> x6, Pallas kernels: none -> 431 us  [the longest x2 187 us: micro_call(): pl.pallas_call(functools.partial(micro_kernel, first), out_shape=(jax.Sha...]
    dot_general x48 -> x0, matrix products: 324 us -> none  [the longest x4 57.3 us: backward(): jnp.einsum('qhd,khd->hqk', grad_block, values, preferred_element_type=jnp...]
    reduce_scatter x4 -> x0, waiting for transfers between devices: 283 us -> none  [the longest x1 142 us: body(): lax.psum_scatter(totals[9], ('dp', 'fsdp'), scatter_dimension=0, tiled=True)]
    all_to_all x3 -> x0, blocking collectives: 95.3 us -> none  [the longest x2 59.6 us: body(): lax.all_to_all(jnp.take(token_grad.reshape(members, piece, width), slot_o...]
    unnamed x2 -> x0, blocking collectives: 95.2 us -> none
    convert_element_type x18 -> x2, other arithmetic: 67.9 us -> 0.09 us  [the longest x1 0.07 us: body(): live = (spots.reshape(micro, rows) < seq_lengths).astype(f32)[:, :, None]]
    all_gather x1 -> x0, blocking collectives: 55.4 us -> none  [body(): lax.all_gather(mix_weight, ('dp', 'fsdp'), axis=0, tiled=True)]
    all_to_all x5 -> x0, waiting for transfers between devices: 34.6 us -> none  [the longest x2 23.1 us: body(): lax.all_to_all(jnp.take(tokens[step].reshape(members, piece, width), send...]
  transfers between devices with their start and end apart: 12 -> 0, of which waited for: 4 -> 0; matrix products, arithmetic and copies ran while one was open for 28% -> 0% of each run, Pallas kernels for 0% -> 0%
where the time goes in v1:
time: 454 us
  Pallas kernels  431 us (95%)
  local copies, waits for them, and re-layouts  15.3 us (3%)
  other arithmetic  7.01 us (2%)
    pallas_call x2, Pallas kernels, micro_call(): pl.pallas_call(functools.partial(micro_kernel, first), out_shape=(jax.Sha...  187 us
    pallas_call x1, Pallas kernels, scatter_call(): pl.pallas_call(functools.partial(scatter_kernel, high, members, others, (...  123 us
    pallas_call x1, Pallas kernels, gather_call(): pl.pallas_call(functools.partial(gather_kernel, sizes, members, others, r...  110 us
    pallas_call x2, Pallas kernels, reorder(): pl.pallas_call(functools.partial(order_kernel, scatter), out_shape=tuple(...  10.7 us

profile of v1, /device:TPU:0, one launch (start us, length us, event | category | flops | bytes accessed | tf_op | source)
XLA Modules:
  0.0 454.1 jit_solution(15368256012763704010)
XLA Ops:
  0.8 5.3 %order_out.1 = (bf16[2,8,128,512]{3,2,1,0:T(8,128)(2,1)}, bf16[2,8,128,512]{3,2,1,0:T(8,128)(2,1)}) custom-call(s32[2,8]{1,0:T(2,128)} %bitcast.66, bf16[2,8,128,512]{3,2,1,0:T(8,128)(2,1)} %bitcast.49, bf16[2,8,128,512]{3,2,1,0:T(8,128)(2,1)} %bitcast.50), custom_call_target="tpu_custom_call" | custom-call | tf_op jit(solution)/shard_map/order_out/pallas_call | solution.py:609
  6.1 0.1 copy.46
  6.2 0.1 copy.47
  6.4 0.1 copy.49
  6.9 0.1 reshape.93
  7.1 0.8 concatenate.12.shard
  7.8 110.5 %gather_in.1 = (bf16[4,2,2,2,16,6272]{5,4,3,2,1,0:T(8,128)(2,1)}, bf16[2,8,128,512]{3,2,1,0:T(8,128)(2,1)}, bf16[2,8,128,512]{3,2,1,0:T(8,128)(2,1)}) custom-call(bf16[16,6272]{1,0:T(8,128)(2,1)} %concatenate.12.shard, bf16[2,8,128,512]{3,2,1,0:T(8,128)(2,1)} %get-tuple-element.41.tokens, bf16[2,8,128,512]{3,2,1,0:T(8,128)(2,1)} %get-tuple-element.42.grads), custom_call_target="tpu_custom_call" | custom-call | tf_op jit(solution)/shard_map/gather_in/pallas_call | solution.py:635
  118.4 4.3 fusion
  122.6 0.9 slice.75
  123.6 0.1 copy.59
  123.7 0.1 copy.55
  123.8 0.8 reshape.97.refs_5_
  124.6 0.6 slice_bitcast_fusion.refs_4_
  125.4 1.0 copy.56.refs_2_
  126.5 92.5 %micro_first.1 = (bf16[1024,512]{1,0:T(8,128)(2,1)}, bf16[1024,512]{1,0:T(8,128)(2,1)}, f32[512,6144]{1,0:T(8,128)}, f32[8,512]{1,0:T(8,128)}, f32[1,2048]{1,0:T(1,128)}) custom-call(bf16[1024,512]{1,0:T(8,128)(2,1)} %bitcast.62, bf16[1024,512]{1,0:T(8,128)(2,1)} %bitcast.61, f32[1024,1]{1,0:T(8,128)} %copy.56.refs_2_, bf16[512,6272]{1,0:T(8,128)(2,1)} %bitcast.70, ...), custom_call_target="tpu_custom_call" | custom-call | flops 49794777088 | bytes 30000000 | tf_op jit(solution)/shard_map/micro_first/pallas_call | solution.py:309
  218.9 1.1 copy.57.refs_2_
  220.0 94.5 %micro_second.1 = (bf16[1024,512]{1,0:T(8,128)(2,1)}, bf16[1024,512]{1,0:T(8,128)(2,1)}, bf16[512,6144]{1,0:T(8,128)(2,1)}, f32[8,512]{1,0:T(8,128)}, f32[1,2048]{1,0:T(1,128)}) custom-call(bf16[1024,512]{1,0:T(8,128)(2,1)} %bitcast.58, bf16[1024,512]{1,0:T(8,128)(2,1)} %bitcast.57, f32[1024,1]{1,0:T(8,128)} %copy.57.refs_2_, bf16[512,6272]{1,0:T(8,128)(2,1)} %bitcast.71, ...), custom_call_target="tpu_custom_call" | custom-call | flops 49794777088 | bytes 30000000 | tf_op jit(solution)/shard_map/micro_second/pallas_call | solution.py:309
  314.5 0.7 convert_bitcast_fusion
  315.2 0.2 copy.58
  315.3 0.7 convert_reduce_fusion
  316.1 0.3 concatenate.14
  316.5 0.8 maximum_maximum_fusion.extra
  317.2 122.7 %scatter_out.1 = (f32[16,1536]{1,0:T(8,128)}, f32[16,512]{1,0:T(8,128)}, f32[16,2048]{1,0:T(8,128)}, f32[16,2048]{1,0:T(8,128)}, f32[16,128]{1,0:T(8,128)}, /*in...) custom-call(bf16[4,2,2,2,16,6144]{5,4,3,2,1,0:T(8,128)(2,1)} %bitcas, ...), custom_call_target="tpu_custom_call" | custom-call | tf_op jit(solution)/shard_map/scatter_out/pallas_call | solution.py:663
  439.9 3.2 pad_maximum_fusion.1.refs_1_
  443.2 1.5 pad_maximum_fusion.refs_0_
  444.7 5.3 %order_in.1 = (bf16[2,8,128,512]{3,2,1,0:T(8,128)(2,1)}, bf16[2,8,128,512]{3,2,1,0:T(8,128)(2,1)}) custom-call(s32[2,8]{1,0:T(2,128)} %bitcast.67, bf16[2,8,128,512]{3,2,1,0:T(8,128)(2,1)} %pad_maximum_fusion.refs_0_, bf16[2,8,128,512]{3,2,1,0:T(8,128)(2,1)} %pad_maximum_fusion.1.refs_1_), custom_call_target="tpu_custom_call" | custom-call | tf_op jit(solution)/shard_map/order_in/pallas_call | solution.py:609
  450.1 0.6 reshape.105
  450.7 0.8 slice_reduce_fusion
  451.5 0.6 copy.66
  452.2 0.6 copy.67
  452.8 0.7 copy.68
  453.4 0.7 copy.69
  (60 shorter events, 0.9 us)
Async XLA Ops:
  0.7 5.5 %copy-start.12 = (bf16[16]{0:T(256)(128)(2,1)S(1)}, bf16[16]{0:T(256)(128)(2,1)}, u32[]{:S(2)}) copy-start(bf16[16]{0:T(256)(128)(2,1)} %param.23) | copy-start | bytes 100
  0.7 5.6 %copy-start.13 = (bf16[16]{0:T(256)(128)(2,1)S(1)}, bf16[16]{0:T(256)(128)(2,1)}, u32[]{:S(2)}) copy-start(bf16[16]{0:T(256)(128)(2,1)} %param.24) | copy-start | bytes 100
  0.7 5.7 %copy-start.14 = (bf16[16]{0:T(256)(128)(2,1)S(1)}, bf16[16]{0:T(256)(128)(2,1)}, u32[]{:S(2)}) copy-start(bf16[16]{0:T(256)(128)(2,1)} %param.26) | copy-start | bytes 100
  0.7 5.7 %copy-start.15 = (bf16[16]{0:T(256)(128)(2,1)S(1)}, bf16[16]{0:T(256)(128)(2,1)}, u32[]{:S(2)}) copy-start(bf16[16]{0:T(256)(128)(2,1)} %param.27) | copy-start | bytes 100
  0.7 5.8 %copy-start.16 = (bf16[16]{0:T(256)(128)(2,1)S(1)}, bf16[16]{0:T(256)(128)(2,1)}, u32[]{:S(2)}) copy-start(bf16[16]{0:T(256)(128)(2,1)} %param.29) | copy-start | bytes 100
  0.7 5.9 %copy-start.17 = (bf16[16]{0:T(256)(128)(2,1)S(1)}, bf16[16]{0:T(256)(128)(2,1)}, u32[]{:S(2)}) copy-start(bf16[16]{0:T(256)(128)(2,1)} %param.30) | copy-start | bytes 100
  0.7 6.0 %copy-start.18 = (bf16[16]{0:T(256)(128)(2,1)S(1)}, bf16[16]{0:T(256)(128)(2,1)}, u32[]{:S(2)}) copy-start(bf16[16]{0:T(256)(128)(2,1)} %param.31) | copy-start | bytes 100
  0.7 6.1 %copy-start.19 = (bf16[16]{0:T(256)(128)(2,1)S(1)}, bf16[16]{0:T(256)(128)(2,1)}, u32[]{:S(2)}) copy-start(bf16[16]{0:T(256)(128)(2,1)} %param.35) | copy-start | bytes 100
  0.7 6.2 %copy-start.20 = (bf16[64]{0:T(256)(128)(2,1)S(1)}, bf16[64]{0:T(256)(128)(2,1)}, u32[]{:S(2)}) copy-start(bf16[64]{0:T(256)(128)(2,1)} %param.33) | copy-start | bytes 388
  0.7 6.3 %copy-start.6 = (bf16[16,2048]{1,0:T(8,128)(2,1)S(1)}, bf16[16,2048]{1,0:T(8,128)(2,1)}, u32[]{:S(2)}) copy-start(bf16[16,2048]{1,0:T(8,128)(2,1)} %param.32) | copy-start | bytes 196612
  0.8 6.3 %copy-start.7 = (bf16[2048,16]{0,1:T(8,128)(2,1)S(1)}, bf16[2048,16]{0,1:T(8,128)(2,1)}, u32[]{:S(2)}) copy-start(bf16[2048,16]{0,1:T(8,128)(2,1)} %param.34) | copy-start | bytes 196612
  0.8 6.3 %copy-start.8 = (bf16[16,1536]{1,0:T(8,128)(2,1)S(1)}, bf16[16,1536]{1,0:T(8,128)(2,1)}, u32[]{:S(2)}) copy-start(bf16[16,1536]{1,0:T(8,128)(2,1)} %param.25) | copy-start | bytes 147460
  0.8 6.3 %copy-start.10 = (bf16[16,512]{1,0:T(8,128)(2,1)S(1)}, bf16[16,512]{1,0:T(8,128)(2,1)}, u32[]{:S(2)}) copy-start(bf16[16,512]{1,0:T(8,128)(2,1)} %param.28) | copy-start | bytes 49156
  118.3 6.9 %copy-start.11 = (s32[2,1,8]{2,1,0:T(1,128)S(1)}, s32[2,1,8]{2,1,0:T(1,128)}, u32[]{:S(2)}) copy-start(s32[2,1,8]{2,1,0:T(1,128)} %param.22) | copy-start | bytes 196
  118.3 7.0 %copy-start.21 = (s32[2,1]{0,1:T(1,128)S(1)}, s32[2,1]{0,1:T(1,128)}, u32[]{:S(2)}) copy-start(s32[2,1]{0,1:T(1,128)} %param.20) | copy-start | bytes 28
  439.9 3.2 copy-start
  439.9 3.2 copy-start.1
  444.6 5.4 %copy-start.2 = (f32[16,128]{1,0:T(8,128)S(1)}, f32[16,128]{1,0:T(8,128)}, u32[]{:S(2)}) copy-start(f32[16,128]{1,0:T(8,128)} %get-tuple-element.62) | copy-start | bytes 24580
  444.7 6.9 %copy-start.5 = (f32[16,1536]{1,0:T(8,128)S(1)}, f32[16,1536]{1,0:T(8,128)}, u32[]{:S(2)}) copy-start(f32[16,1536]{1,0:T(8,128)} %get-tuple-element.102) | copy-start | bytes 294916
  444.7 7.5 %copy-start.9 = (f32[16,512]{1,0:T(8,128)S(1)}, f32[16,512]{1,0:T(8,128)}, u32[]{:S(2)}) copy-start(f32[16,512]{1,0:T(8,128)} %get-tuple-element.105) | copy-start | bytes 98308
  444.7 8.1 %copy-start.4 = (f32[16,2048]{1,0:T(8,128)S(1)}, f32[16,2048]{1,0:T(8,128)}, u32[]{:S(2)}) copy-start(f32[16,2048]{1,0:T(8,128)} %get-tuple-element.109) | copy-start | bytes 393220
  444.7 8.8 %copy-start.3 = (f32[16,2048]{1,0:T(8,128)S(1)}, f32[16,2048]{1,0:T(8,128)}, u32[]{:S(2)}) copy-start(f32[16,2048]{1,0:T(8,128)} %get-tuple-element.66) | copy-start | bytes 393220

commit v2 on v1

--- a/solution.py
+++ b/solution.py
@@ -318,7 +318,7 @@
         in_specs=[vmem] * len(args),
         out_specs=(vmem,) * 5,
         scratch_shapes=scratch,
-        compiler_params=pltpu.CompilerParams(vmem_limit_bytes=63 * 1024 * 1024),
+        compiler_params=pltpu.CompilerParams(vmem_limit_bytes=67_043_328),
         cost_estimate=pl.CostEstimate(flops=flops, bytes_accessed=30_000_000, transcendentals=3 * HEADS * rows * rows),
         name="micro_first" if first else "micro_second",
     )(*args)
@@ -674,7 +674,7 @@
             pltpu.SemaphoreType.DMA((4,)),
         ],
         compiler_params=pltpu.CompilerParams(
-            collective_id=1, has_side_effects=True, vmem_limit_bytes=63 * 1024 * 1024),
+            collective_id=1, has_side_effects=True, vmem_limit_bytes=67_043_328),
         name="scatter_out",
     )(grads, extra, *arrays)
 
@@ -728,12 +728,659 @@
     )
 
 
+SMALL = 256
+
+
+class Layer:
+    def __init__(self, x, g, live, weight, offsets, vec, upb, final, tg, put, vsum, usum, scratch):
+        self.x, self.g, self.live, self.weight, self.offsets = x, g, live, weight, offsets
+        self.vec, self.upb, self.final, self.tg, self.put, self.vsum, self.usum = vec, upb, final, tg, put, vsum, usum
+        (self.q, self.k, self.v, self.att, self.qaug, self.first_t, self.second_t, self.down_t, self.att_t, self.mixin,
+         self.mg, self.dout, self.hid, self.pre, self.kaug, self.vaug_a, self.vaug_b, self.dk, self.dv, self.acc_a,
+         self.acc_b) = scratch
+        self.rows, self.width = self.q.shape
+        self.hidden = upb.shape[1]
+        self.blocks = self.rows // BLK
+        self.pairs = self.width // 128
+        self.lane = lax.broadcasted_iota(jnp.int32, (1, 128), 1)
+        self.low = self.lane < HEAD_DIM
+
+    def at(self, i, size=BLK):
+        return pl.ds(pl.multiple_of(i * size, size), size)
+
+    def row(self, n):
+        return self.vec[n : n + 1, :]
+
+    def load(self, ref, i):
+        per = BLK // ref.shape[1]
+        return ref[pl.ds(i * per, per)].reshape(BLK, self.width)
+
+    def save(self, ref, i, value):
+        per = BLK // ref.shape[1]
+        ref[pl.ds(i * per, per)] = value.reshape(per, ref.shape[1], self.width)
+
+    def masks(self):
+        rows, lane = self.rows, self.lane
+        self.kaug[:, 128:] = jnp.where(
+            lane == 0, (self.live[...] - 1.0) * (-masked_score), jnp.where(lane < 4, 1.0, 0.0)
+        ).astype(bf16)
+        self.vaug_a[:, 128:] = jnp.ones((rows, 128), bf16)
+        self.vaug_b[:, 128:] = jnp.ones((rows, 128), bf16)
+
+    def project(self):
+        width = self.width
+
+        def one(i, carry):
+            rs = self.at(i)
+            normed, _ = normalize(self.load(self.x, i).astype(f32))
+            first_in = (normed * self.row(0) + self.row(1)).astype(bf16)
+            self.first_t[:, rs] = first_in.T
+            query = (nn(first_in, self.weight(0, width)) + self.row(2)).astype(bf16)
+            self.q[rs, :] = query * jnp.array(HEAD_DIM ** (-0.5), bf16)
+            self.k[rs, :] = nn(first_in, self.weight(width, width)).astype(bf16)
+            self.v[rs, :] = (nn(first_in, self.weight(2 * width, width)) + self.row(3)).astype(bf16)
+            return carry
+
+        lax.fori_loop(0, self.blocks, one, 0)
+
+    def attend(self, hook):
+        lane, low = self.lane, self.low
+
+        def pair(p, carry):
+            ls = self.at(p, 128)
+            self.kaug[:, :128] = self.k[:, ls]
+            values = self.v[:, ls]
+            zero = jnp.zeros_like(values)
+            self.vaug_a[:, :128] = jnp.where(low, values, zero)
+            self.vaug_b[:, :128] = jnp.where(low, zero, values)
+
+            def one(i, carry):
+                rs = self.at(i)
+                query = self.q[rs, ls]
+                qzero = jnp.zeros_like(query)
+                lead = jnp.broadcast_to(jnp.where(lane == 0, 1.0, 0.0), (BLK, 128)).astype(bf16)
+                out = None
+                for half, vaug in ((0, self.vaug_a), (1, self.vaug_b)):
+                    mine = jnp.where(low if half == 0 else jnp.logical_not(low), query, qzero)
+                    scores = nt(jnp.concatenate([mine, lead], axis=1), self.kaug[...])
+                    peak = jnp.max(scores, axis=-1, keepdims=True)
+                    chances = jnp.exp(scores - peak).astype(bf16)
+                    got = nn(chances, vaug[...])
+                    total = got[:, 128:]
+                    hi, mid, lo = three_parts(peak + jnp.log(total))
+                    self.qaug[2 * p + half, rs, :] = jnp.where(
+                        lane == 0, 1.0,
+                        jnp.where(lane == 1, -hi, jnp.where(lane == 2, -mid, jnp.where(lane == 3, -lo, 0.0))),
+                    ).astype(bf16)
+                    part = got[:, :128] / total
+                    out = part if out is None else out + part
+                self.att[rs, ls] = out
+                return carry
+
+            lax.fori_loop(0, self.blocks, one, carry)
+            hook(p)
+            return carry
+
+        lax.fori_loop(0, self.pairs, pair, 0)
+
+    def feed(self):
+        chunk = 512
+        mix_at, up_at, down_at = self.offsets
+
+        def one(i, carry):
+            rs = self.at(i)
+            live = self.live[rs, :]
+            attended = self.att[rs, :].astype(bf16)
+            self.att_t[:, rs] = attended.T
+            mix_w = self.weight(mix_at, self.width)
+            middle = self.load(self.x, i).astype(f32) + live * (nn(attended, mix_w) + self.row(4))
+            second_norm, factor = normalize(middle)
+            second_in = (second_norm * self.row(5) + self.row(6)).astype(bf16)
+            self.second_t[:, rs] = second_in.T
+            outer = self.load(self.g, i).astype(f32)
+            down_in = (live * outer).astype(bf16)
+            self.down_t[:, rs] = down_in.T
+            self.vsum[7:8, :] += col_sum(down_in.astype(f32))
+            self.acc_a[...] = jnp.zeros_like(self.acc_a)
+            self.acc_b[...] = jnp.zeros_like(self.acc_b)
+
+            def part(c, carry):
+                cs = self.at(c, chunk)
+                up = self.weight(pl.multiple_of(up_at + c * chunk, 128), chunk)
+                down = self.weight(pl.multiple_of(down_at + c * chunk, 128), chunk)
+                pre = nn(second_in, up) + self.upb[:, cs]
+                phi = 0.5 * (1.0 + lax.erf(pre * root_half))
+                hid = (pre * phi).astype(bf16)
+                slope = phi + pre * jnp.exp(-0.5 * pre * pre) * gauss_norm
+                self.hid[rs, cs] = hid
+                self.acc_a[...] += nt(hid, down)
+                pre_grad = (nn(down_in, down) * slope).astype(bf16)
+                self.pre[rs, cs] = pre_grad
+                self.usum[:, cs] += col_sum(pre_grad.astype(f32))
+                self.acc_b[...] += nt(pre_grad, up)
+                return carry
+
+            lax.fori_loop(0, self.hidden // chunk, part, 0)
+            self.save(self.final, i, (middle + live * (self.acc_a[...] + self.row(7))).astype(bf16))
+            second_in_grad = self.acc_b[...]
+            self.vsum[5:6, :] += col_sum(second_in_grad * second_norm)
+            self.vsum[6:7, :] += col_sum(second_in_grad)
+            middle_grad = outer + norm_back(second_in_grad * self.row(5), second_norm, factor)
+            self.mg[rs, :] = middle_grad
+            mix_in = (live * middle_grad).astype(bf16)
+            self.mixin[rs, :] = mix_in
+            self.vsum[4:5, :] += col_sum(mix_in.astype(f32))
+            self.dout[rs, :] = nt(mix_in, mix_w).astype(bf16)
+            return carry
+
+        lax.fori_loop(0, self.blocks, one, 0)
+
+    def wide(self, lhs_t, rhs, base, count):
+        def one(c, carry):
+            self.put(base + c, nn(lhs_t[...], rhs[:, self.at(c, 512)]))
+            return carry
+
+        lax.fori_loop(0, count, one, 0)
+
+    def down_grad(self):
+        self.wide(self.down_t, self.hid, 0, self.hidden // 512)
+
+    def up_grad(self):
+        self.wide(self.second_t, self.pre, self.hidden // 512, self.hidden // 512)
+
+    def mix_grad(self):
+        self.wide(self.att_t, self.mixin, 2 * self.hidden // 512, self.width // 512)
+
+    def joint_grad(self):
+        self.wide(self.first_t, self.hid, (2 * self.hidden + self.width) // 512, 3 * self.width // 512)
+
+    def attend_back(self, hook):
+        lane, low, width = self.lane, self.low, self.width
+        joint = self.hid
+
+        def pair(p, carry):
+            ls = self.at(p, 128)
+            keys = self.k[:, ls]
+            self.kaug[:, :128] = keys
+            self.vaug_a[:, :128] = self.v[:, ls]
+            self.vaug_a[:, 128:] = self.kaug[:, 128:]
+            zero = jnp.zeros_like(keys)
+            self.vaug_b[:, :128] = jnp.where(low, keys, zero)
+            self.vaug_b[:, 128:] = jnp.where(low, zero, keys)
+            self.dk[...] = jnp.zeros_like(self.dk)
+            self.dv[...] = jnp.zeros_like(self.dv)
+
+            def one(i, carry):
+                rs = self.at(i)
+                query = self.q[rs, ls]
+                grad = self.dout[rs, ls]
+                both = grad.astype(f32) * self.att[rs, ls]
+                dq = None
+                for half in (0, 1):
+                    keep = low if half == 0 else jnp.logical_not(low)
+                    mine = jnp.where(keep, query, jnp.zeros_like(query))
+                    grads = jnp.where(keep, grad, jnp.zeros_like(grad))
+                    hi, mid, lo = three_parts(jnp.sum(jnp.where(keep, both, 0.0), axis=-1, keepdims=True))
+                    gaug = jnp.where(
+                        lane == 1, -hi, jnp.where(lane == 2, -mid, jnp.where(lane == 3, -lo, 0.0))
+                    ).astype(bf16)
+                    scores = nt(self.kaug[...], jnp.concatenate([mine, self.qaug[2 * p + half, rs, :]], axis=1))
+                    chances = jnp.exp(scores)
+                    centered = nt(self.vaug_a[...], jnp.concatenate([grads, gaug], axis=1))
+                    score_grad = (chances * centered).astype(bf16)
+                    self.dv[...] += nn(chances.astype(bf16), grads)
+                    self.dk[...] += nn(score_grad, mine)
+                    part = tn(score_grad, self.vaug_b[:, 128 * half : 128 * half + 128])
+                    dq = part if dq is None else dq + part
+                joint[rs, ls] = (dq * HEAD_DIM ** (-0.5)).astype(bf16)
+                return carry
+
+            lax.fori_loop(0, self.blocks, one, 0)
+            joint[:, pl.ds(pl.multiple_of(width + p * 128, 128), 128)] = self.dk[...].astype(bf16)
+            joint[:, pl.ds(pl.multiple_of(2 * width + p * 128, 128), 128)] = self.dv[...].astype(bf16)
+            hook(p)
+            return carry
+
+        lax.fori_loop(0, self.pairs, pair, 0)
+
+    def first_back(self, hook):
+        width = self.width
+
+        def one(i, carry):
+            rs = self.at(i)
+            grads = self.hid[rs, : 3 * width]
+            self.vsum[2:3, :] += col_sum(grads[:, :width].astype(f32))
+            self.vsum[3:4, :] += col_sum(grads[:, 2 * width :].astype(f32))
+            first_in_grad = nt(grads, self.weight(0, 3 * width))
+            normed, factor = normalize(self.load(self.x, i).astype(f32))
+            self.vsum[0:1, :] += col_sum(first_in_grad * normed)
+            self.vsum[1:2, :] += col_sum(first_in_grad)
+            token_grad = self.load_mg(rs) + norm_back(first_in_grad * self.row(0), normed, factor)
+            self.save(self.tg, i, token_grad.astype(bf16))
+            hook(i)
+            return carry
+
+        lax.fori_loop(0, self.blocks, one, 0)
+
+    def load_mg(self, rs):
+        return self.mg[rs, :]
+
+
+def layer_scratch(rows, width, hidden):
+    return [
+        pltpu.VMEM((rows, width), bf16),
+        pltpu.VMEM((rows, width), bf16),
+        pltpu.VMEM((rows, width), bf16),
+        pltpu.VMEM((rows, width), f32),
+        pltpu.VMEM((HEADS, rows, 128), bf16),
+        pltpu.VMEM((width, rows), bf16),
+        pltpu.VMEM((width, rows), bf16),
+        pltpu.VMEM((width, rows), bf16),
+        pltpu.VMEM((width, rows), bf16),
+        pltpu.VMEM((rows, width), bf16),
+        pltpu.VMEM((rows, width), f32),
+        pltpu.VMEM((rows, width), bf16),
+        pltpu.VMEM((rows, hidden), bf16),
+        pltpu.VMEM((rows, hidden), bf16),
+        pltpu.VMEM((rows, 256), bf16),
+        pltpu.VMEM((rows, 256), bf16),
+        pltpu.VMEM((rows, 256), bf16),
+        pltpu.VMEM((rows, 128), f32),
+        pltpu.VMEM((rows, 128), f32),
+        pltpu.VMEM((BLK, width), f32),
+        pltpu.VMEM((BLK, width), f32),
+    ]
+
+
+class Exchange:
+    def __init__(self, grads, cs, wide_first, emit, scratch, send, recv, high):
+        self.grads, self.cs, self.wide_first, self.emit, self.high = grads, cs, wide_first, emit, high
+        self.from_core, self.after_core, self.from_one, self.after_one, self.from_two, self.after_two, self.last = scratch
+        _, _, (a, b, c, e) = my_place()
+        self.place = (a, b, c, e)
+        across = {"fsdp": (1 - c) * 2 + e}, {"dp": a * 2 + 1 - b}
+
+        def describe(source, target, slot, device):
+            return pltpu.make_async_remote_copy(
+                src_ref=source, dst_ref=target, send_sem=send.at[slot], recv_sem=recv.at[slot],
+                device_id=device, device_id_type=MESH)
+
+        stages = [[describe(grads.at[:, :, :, 1 - e, :, cs], self.from_core, 0, {"fsdp": c * 2 + 1 - e})]]
+        if wide_first:
+            stages.append([describe(self.after_core.at[:, :, 1 - c], self.from_one, 1, across[0])])
+            stages.append([describe(self.after_one.at[:, 1 - b], self.from_two, 2, across[1])])
+        else:
+            stages.append([describe(self.after_core.at[:, 1 - b], self.from_one, 1, across[1])])
+            stages.append([describe(self.after_one.at[:, 1 - c], self.from_two, 2, across[0])])
+        copies = []
+        for s in range(1, high):
+            other = lax.rem(a + s, high)
+            copies.append(describe(self.after_two.at[other], self.last.at[a], 2 + s, {"dp": other * 2 + b}))
+        stages.append(copies)
+        self.stages = stages
+
+    def launch(self, number):
+        for copy in self.stages[number]:
+            copy.start()
+
+    def start(self):
+        self.launch(0)
+
+    def step(self, number):
+        a, b, c, e = self.place
+        for copy in self.stages[number]:
+            copy.wait_recv()
+        if number == 0:
+            def one(i, carry):
+                mine = self.grads[i, :, :, e, :, self.cs]
+                self.after_core[i] = (mine.astype(f32) + self.from_core[i].astype(f32)).astype(bf16)
+                return carry
+        elif number == 1:
+            def one(i, carry):
+                mine = self.after_core[i, :, c] if self.wide_first else self.after_core[i, b]
+                self.after_one[i] = (mine.astype(f32) + self.from_one[i].astype(f32)).astype(bf16)
+                return carry
+        elif number == 2:
+            def one(i, carry):
+                mine = self.after_one[i, b] if self.wide_first else self.after_one[i, c]
+                self.after_two[i] = (mine.astype(f32) + self.from_two[i].astype(f32)).astype(bf16)
+                return carry
+        if number < 3:
+            lax.fori_loop(0, self.high, one, 0)
+            self.launch(number + 1)
+        else:
+            total = self.after_two[a].astype(f32)
+            for s in range(1, self.high):
+                total = total + self.last[lax.rem(a + s, self.high)].astype(f32)
+            self.emit(total)
+
+    def wait_sent(self):
+        for stage in self.stages:
+            for copy in stage:
+                copy.wait_send()
+
+
+def when_at(index, value, action):
+    @pl.when(index == value)
+    def _():
+        action()
+
+
+def fill_vectors(small, vec, upb):
+    devices, own, _ = small.shape
+    turned = small[:, :, :128].reshape(devices * own, 128).astype(f32).T
+    vec[...] = turned[:8]
+    low = lax.broadcasted_iota(jnp.int32, (1, 128), 1) < 64
+    for i in range(devices // 2):
+        left, right = small[2 * i, :, 128:].astype(f32), small[2 * i + 1, :, 128:].astype(f32)
+        upb[:, 128 * i : 128 * i + 128] = jnp.where(low, left[0:1], right[0:1])
+
+
+def first_kernel(sizes, members, others, *refs):
+    shard, live, tokens, grads = refs[:4]
+    weights_out, final, tg, total, vsum, usum, next_x, next_g, vec, upb = refs[4:14]
+    weights, x, g, wsend, wrecv, tsend, trecv, local = refs[14:22]
+    scratch = refs[22:]
+    own = shard.shape[0]
+    width, hidden = vec.shape[1], upb.shape[1]
+    devices = members * others
+    greet(members, others)
+    swaps = [
+        Swap(src, dst, local.at[n], tsend.at[n], trecv.at[n], members)
+        for n, (src, dst) in enumerate(
+            ((tokens.at[0], x), (grads.at[0], g), (tokens.at[1], next_x), (grads.at[1], next_g)))
+    ]
+    mix_at = 3 * width + SMALL
+    up_at = mix_at + width
+    down_at = up_at + hidden
+    ranges = (
+        (pl.ds(0, 1024), (0, 1, 2, 3)),
+        (pl.ds(1024, mix_at - 1024), (0, 2, 1, 3)),
+        (pl.ds(up_at, hidden), (0, 1, 2, 3)),
+        (pl.ds(down_at, hidden), (0, 2, 1, 3)),
+        (pl.ds(mix_at, width), (0, 1, 2, 3)),
+    )
+    gathers = [
+        Gather(shard, weights, cs, order, local.at[4 + n], wsend.at[n], wrecv.at[n], sizes)
+        for n, (cs, order) in enumerate(ranges)
+    ]
+    early, late = gathers[:2], gathers[2:]
+    for gather in early:
+        gather.start(0)
+    swaps[0].start()
+    for number in range(1, 4):
+        for gather in early:
+            gather.wait(number - 1)
+            gather.start(number)
+    for gather in late:
+        gather.start(0)
+    swaps[1].start()
+
+    def weight(start, size):
+        return weights[:, :, :, :, :, pl.ds(start, size)].reshape(width, size)
+
+    def put(k, value):
+        total[:, pl.ds(pl.multiple_of(k * 512, 512), 512)] = value
+
+    vsum[...] = jnp.zeros_like(vsum)
+    usum[...] = jnp.zeros_like(usum)
+    layer = Layer(x, g, live, weight, (mix_at, up_at, down_at), vec, upb, final, tg, put, vsum, usum, scratch)
+    layer.masks()
+    for gather in early:
+        gather.wait(3)
+    fill_vectors(weights[:, :, :, :, :, 3 * width : mix_at].reshape(devices, own, SMALL), vec, upb)
+    swaps[0].wait()
+    layer.project()
+
+    def relay(number):
+        def action():
+            for gather in late:
+                gather.wait(number - 1)
+                gather.start(number)
+        return action
+
+    def hook(p):
+        for number in (1, 2, 3):
+            when_at(p, number - 1, relay(number))
+
+    layer.attend(hook)
+    for gather in late:
+        gather.wait(3)
+    swaps[1].wait()
+    swaps[2].start()
+    swaps[3].start()
+    keep = pltpu.make_async_copy(weights, weights_out, local.at[4 + len(ranges)])
+    keep.start()
+    layer.feed()
+    layer.down_grad()
+    layer.up_grad()
+    layer.mix_grad()
+    layer.attend_back(lambda p: None)
+    layer.joint_grad()
+    layer.first_back(lambda i: None)
+    keep.wait()
+    for swap in swaps[2:]:
+        swap.wait()
+    for item in swaps + gathers:
+        item.wait_sent()
+
+
+def second_kernel(sizes, members, others, *refs):
+    x, g, live, weights, vec, upb, previous, vprev, uprev, final0, tg0 = refs[:11]
+    outs = refs[11:16]
+    returned = refs[16:20]
+    refs = refs[20:]
+    final, tg, total, extra, vsum, usum, stage, wsend, wrecv, tsend, trecv, local, prior = refs[:13]
+    pools = [refs[13 + 7 * n : 20 + 7 * n] for n in range(4)]
+    scratch = refs[41:]
+    high = sizes[0]
+    width, hidden = vec.shape[1], upb.shape[1]
+    devices = members * others
+    own = width // devices
+    greet(members, others)
+    swaps = [
+        Swap(src, dst, local.at[n], tsend.at[n], trecv.at[n], members)
+        for n, (src, dst) in enumerate(zip((final0, tg0, final, tg), returned))
+    ]
+    swaps[0].start()
+    swaps[1].start()
+
+    def fetch(k):
+        slot = lax.rem(k, 2)
+        return pltpu.make_async_copy(
+            previous.at[:, pl.ds(pl.multiple_of(k * 512, 512), 512)], stage.at[slot], prior.at[slot])
+
+    chunks = (2 * hidden + 4 * width) // 512
+    fetch(0).start()
+
+    def put(k, value):
+        fetch(k).wait()
+
+        @pl.when(k + 1 < chunks)
+        def _():
+            fetch(k + 1).start()
+
+        value = (value + stage[lax.rem(k, 2)]).astype(bf16)
+        total[:, :, :, :, :, pl.ds(pl.multiple_of(k * 512, 512), 512)] = value.reshape(sizes + (own, 512))
+
+    def weight(start, size):
+        return weights[:, pl.ds(start, size)]
+
+    mix_at = 3 * width + SMALL
+    up_at = mix_at + width
+    down_at = up_at + hidden
+    vsum[...] = vprev[...]
+    usum[...] = uprev[...]
+    layer = Layer(x, g, live, weight, (mix_at, up_at, down_at), vec, upb, final, tg, put, vsum, usum, scratch)
+
+    def emit_to(ref, lo=None, hi=None):
+        def emit(value):
+            ref[...] = value
+        return emit
+
+    joint_at = 2 * hidden + width
+    down, up, rest, tail = (
+        Exchange(grads, cs, wide_first, emit, pools[n], wsend.at[n], wrecv.at[n], high)
+        for n, (grads, cs, wide_first, emit) in enumerate((
+            (total, pl.ds(0, hidden), True, emit_to(outs[3])),
+            (total, pl.ds(hidden, hidden + width), False, lambda v: emit_pair(v)),
+            (total, pl.ds(joint_at, 3 * width), True, emit_to(outs[0])),
+            (extra, pl.ds(0, SMALL), False, emit_to(outs[4])),
+        ))
+    )
+
+    def emit_pair(value):
+        outs[2][...] = value[:, :hidden]
+        outs[1][...] = value[:, hidden:]
+
+    layer.masks()
+    layer.project()
+    layer.attend(lambda p: None)
+    layer.feed()
+    layer.down_grad()
+    layer.up_grad()
+    down.start()
+    layer.mix_grad()
+    swaps[2].start()
+
+    def hook(p):
+        for number in range(4):
+            when_at(p, number, lambda number=number: down.step(number))
+        when_at(p, 0, up.start)
+        for number in range(3):
+            when_at(p, number + 1, lambda number=number: up.step(number))
+
+    layer.attend_back(hook)
+    layer.joint_grad()
+    up.step(3)
+    rest.start()
+    first = swaps[3]
+    per = BLK // tg.shape[1]
+    me = lax.axis_index("dp")
+
+    layer.first_back(lambda i: None)
+    first.start()
+    vectors = jnp.concatenate([vsum[...], jnp.zeros((120, width), f32)], axis=0).T
+    extra[:, :, :, :, :, :128] = vectors.astype(bf16).reshape(sizes + (own, 128))
+    for n in range(devices):
+        a, b, c, e = n // (2 * others), (n // others) % 2, (n % others) // 2, n % 2
+        piece = usum[:, 128 * (n // 2) : 128 * (n // 2) + 128]
+        extra[a, b, c, e, :, 128:] = jnp.broadcast_to(piece, (own, 128)).astype(bf16)
+    tail.start()
+    for number in range(4):
+        rest.step(number)
+        tail.step(number)
+    for swap in swaps:
+        swap.wait()
+    for item in swaps + [down, up, rest, tail]:
+        item.wait_sent()
+
+
+def first_call(shard, live, tokens, grads, members, others, hidden):
+    own, columns = shard.shape
+    micro, _, piece, width = tokens.shape
+    rows = members * piece
+    sizes = (members // 2, 2, others // 2, 2)
+    slots = sizes[0] + 1 + sizes[2]
+    block = jax.ShapeDtypeStruct((members, piece, width), bf16)
+    dma = pltpu.SemaphoreType.DMA
+    return pl.pallas_call(
+        functools.partial(first_kernel, sizes, members, others),
+        out_shape=(
+            jax.ShapeDtypeStruct(sizes + (own, columns), bf16), block, block,
+            jax.ShapeDtypeStruct((width, 2 * hidden + 4 * width), f32),
+            jax.ShapeDtypeStruct((8, width), f32), jax.ShapeDtypeStruct((1, hidden), f32), block, block,
+            jax.ShapeDtypeStruct((8, width), f32), jax.ShapeDtypeStruct((1, hidden), f32),
+        ),
+        in_specs=[VMEM, VMEM, ANY, ANY],
+        out_specs=(ANY,) + (VMEM,) * 5 + (ANY,) * 2 + (VMEM,) * 2,
+        scratch_shapes=[
+            pltpu.VMEM(sizes + (own, columns), bf16),
+            pltpu.VMEM((members, piece, width), bf16),
+            pltpu.VMEM((members, piece, width), bf16),
+            dma((5, slots)), dma((5, slots)), dma((4, members)), dma((4, members)), dma((10,)),
+        ] + layer_scratch(rows, width, hidden),
+        compiler_params=pltpu.CompilerParams(
+            collective_id=2, has_side_effects=True, vmem_limit_bytes=67_043_328),
+        name="first_sequence",
+    )(shard, live, tokens, grads)
+
+
+def second_call(x, g, live, weights, vec, upb, previous, vprev, uprev, final0, tg0, members, others):
+    _, piece, width = x.shape
+    rows, hidden = members * piece, upb.shape[1]
+    sizes = (members // 2, 2, others // 2, 2)
+    own = width // (members * others)
+    dma = pltpu.SemaphoreType.DMA
+    block = jax.ShapeDtypeStruct((members, piece, width), bf16)
+    pools = []
+    for columns in (hidden, hidden + width, 3 * width, SMALL):
+        pools += reduce_scratch(sizes[0], own, columns)
+    shapes = [(own, 3 * width), (own, width), (own, hidden), (own, hidden), (own, SMALL)]
+    return pl.pallas_call(
+        functools.partial(second_kernel, sizes, members, others),
+        out_shape=tuple(jax.ShapeDtypeStruct(shape, f32) for shape in shapes) + (block,) * 4,
+        in_specs=[VMEM] * 6 + [ANY] + [VMEM] * 2 + [ANY] * 2,
+        out_specs=(VMEM,) * 5 + (ANY,) * 4,
+        scratch_shapes=[
+            pltpu.VMEM((members, piece, width), bf16),
+            pltpu.VMEM((members, piece, width), bf16),
+            pltpu.VMEM(sizes + (own, 2 * hidden + 4 * width), bf16),
+            pltpu.VMEM(sizes + (own, SMALL), bf16),
+            pltpu.VMEM((8, width), f32),
+            pltpu.VMEM((1, hidden), f32),
+            pltpu.VMEM((2, width, 512), f32),
+            dma((4, sizes[0] + 2)), dma((4, sizes[0] + 2)), dma((4, members)), dma((4, members)), dma((4,)), dma((2,)),
+        ] + pools + layer_scratch(rows, width, hidden),
+        compiler_params=pltpu.CompilerParams(
+            collective_id=3, has_side_effects=True, vmem_limit_bytes=67_043_328),
+        name="second_sequence",
+    )(x, g, live, weights, vec, upb, previous, vprev, uprev, final0, tg0)
+
+
+def fused_body(
+    tokens, out_grad, seq_lengths, send_to, slot_of, first_gain, first_shift, joint_weight, query_bias,
+    value_bias, mix_weight, mix_bias, second_gain, second_shift, up_weight, up_bias, down_weight, down_bias,
+):
+    members, others = lax.axis_size("dp"), lax.axis_size("fsdp")
+    micro, rows, width = tokens.shape
+    piece = rows // members
+    own = first_gain.shape[0]
+    hidden = down_weight.shape[0]
+    vectors = (first_gain, first_shift, query_bias, value_bias, mix_bias, second_gain, second_shift, down_bias)
+    twice = jnp.broadcast_to(jnp.concatenate([up_bias, up_bias])[None], (own, 128))
+    small = jnp.concatenate([jnp.stack(vectors, axis=1), jnp.zeros((own, 120), bf16), twice], axis=1)
+    shard = jnp.concatenate([joint_weight, small, mix_weight, up_weight, down_weight.T], axis=1)
+    table = send_to[:, 0]
+    pieces = (micro, members, piece, width)
+    sent, sent_grad = reorder(True, table, tokens.reshape(pieces), out_grad.reshape(pieces))
+    spots = slot_of[:, 0, :, None] * piece + jnp.arange(piece, dtype=jnp.int32)
+    live = (spots.reshape(micro, rows) < seq_lengths).astype(f32)[:, :, None]
+    weights, final0, tg0, total, vsum, usum, x, g, vec, upb = first_call(
+        shard, live[0], sent, sent_grad, members, others, hidden)
+    whole = weights.reshape(width, shard.shape[1])
+    joint, mix, up, down, tail, *returned = second_call(
+        x, g, live[1], whole, vec, upb, total, vsum, usum, final0, tg0, members, others)
+    layer_output, input_grad = reorder(
+        False, table, jnp.stack([returned[0], returned[2]]), jnp.stack([returned[1], returned[3]]))
+    vec_grad = [tail[:, n] for n in range(8)]
+    odd = lax.rem(lax.axis_index("fsdp"), 2) == 1
+    up_bias_grad = jnp.where(odd, tail[0, 192:256], tail[0, 128:192])
+    return (
+        layer_output.reshape(tokens.shape), input_grad.reshape(tokens.shape),
+        vec_grad[0], vec_grad[1], joint, vec_grad[2], vec_grad[3], mix, vec_grad[4], vec_grad[5], vec_grad[6],
+        up, up_bias_grad, down.T, vec_grad[7],
+    )
+
+
 def solution(mesh):
     both = ("dp", "fsdp")
     row3, row2, vector, matrix = P(None, both, None), P(None, both), P(both), P(both, None)
     turned = P(None, both)
+    members, others = mesh.shape["dp"], mesh.shape["fsdp"]
+    fits = members * others == 32 and others == 4
     return jax.shard_map(
-        body,
+        fused_body if fits else body,
         mesh=mesh,
         in_specs=(row3, row3, row2, row3, row3, vector, vector, matrix, vector, vector, matrix, vector, vector,
                   vector, matrix, vector, turned, vector),

time: 454 us -> 331 us (0.73)
  Pallas kernels: 431 us -> 315 us
  local copies, waits for them, and re-layouts: 15.3 us -> 8.43 us
    pallas_call x4 -> x2, Pallas kernels: 420 us -> 305 us  [the longest x1 152 us: second_call(): pl.pallas_call(functools.partial(second_kernel, sizes, members, others),...]
    slice x6 -> x1, local copies, waits for them, and re-layouts: 6.23 us -> 0.81 us  [fused_body(): vec_grad = [tail[:, n] for n in range(8)]]
where the time goes in v2:
time: 331 us; the launch traced here: 330 us
  Pallas kernels  315 us (95%)
  local copies, waits for them, and re-layouts  8.43 us (3%)
  other arithmetic  5.24 us (2%)
    pallas_call x1, Pallas kernels, second_call(): pl.pallas_call(functools.partial(second_kernel, sizes, members, others),...  152 us
    pallas_call x1, Pallas kernels, first_call(): pl.pallas_call(functools.partial(first_kernel, sizes, members, others), o...  152 us
    pallas_call x2, Pallas kernels, reorder(): pl.pallas_call(functools.partial(order_kernel, scatter), out_shape=tuple(...  10.7 us

profile of v2, /device:TPU:0, one launch (start us, length us, event | category | flops | bytes accessed | tf_op | source)
XLA Modules:
  0.0 330.0 jit_solution(9292809739572770495)
XLA Ops:
  0.7 0.0 copy-start.9
  0.8 5.3 %order_out.1 = (bf16[2,8,128,512]{3,2,1,0:T(8,128)(2,1)}, bf16[2,8,128,512]{3,2,1,0:T(8,128)(2,1)}) custom-call(s32[2,8]{1,0:T(2,128)} %bitcast.45, bf16[2,8,128,512]{3,2,1,0:T(8,128)(2,1)} %bitcast.37, bf16[2,8,128,512]{3,2,1,0:T(8,128)(2,1)} %bitcast.38), custom_call_target="tpu_custom_call" | custom-call | tf_op jit(solution)/shard_map/order_out/pallas_call | solution.py:609
  6.2 0.1 broadcast_bitcast_fusion
  6.2 0.1 compare_convert_fusion
  6.3 0.6 slice_bitcast_fusion
  6.9 1.0 copy.49.refs_1_
  7.9 0.0 copy-done.19
  7.9 0.1 pad_maximum_fusion.2
  8.0 0.1 copy.41
  8.1 0.1 copy.42
  8.2 0.1 copy.43
  8.3 0.1 copy.44
  8.4 0.0 copy-done.14
  8.4 0.1 copy.45
  8.5 0.1 copy.46
  8.6 0.0 copy-done.16
  8.6 0.1 copy.47
  8.7 0.1 copy.48
  8.8 0.0 copy-done.4
  8.8 0.0 copy-done.5
  8.9 0.8 concatenate.7.refs_0_
  9.6 152.3 %first_sequence.1 = (bf16[4,2,2,2,16,6400]{5,4,3,2,1,0:T(8,128)(2,1)}, bf16[8,128,512]{2,1,0:T(8,128)(2,1)}, bf16[8,128,512]{2,1,0:T(8,128)(2,1)}, f32[512,6144]...) custom-call(bf16[16,6400]{1,0:T(8,128)(2,1)} %concatenate.7.refs_0_,, ...), custom_call_target="tpu_custom_call" | custom-call | tf_op jit(solution)/shard_map/first_sequence/pallas_call | solution.py:1287
  162.0 1.7 copy.50.refs_2_
  163.7 152.5 %second_sequence.1 = (f32[16,1536]{1,0:T(8,128)}, f32[16,512]{1,0:T(8,128)}, f32[16,2048]{1,0:T(8,128)}, f32[16,2048]{1,0:T(8,128)}, f32[16,256]{1,0:T(8,128)}, ...) custom-call(bf16[8,128,512]{2,1,0:T(8,128)(2,1)} %get-tuple-element., ...), custom_call_target="tpu_custom_call" | custom-call | tf_op jit(solution)/shard_map/second_sequence/pallas_call | solution.py:1320
  316.2 4.5 %pad_maximum_fusion = (bf16[2,8,128,512]{3,2,1,0:T(8,128)(2,1)}, bf16[2,8,128,512]{3,2,1,0:T(8,128)(2,1)}) fusion(bf16[1,8,128,512]{3,2,1,0:T(8,128)(2,1)} %bitcast.41, bf16[1,8,128,512]{3,2,1,0:T(8,128)(2,1)} %bitcast.39, bf16[1,8,128,512]{3,2,1,0:T(8,128)(2,1)} %bitcast.42, bf16[1,8,128,512]{3,2,1,0:T(8,128)(2,1)} %bitcast.40), kind=kLoop, calls=%fused_computation | loop fusion | flops 2097152 | bytes 8388608 | tf_op jit(solution)/shard_map/stack | solution.py:1365
  320.7 5.3 %order_in.1 = (bf16[2,8,128,512]{3,2,1,0:T(8,128)(2,1)}, bf16[2,8,128,512]{3,2,1,0:T(8,128)(2,1)}) custom-call(s32[2,8]{1,0:T(2,128)} %bitcast.46, bf16[2,8,128,512]{3,2,1,0:T(8,128)(2,1)} %get-tuple-element.71.refs_0_, bf16[2,8,128,512]{3,2,1,0:T(8,128)(2,1)} %get-tuple-element.72.refs_1_), custom_call_target="tpu_custom_call" | custom-call | tf_op jit(solution)/shard_map/order_in/pallas_call | solution.py:609
  326.1 0.6 fusion
  326.6 0.8 slice_reduce_fusion
  327.5 0.6 copy.57
  328.1 0.6 copy.58
  328.7 0.7 copy.59
  329.4 0.7 copy.60
  (38 shorter events, 0.1 us)
Async XLA Ops:
  0.7 5.5 %copy-start.9 = (s32[2,1,8]{2,1,0:T(1,128)S(1)}, s32[2,1,8]{2,1,0:T(1,128)}, u32[]{:S(2)}) copy-start(s32[2,1,8]{2,1,0:T(1,128)} %param.22) | copy-start | bytes 196
  0.7 5.6 %copy-start.18 = (s32[2,1]{0,1:T(1,128)S(1)}, s32[2,1]{0,1:T(1,128)}, u32[]{:S(2)}) copy-start(s32[2,1]{0,1:T(1,128)} %param.20) | copy-start | bytes 28
  0.7 7.3 %copy-start.19 = (bf16[64]{0:T(256)(128)(2,1)S(1)}, bf16[64]{0:T(256)(128)(2,1)}, u32[]{:S(2)}) copy-start(bf16[64]{0:T(256)(128)(2,1)} %param.33) | copy-start | bytes 388
  0.7 7.3 %copy-start.10 = (bf16[16]{0:T(256)(128)(2,1)S(1)}, bf16[16]{0:T(256)(128)(2,1)}, u32[]{:S(2)}) copy-start(bf16[16]{0:T(256)(128)(2,1)} %param.23) | copy-start | bytes 100
  0.7 7.4 %copy-start.11 = (bf16[16]{0:T(256)(128)(2,1)S(1)}, bf16[16]{0:T(256)(128)(2,1)}, u32[]{:S(2)}) copy-start(bf16[16]{0:T(256)(128)(2,1)} %param.24) | copy-start | bytes 100
  0.7 7.5 %copy-start.12 = (bf16[16]{0:T(256)(128)(2,1)S(1)}, bf16[16]{0:T(256)(128)(2,1)}, u32[]{:S(2)}) copy-start(bf16[16]{0:T(256)(128)(2,1)} %param.26) | copy-start | bytes 100
  0.7 7.6 %copy-start.13 = (bf16[16]{0:T(256)(128)(2,1)S(1)}, bf16[16]{0:T(256)(128)(2,1)}, u32[]{:S(2)}) copy-start(bf16[16]{0:T(256)(128)(2,1)} %param.27) | copy-start | bytes 100
  0.7 7.7 %copy-start.14 = (bf16[16]{0:T(256)(128)(2,1)S(1)}, bf16[16]{0:T(256)(128)(2,1)}, u32[]{:S(2)}) copy-start(bf16[16]{0:T(256)(128)(2,1)} %param.29) | copy-start | bytes 100
  0.7 7.8 %copy-start.15 = (bf16[16]{0:T(256)(128)(2,1)S(1)}, bf16[16]{0:T(256)(128)(2,1)}, u32[]{:S(2)}) copy-start(bf16[16]{0:T(256)(128)(2,1)} %param.30) | copy-start | bytes 100
  0.7 7.9 %copy-start.16 = (bf16[16]{0:T(256)(128)(2,1)S(1)}, bf16[16]{0:T(256)(128)(2,1)}, u32[]{:S(2)}) copy-start(bf16[16]{0:T(256)(128)(2,1)} %param.31) | copy-start | bytes 100
  0.8 8.0 %copy-start.17 = (bf16[16]{0:T(256)(128)(2,1)S(1)}, bf16[16]{0:T(256)(128)(2,1)}, u32[]{:S(2)}) copy-start(bf16[16]{0:T(256)(128)(2,1)} %param.35) | copy-start | bytes 100
  0.8 8.1 %copy-start.4 = (bf16[16,2048]{1,0:T(8,128)(2,1)S(1)}, bf16[16,2048]{1,0:T(8,128)(2,1)}, u32[]{:S(2)}) copy-start(bf16[16,2048]{1,0:T(8,128)(2,1)} %param.32) | copy-start | bytes 196612
  0.8 8.1 %copy-start.5 = (bf16[2048,16]{0,1:T(8,128)(2,1)S(1)}, bf16[2048,16]{0,1:T(8,128)(2,1)}, u32[]{:S(2)}) copy-start(bf16[2048,16]{0,1:T(8,128)(2,1)} %param.34) | copy-start | bytes 196612
  0.8 8.1 %copy-start.6 = (bf16[16,1536]{1,0:T(8,128)(2,1)S(1)}, bf16[16,1536]{1,0:T(8,128)(2,1)}, u32[]{:S(2)}) copy-start(bf16[16,1536]{1,0:T(8,128)(2,1)} %param.25) | copy-start | bytes 147460
  0.8 8.1 %copy-start.8 = (bf16[16,512]{1,0:T(8,128)(2,1)S(1)}, bf16[16,512]{1,0:T(8,128)(2,1)}, u32[]{:S(2)}) copy-start(bf16[16,512]{1,0:T(8,128)(2,1)} %param.28) | copy-start | bytes 49156
  320.7 5.4 %copy-start = (f32[16,256]{1,0:T(8,128)S(1)}, f32[16,256]{1,0:T(8,128)}, u32[]{:S(2)}) copy-start(f32[16,256]{1,0:T(8,128)} %get-tuple-element.56) | copy-start | bytes 49156
  320.7 6.8 %copy-start.3 = (f32[16,1536]{1,0:T(8,128)S(1)}, f32[16,1536]{1,0:T(8,128)}, u32[]{:S(2)}) copy-start(f32[16,1536]{1,0:T(8,128)} %get-tuple-element.92) | copy-start | bytes 294916
  320.7 7.4 %copy-start.7 = (f32[16,512]{1,0:T(8,128)S(1)}, f32[16,512]{1,0:T(8,128)}, u32[]{:S(2)}) copy-start(f32[16,512]{1,0:T(8,128)} %get-tuple-element.95) | copy-start | bytes 98308
  320.7 8.0 %copy-start.2 = (f32[16,2048]{1,0:T(8,128)S(1)}, f32[16,2048]{1,0:T(8,128)}, u32[]{:S(2)}) copy-start(f32[16,2048]{1,0:T(8,128)} %get-tuple-element.99) | copy-start | bytes 393220
  320.7 8.7 %copy-start.1 = (f32[16,2048]{1,0:T(8,128)S(1)}, f32[16,2048]{1,0:T(8,128)}, u32[]{:S(2)}) copy-start(f32[16,2048]{1,0:T(8,128)} %get-tuple-element.60) | copy-start | bytes 393220

commit v3 on v2

--- a/solution.py
+++ b/solution.py
@@ -767,10 +767,12 @@
         self.vaug_a[:, 128:] = jnp.ones((rows, 128), bf16)
         self.vaug_b[:, 128:] = jnp.ones((rows, 128), bf16)
 
-    def project(self):
+    def project(self, turn, arrive):
         width = self.width
 
-        def one(i, carry):
+        def one(s, carry):
+            arrive(s)
+            i = turn(s)
             rs = self.at(i)
             normed, _ = normalize(self.load(self.x, i).astype(f32))
             first_in = (normed * self.row(0) + self.row(1)).astype(bf16)
@@ -815,19 +817,20 @@
                     part = got[:, :128] / total
                     out = part if out is None else out + part
                 self.att[rs, ls] = out
+                hook(p * self.blocks + i)
                 return carry
 
-            lax.fori_loop(0, self.blocks, one, carry)
-            hook(p)
-            return carry
+            return lax.fori_loop(0, self.blocks, one, carry)
 
         lax.fori_loop(0, self.pairs, pair, 0)
 
-    def feed(self):
+    def feed(self, turn, arrive):
         chunk = 512
         mix_at, up_at, down_at = self.offsets
 
-        def one(i, carry):
+        def one(s, carry):
+            arrive(s)
+            i = turn(s)
             rs = self.at(i)
             live = self.live[rs, :]
             attended = self.att[rs, :].astype(bf16)
@@ -852,10 +855,10 @@
                 phi = 0.5 * (1.0 + lax.erf(pre * root_half))
                 hid = (pre * phi).astype(bf16)
                 slope = phi + pre * jnp.exp(-0.5 * pre * pre) * gauss_norm
-                self.hid[rs, cs] = hid
+                self.hid[c, rs, :] = hid
                 self.acc_a[...] += nt(hid, down)
                 pre_grad = (nn(down_in, down) * slope).astype(bf16)
-                self.pre[rs, cs] = pre_grad
+                self.pre[c, rs, :] = pre_grad
                 self.usum[:, cs] += col_sum(pre_grad.astype(f32))
                 self.acc_b[...] += nt(pre_grad, up)
                 return carry
@@ -877,7 +880,7 @@
 
     def wide(self, lhs_t, rhs, base, count):
         def one(c, carry):
-            self.put(base + c, nn(lhs_t[...], rhs[:, self.at(c, 512)]))
+            self.put(base + c, nn(lhs_t[...], rhs[c]))
             return carry
 
         lax.fori_loop(0, count, one, 0)
@@ -889,13 +892,13 @@
         self.wide(self.second_t, self.pre, self.hidden // 512, self.hidden // 512)
 
     def mix_grad(self):
-        self.wide(self.att_t, self.mixin, 2 * self.hidden // 512, self.width // 512)
+        self.put(2 * self.hidden // 512, nn(self.att_t[...], self.mixin[...]))
 
     def joint_grad(self):
         self.wide(self.first_t, self.hid, (2 * self.hidden + self.width) // 512, 3 * self.width // 512)
 
     def attend_back(self, hook):
-        lane, low, width = self.lane, self.low, self.width
+        lane, low = self.lane, self.low
         joint = self.hid
 
         def pair(p, carry):
@@ -932,38 +935,36 @@
                     self.dk[...] += nn(score_grad, mine)
                     part = tn(score_grad, self.vaug_b[:, 128 * half : 128 * half + 128])
                     dq = part if dq is None else dq + part
-                joint[rs, ls] = (dq * HEAD_DIM ** (-0.5)).astype(bf16)
+                joint[0, rs, ls] = (dq * HEAD_DIM ** (-0.5)).astype(bf16)
+                hook(p * self.blocks + i)
                 return carry
 
             lax.fori_loop(0, self.blocks, one, 0)
-            joint[:, pl.ds(pl.multiple_of(width + p * 128, 128), 128)] = self.dk[...].astype(bf16)
-            joint[:, pl.ds(pl.multiple_of(2 * width + p * 128, 128), 128)] = self.dv[...].astype(bf16)
-            hook(p)
+            joint[1, :, ls] = self.dk[...].astype(bf16)
+            joint[2, :, ls] = self.dv[...].astype(bf16)
             return carry
 
         lax.fori_loop(0, self.pairs, pair, 0)
 
-    def first_back(self, hook):
+    def first_back(self, turn, done):
         width = self.width
 
-        def one(i, carry):
+        def one(s, carry):
+            i = turn(s)
             rs = self.at(i)
-            grads = self.hid[rs, : 3 * width]
+            grads = jnp.concatenate([self.hid[0, rs, :], self.hid[1, rs, :], self.hid[2, rs, :]], axis=1)
             self.vsum[2:3, :] += col_sum(grads[:, :width].astype(f32))
             self.vsum[3:4, :] += col_sum(grads[:, 2 * width :].astype(f32))
             first_in_grad = nt(grads, self.weight(0, 3 * width))
             normed, factor = normalize(self.load(self.x, i).astype(f32))
             self.vsum[0:1, :] += col_sum(first_in_grad * normed)
             self.vsum[1:2, :] += col_sum(first_in_grad)
-            token_grad = self.load_mg(rs) + norm_back(first_in_grad * self.row(0), normed, factor)
+            token_grad = self.mg[rs, :] + norm_back(first_in_grad * self.row(0), normed, factor)
             self.save(self.tg, i, token_grad.astype(bf16))
-            hook(i)
+            done(s)
             return carry
 
         lax.fori_loop(0, self.blocks, one, 0)
-
-    def load_mg(self, rs):
-        return self.mg[rs, :]
 
 
 def layer_scratch(rows, width, hidden):
@@ -980,8 +981,8 @@
         pltpu.VMEM((rows, width), bf16),
         pltpu.VMEM((rows, width), f32),
         pltpu.VMEM((rows, width), bf16),
-        pltpu.VMEM((rows, hidden), bf16),
-        pltpu.VMEM((rows, hidden), bf16),
+        pltpu.VMEM((hidden // 512, rows, 512), bf16),
+        pltpu.VMEM((hidden // 512, rows, 512), bf16),
         pltpu.VMEM((rows, 256), bf16),
         pltpu.VMEM((rows, 256), bf16),
         pltpu.VMEM((rows, 256), bf16),
@@ -992,10 +993,72 @@
     ]
 
 
+class Route:
+    def __init__(self, src, dst, local, send, recv, members):
+        self.src, self.dst, self.send, self.recv, self.members = src, dst, send, recv, members
+        self.me = lax.axis_index("dp")
+        self.own = pltpu.make_async_copy(src.at[self.me], dst.at[self.me], local)
+
+    def outgoing(self, to):
+        slot = lax.rem(to - self.me + self.members, self.members)
+        return pltpu.make_async_remote_copy(
+            src_ref=self.src.at[to], dst_ref=self.dst.at[self.me], send_sem=self.send.at[slot],
+            recv_sem=self.recv.at[slot], device_id={"dp": to}, device_id_type=MESH)
+
+    def incoming(self, source):
+        slot = lax.rem(self.me - source + self.members, self.members)
+        return pltpu.make_async_remote_copy(
+            src_ref=self.src.at[source], dst_ref=self.dst.at[source], send_sem=self.send.at[slot],
+            recv_sem=self.recv.at[slot], device_id={"dp": source}, device_id_type=MESH)
+
+    def beside(self):
+        return self.me + 1 - 2 * lax.rem(self.me, 2)
+
+    def pair(self, s):
+        block = lax.rem(self.me // 2 + s, self.members // 2)
+        return 2 * block, 2 * block + 1
+
+    def start(self):
+        for s in range(1, self.members):
+            self.outgoing(lax.rem(self.me + s, self.members)).start()
+        self.own.start()
+
+    def give(self, s):
+        @pl.when(s > 0)
+        def _():
+            for to in self.pair(s):
+                self.outgoing(to).start()
+
+        @pl.when(s == 0)
+        def _():
+            self.outgoing(self.beside()).start()
+            self.own.start()
+
+    def take(self, s):
+        @pl.when(s > 0)
+        def _():
+            for source in self.pair(s):
+                self.incoming(source).wait_recv()
+
+        @pl.when(s == 0)
+        def _():
+            self.own.wait()
+            self.incoming(self.beside()).wait_recv()
+
+    def wait(self):
+        for s in range(1, self.members):
+            self.incoming(lax.rem(self.me + s, self.members)).wait_recv()
+        self.own.wait()
+
+    def wait_sent(self):
+        for s in range(1, self.members):
+            self.outgoing(lax.rem(self.me + s, self.members)).wait_send()
+
+
 class Exchange:
     def __init__(self, grads, cs, wide_first, emit, scratch, send, recv, high):
         self.grads, self.cs, self.wide_first, self.emit, self.high = grads, cs, wide_first, emit, high
-        self.from_core, self.after_core, self.from_one, self.after_one, self.from_two, self.after_two, self.last = scratch
+        self.from_core, self.from_one, self.from_two, self.last = scratch
         _, _, (a, b, c, e) = my_place()
         self.place = (a, b, c, e)
         across = {"fsdp": (1 - c) * 2 + e}, {"dp": a * 2 + 1 - b}
@@ -1007,15 +1070,16 @@
 
         stages = [[describe(grads.at[:, :, :, 1 - e, :, cs], self.from_core, 0, {"fsdp": c * 2 + 1 - e})]]
         if wide_first:
-            stages.append([describe(self.after_core.at[:, :, 1 - c], self.from_one, 1, across[0])])
-            stages.append([describe(self.after_one.at[:, 1 - b], self.from_two, 2, across[1])])
+            stages.append([describe(grads.at[:, :, 1 - c, e, :, cs], self.from_one, 1, across[0])])
+            stages.append([describe(grads.at[:, 1 - b, c, e, :, cs], self.from_two, 2, across[1])])
         else:
-            stages.append([describe(self.after_core.at[:, 1 - b], self.from_one, 1, across[1])])
-            stages.append([describe(self.after_one.at[:, 1 - c], self.from_two, 2, across[0])])
+            stages.append([describe(grads.at[:, 1 - b, :, e, :, cs], self.from_one, 1, across[1])])
+            stages.append([describe(grads.at[:, b, 1 - c, e, :, cs], self.from_two, 2, across[0])])
         copies = []
         for s in range(1, high):
             other = lax.rem(a + s, high)
-            copies.append(describe(self.after_two.at[other], self.last.at[a], 2 + s, {"dp": other * 2 + b}))
+            copies.append(describe(
+                grads.at[other, b, c, e, :, cs], self.last.at[a], 2 + s, {"dp": other * 2 + b}))
         stages.append(copies)
         self.stages = stages
 
@@ -1028,28 +1092,34 @@
 
     def step(self, number):
         a, b, c, e = self.place
+        grads, cs = self.grads, self.cs
         for copy in self.stages[number]:
             copy.wait_recv()
         if number == 0:
             def one(i, carry):
-                mine = self.grads[i, :, :, e, :, self.cs]
-                self.after_core[i] = (mine.astype(f32) + self.from_core[i].astype(f32)).astype(bf16)
+                mine = grads[i, :, :, e, :, cs].astype(f32)
+                grads[i, :, :, e, :, cs] = (mine + self.from_core[i].astype(f32)).astype(bf16)
+                return carry
+        elif number == 1 and self.wide_first:
+            def one(i, carry):
+                mine = grads[i, :, c, e, :, cs].astype(f32)
+                grads[i, :, c, e, :, cs] = (mine + self.from_one[i].astype(f32)).astype(bf16)
                 return carry
         elif number == 1:
             def one(i, carry):
-                mine = self.after_core[i, :, c] if self.wide_first else self.after_core[i, b]
-                self.after_one[i] = (mine.astype(f32) + self.from_one[i].astype(f32)).astype(bf16)
+                mine = grads[i, b, :, e, :, cs].astype(f32)
+                grads[i, b, :, e, :, cs] = (mine + self.from_one[i].astype(f32)).astype(bf16)
                 return carry
         elif number == 2:
             def one(i, carry):
-                mine = self.after_one[i, b] if self.wide_first else self.after_one[i, c]
-                self.after_two[i] = (mine.astype(f32) + self.from_two[i].astype(f32)).astype(bf16)
+                mine = grads[i, b, c, e, :, cs].astype(f32)
+                grads[i, b, c, e, :, cs] = (mine + self.from_two[i].astype(f32)).astype(bf16)
                 return carry
         if number < 3:
             lax.fori_loop(0, self.high, one, 0)
             self.launch(number + 1)
         else:
-            total = self.after_two[a].astype(f32)
+            total = grads[a, b, c, e, :, cs].astype(f32)
             for s in range(1, self.high):
                 total = total + self.last[lax.rem(a + s, self.high)].astype(f32)
             self.emit(total)
@@ -1060,282 +1130,311 @@
                 copy.wait_send()
 
 
-def when_at(index, value, action):
-    @pl.when(index == value)
-    def _():
-        action()
+def exchange_scratch(high, rows, columns):
+    return [pltpu.VMEM(lead + (rows, columns), bf16) for lead in ((high, 2, 2), (high, 2), (high,), (high,))]
 
 
 def fill_vectors(small, vec, upb):
     devices, own, _ = small.shape
-    turned = small[:, :, :128].reshape(devices * own, 128).astype(f32).T
-    vec[...] = turned[:8]
+    rows = small[:, :, :128].reshape(devices * own, 128).astype(f32)
+    spot = lax.broadcasted_iota(jnp.int32, rows.shape, 1)
+    turn = lax.broadcasted_iota(jnp.int32, rows.shape, 0)
+    mine = jnp.where(lax.rem(spot, own) == lax.rem(turn, own), rows, 0.0).astype(bf16)
+    lanes = lax.broadcasted_iota(jnp.int32, (16, 128), 1)
+    picks = lax.broadcasted_iota(jnp.int32, (16, 128), 0)
+    choose = jnp.where(lanes - picks * own == lax.rem(lanes, own), 1.0, 0.0).astype(bf16)
+    vec[...] = nt(choose, mine)[:8]
     low = lax.broadcasted_iota(jnp.int32, (1, 128), 1) < 64
     for i in range(devices // 2):
         left, right = small[2 * i, :, 128:].astype(f32), small[2 * i + 1, :, 128:].astype(f32)
         upb[:, 128 * i : 128 * i + 128] = jnp.where(low, left[0:1], right[0:1])
 
 
-def first_kernel(sizes, members, others, *refs):
-    shard, live, tokens, grads = refs[:4]
-    weights_out, final, tg, total, vsum, usum, next_x, next_g, vec, upb = refs[4:14]
-    weights, x, g, wsend, wrecv, tsend, trecv, local = refs[14:22]
-    scratch = refs[22:]
-    own = shard.shape[0]
-    width, hidden = vec.shape[1], upb.shape[1]
+def at_points(index, plan):
+    for point, action in plan:
+        @pl.when(index == point)
+        def _(action=action):
+            action()
+
+
+def permute(target, source, table, m):
+    def one(n, carry):
+        target[n] = source[table[m, n]]
+        return carry
+
+    lax.fori_loop(0, target.shape[0], one, 0)
+
+
+def layer_kernel(sizes, members, others, *refs):
+    came_from, goes_to, slot, length, joint, small, mix, up, down, tokens, grads = refs[:11]
+    joint_out, mix_out, up_out, down_out, tail_out, layer_out, input_out = refs[11:18]
+    (shard, weights, held, taken, back_0, back_1, back_2, back_3, total, extra, live, vec, upb, vsum, usum,
+     wsend, wrecv, tsend, trecv, rsend, rrecv, local) = refs[18:40]
+    back = (back_0, back_1, back_2, back_3)
+    pools = [refs[40 + 4 * n : 44 + 4 * n] for n in range(4)]
+    scratch = refs[56:]
+    high = sizes[0]
+    own, hidden = up.shape
+    width = mix.shape[1]
+    piece = tokens.shape[2]
     devices = members * others
-    greet(members, others)
-    swaps = [
-        Swap(src, dst, local.at[n], tsend.at[n], trecv.at[n], members)
-        for n, (src, dst) in enumerate(
-            ((tokens.at[0], x), (grads.at[0], g), (tokens.at[1], next_x), (grads.at[1], next_g)))
+    z = lax.axis_index("dp") // 2
+
+    loads = [
+        pltpu.make_async_copy((grads if n % 2 else tokens).at[n // 2], back[n], local.at[n]) for n in range(4)
     ]
+    for load in loads:
+        load.start()
     mix_at = 3 * width + SMALL
     up_at = mix_at + width
     down_at = up_at + hidden
+    shard[:, : 3 * width] = joint[...]
+    shard[:, 3 * width : mix_at] = small[...]
+    shard[:, mix_at:up_at] = mix[...]
+    shard[:, up_at:down_at] = up[...]
+    shard[:, down_at:] = down[...]
+    loads[0].wait()
+    permute(held.at[0], back[0], came_from, 0)
+    greet(members, others)
+
+    into = [
+        Route(held.at[n], taken.at[n], local.at[4 + n], tsend.at[n], trecv.at[n], members) for n in range(4)
+    ]
+    returns = [
+        Route(held.at[n], back[n], local.at[8 + n], tsend.at[4 + n], trecv.at[4 + n], members) for n in range(4)
+    ]
+    results = [
+        pltpu.make_async_copy(taken.at[n], (input_out if n % 2 else layer_out).at[n // 2], local.at[12 + n])
+        for n in range(4)
+    ]
     ranges = (
         (pl.ds(0, 1024), (0, 1, 2, 3)),
         (pl.ds(1024, mix_at - 1024), (0, 2, 1, 3)),
+        (pl.ds(mix_at, width), (0, 1, 2, 3)),
         (pl.ds(up_at, hidden), (0, 1, 2, 3)),
         (pl.ds(down_at, hidden), (0, 2, 1, 3)),
-        (pl.ds(mix_at, width), (0, 1, 2, 3)),
     )
     gathers = [
-        Gather(shard, weights, cs, order, local.at[4 + n], wsend.at[n], wrecv.at[n], sizes)
+        Gather(shard, weights, cs, order, local.at[16 + n], wsend.at[n], wrecv.at[n], sizes)
         for n, (cs, order) in enumerate(ranges)
     ]
     early, late = gathers[:2], gathers[2:]
     for gather in early:
         gather.start(0)
-    swaps[0].start()
+    into[0].start()
+    for n in range(1, 4):
+        loads[n].wait()
+        permute(held.at[n], back[n], came_from, n // 2)
     for number in range(1, 4):
         for gather in early:
             gather.wait(number - 1)
             gather.start(number)
-    for gather in late:
-        gather.start(0)
-    swaps[1].start()
+    vsum[...] = jnp.zeros_like(vsum)
+    usum[...] = jnp.zeros_like(usum)
+
+    def mark(m):
+        places = lax.broadcasted_iota(jnp.int32, (piece, 1), 0)
+        for n in range(members):
+            live[n * piece : (n + 1) * piece, :] = jnp.where(
+                places + slot[m, n] * piece < length[m, 0], 1.0, 0.0)
 
     def weight(start, size):
         return weights[:, :, :, :, :, pl.ds(start, size)].reshape(width, size)
 
-    def put(k, value):
-        total[:, pl.ds(pl.multiple_of(k * 512, 512), 512)] = value
-
-    vsum[...] = jnp.zeros_like(vsum)
-    usum[...] = jnp.zeros_like(usum)
-    layer = Layer(x, g, live, weight, (mix_at, up_at, down_at), vec, upb, final, tg, put, vsum, usum, scratch)
-    layer.masks()
+    def columns(k):
+        return pl.ds(pl.multiple_of(k * 512, 512), 512)
+
+    def put_first(k, value):
+        total[:, :, :, :, :, columns(k)] = value.astype(bf16).reshape(sizes + (own, 512))
+
+    def put_second(k, value):
+        value = value + total[:, :, :, :, :, columns(k)].reshape(width, 512).astype(f32)
+        total[:, :, :, :, :, columns(k)] = value.astype(bf16).reshape(sizes + (own, 512))
+
+    def turn(s):
+        return lax.rem(z + s, high)
+
+    def turn_last(s):
+        return lax.rem(z + 1 + s, high)
+
+    def nothing(s):
+        pass
+
+    first, second = (
+        Layer(taken.at[2 * m], taken.at[2 * m + 1], live, weight, (mix_at, up_at, down_at), vec, upb,
+              held.at[2 * m], held.at[2 * m + 1], put, vsum, usum, scratch)
+        for m, put in enumerate((put_first, put_second))
+    )
+
+    mark(0)
+    first.masks()
     for gather in early:
         gather.wait(3)
     fill_vectors(weights[:, :, :, :, :, 3 * width : mix_at].reshape(devices, own, SMALL), vec, upb)
-    swaps[0].wait()
-    layer.project()
-
-    def relay(number):
+
+    def arrive_tokens(s):
+        @pl.when(s == high - 1)
+        def _():
+            for gather in late:
+                gather.start(0)
+            into[1].start()
+
+        into[0].take(s)
+
+    first.project(turn, arrive_tokens)
+
+    def relay(gather, number):
         def action():
-            for gather in late:
-                gather.wait(number - 1)
-                gather.start(number)
+            gather.wait(number - 1)
+            gather.start(number)
         return action
 
-    def hook(p):
-        for number in (1, 2, 3):
-            when_at(p, number - 1, relay(number))
-
-    layer.attend(hook)
+    points = ((0, 2, 4), (4, 8, 13), (8, 12, 15))
+    plan = [
+        (point, relay(gather, number + 1))
+        for gather, when in zip(late, points) for number, point in enumerate(when)
+    ]
+    plan.sort(key=lambda item: item[0])
+    first.attend(lambda h: at_points(h, plan))
     for gather in late:
         gather.wait(3)
-    swaps[1].wait()
-    swaps[2].start()
-    swaps[3].start()
-    keep = pltpu.make_async_copy(weights, weights_out, local.at[4 + len(ranges)])
-    keep.start()
-    layer.feed()
-    layer.down_grad()
-    layer.up_grad()
-    layer.mix_grad()
-    layer.attend_back(lambda p: None)
-    layer.joint_grad()
-    layer.first_back(lambda i: None)
-    keep.wait()
-    for swap in swaps[2:]:
-        swap.wait()
-    for item in swaps + gathers:
-        item.wait_sent()
-
-
-def second_kernel(sizes, members, others, *refs):
-    x, g, live, weights, vec, upb, previous, vprev, uprev, final0, tg0 = refs[:11]
-    outs = refs[11:16]
-    returned = refs[16:20]
-    refs = refs[20:]
-    final, tg, total, extra, vsum, usum, stage, wsend, wrecv, tsend, trecv, local, prior = refs[:13]
-    pools = [refs[13 + 7 * n : 20 + 7 * n] for n in range(4)]
-    scratch = refs[41:]
-    high = sizes[0]
-    width, hidden = vec.shape[1], upb.shape[1]
-    devices = members * others
-    own = width // devices
-    greet(members, others)
-    swaps = [
-        Swap(src, dst, local.at[n], tsend.at[n], trecv.at[n], members)
-        for n, (src, dst) in enumerate(zip((final0, tg0, final, tg), returned))
-    ]
-    swaps[0].start()
-    swaps[1].start()
-
-    def fetch(k):
-        slot = lax.rem(k, 2)
-        return pltpu.make_async_copy(
-            previous.at[:, pl.ds(pl.multiple_of(k * 512, 512), 512)], stage.at[slot], prior.at[slot])
-
-    chunks = (2 * hidden + 4 * width) // 512
-    fetch(0).start()
-
-    def put(k, value):
-        fetch(k).wait()
-
-        @pl.when(k + 1 < chunks)
+    into[0].wait_sent()
+
+    def arrive_grads(s):
+        into[1].take(s)
+
+        @pl.when(s == high - 1)
         def _():
-            fetch(k + 1).start()
-
-        value = (value + stage[lax.rem(k, 2)]).astype(bf16)
-        total[:, :, :, :, :, pl.ds(pl.multiple_of(k * 512, 512), 512)] = value.reshape(sizes + (own, 512))
-
-    def weight(start, size):
-        return weights[:, pl.ds(start, size)]
-
-    mix_at = 3 * width + SMALL
-    up_at = mix_at + width
-    down_at = up_at + hidden
-    vsum[...] = vprev[...]
-    usum[...] = uprev[...]
-    layer = Layer(x, g, live, weight, (mix_at, up_at, down_at), vec, upb, final, tg, put, vsum, usum, scratch)
-
-    def emit_to(ref, lo=None, hi=None):
+            into[2].start()
+            into[3].start()
+
+    first.feed(turn, arrive_grads)
+    returns[0].start()
+    into[1].wait_sent()
+    first.down_grad()
+    first.up_grad()
+    first.mix_grad()
+    first.attend_back(nothing)
+    first.joint_grad()
+    first.first_back(turn, nothing)
+    returns[1].start()
+
+    def emit_to(ref):
         def emit(value):
             ref[...] = value
         return emit
 
-    joint_at = 2 * hidden + width
-    down, up, rest, tail = (
-        Exchange(grads, cs, wide_first, emit, pools[n], wsend.at[n], wrecv.at[n], high)
-        for n, (grads, cs, wide_first, emit) in enumerate((
-            (total, pl.ds(0, hidden), True, emit_to(outs[3])),
-            (total, pl.ds(hidden, hidden + width), False, lambda v: emit_pair(v)),
-            (total, pl.ds(joint_at, 3 * width), True, emit_to(outs[0])),
-            (extra, pl.ds(0, SMALL), False, emit_to(outs[4])),
+    def emit_pair(value):
+        up_out[...] = value[:, :hidden]
+        mix_out[...] = value[:, hidden:]
+
+    downs, ups, rest, last = (
+        Exchange(source, cs, wide_first, emit, pools[n], rsend.at[n], rrecv.at[n], high)
+        for n, (source, cs, wide_first, emit) in enumerate((
+            (total, pl.ds(0, hidden), True, emit_to(down_out)),
+            (total, pl.ds(hidden, hidden + width), False, emit_pair),
+            (total, pl.ds(2 * hidden + width, 3 * width), True, emit_to(joint_out)),
+            (extra, pl.ds(0, SMALL), False, emit_to(tail_out)),
         ))
     )
-
-    def emit_pair(value):
-        outs[2][...] = value[:, :hidden]
-        outs[1][...] = value[:, hidden:]
-
-    layer.masks()
-    layer.project()
-    layer.attend(lambda p: None)
-    layer.feed()
-    layer.down_grad()
-    layer.up_grad()
-    down.start()
-    layer.mix_grad()
-    swaps[2].start()
-
-    def hook(p):
-        for number in range(4):
-            when_at(p, number, lambda number=number: down.step(number))
-        when_at(p, 0, up.start)
-        for number in range(3):
-            when_at(p, number + 1, lambda number=number: up.step(number))
-
-    layer.attend_back(hook)
-    layer.joint_grad()
-    up.step(3)
+    mark(1)
+    second.masks()
+    into[2].wait()
+    second.project(turn, nothing)
+    second.attend(nothing)
+    into[2].wait_sent()
+    into[3].wait()
+    second.feed(turn, nothing)
+    returns[2].start()
+    into[3].wait_sent()
+    second.down_grad()
+    downs.start()
+    second.up_grad()
+    second.mix_grad()
+    ups.start()
+
+    def result(n):
+        def action():
+            returns[n].wait()
+            permute(taken.at[n], back[n], goes_to, n // 2)
+            results[n].start()
+        return action
+
+    def step(exchange, number):
+        return lambda: exchange.step(number)
+
+    plan_back = [
+        (0, step(downs, 0)), (1, step(ups, 0)), (3, result(0)), (6, step(downs, 1)), (8, step(ups, 1)),
+        (9, result(1)), (10, step(downs, 2)), (12, step(ups, 2)), (15, step(downs, 3)),
+    ]
+    second.attend_back(lambda h: at_points(h, plan_back))
+
+    def send_grads(s):
+        returns[3].give(lax.rem(s + 1, high))
+
+    second.first_back(turn_last, send_grads)
+    second.joint_grad()
     rest.start()
-    first = swaps[3]
-    per = BLK // tg.shape[1]
-    me = lax.axis_index("dp")
-
-    layer.first_back(lambda i: None)
-    first.start()
-    vectors = jnp.concatenate([vsum[...], jnp.zeros((120, width), f32)], axis=0).T
-    extra[:, :, :, :, :, :128] = vectors.astype(bf16).reshape(sizes + (own, 128))
+    turned = jnp.concatenate([vsum[...], jnp.zeros((120, width), f32)], axis=0).T
+    extra[:, :, :, :, :, :128] = turned.astype(bf16).reshape(sizes + (own, 128))
     for n in range(devices):
         a, b, c, e = n // (2 * others), (n // others) % 2, (n % others) // 2, n % 2
-        piece = usum[:, 128 * (n // 2) : 128 * (n // 2) + 128]
-        extra[a, b, c, e, :, 128:] = jnp.broadcast_to(piece, (own, 128)).astype(bf16)
-    tail.start()
-    for number in range(4):
+        part = usum[:, 128 * (n // 2) : 128 * (n // 2) + 128]
+        extra[a, b, c, e, :, 128:] = jnp.broadcast_to(part, (own, 128)).astype(bf16)
+    last.start()
+    ups.step(3)
+    rest.step(0)
+    last.step(0)
+    result(2)()
+    for number in range(1, 4):
         rest.step(number)
-        tail.step(number)
-    for swap in swaps:
-        swap.wait()
-    for item in swaps + [down, up, rest, tail]:
+        last.step(number)
+    result(3)()
+    for item in gathers + returns + [downs, ups, rest, last]:
         item.wait_sent()
-
-
-def first_call(shard, live, tokens, grads, members, others, hidden):
-    own, columns = shard.shape
-    micro, _, piece, width = tokens.shape
+    for item in results:
+        item.wait()
+
+
+def layer_call(tables, shards, tokens, grads, members, others):
+    joint, small, mix, up, down = shards
+    own, hidden = up.shape
+    _, _, piece, width = tokens.shape
     rows = members * piece
     sizes = (members // 2, 2, others // 2, 2)
-    slots = sizes[0] + 1 + sizes[2]
-    block = jax.ShapeDtypeStruct((members, piece, width), bf16)
+    high = sizes[0]
+    slots = high + 1 + sizes[2]
+    columns = 4 * width + 2 * hidden
     dma = pltpu.SemaphoreType.DMA
+    smem = pl.BlockSpec(memory_space=pltpu.SMEM)
+    pools = []
+    for count in (hidden, hidden + width, 3 * width, SMALL):
+        pools += exchange_scratch(high, own, count)
+    shapes = [(own, 3 * width), (own, width), (own, hidden), (own, hidden), (own, SMALL)]
+    blocks = pltpu.VMEM((4, members, piece, width), bf16)
     return pl.pallas_call(
-        functools.partial(first_kernel, sizes, members, others),
-        out_shape=(
-            jax.ShapeDtypeStruct(sizes + (own, columns), bf16), block, block,
-            jax.ShapeDtypeStruct((width, 2 * hidden + 4 * width), f32),
-            jax.ShapeDtypeStruct((8, width), f32), jax.ShapeDtypeStruct((1, hidden), f32), block, block,
-            jax.ShapeDtypeStruct((8, width), f32), jax.ShapeDtypeStruct((1, hidden), f32),
-        ),
-        in_specs=[VMEM, VMEM, ANY, ANY],
-        out_specs=(ANY,) + (VMEM,) * 5 + (ANY,) * 2 + (VMEM,) * 2,
+        functools.partial(layer_kernel, sizes, members, others),
+        out_shape=tuple(jax.ShapeDtypeStruct(shape, f32) for shape in shapes)
+        + (jax.ShapeDtypeStruct(tokens.shape, bf16),) * 2,
+        in_specs=[smem] * 4 + [VMEM] * 5 + [ANY] * 2,
+        out_specs=(VMEM,) * 5 + (ANY,) * 2,
         scratch_shapes=[
+            pltpu.VMEM((own, columns + SMALL), bf16),
+            pltpu.VMEM(sizes + (own, columns + SMALL), bf16),
+            blocks, blocks,
+        ] + [pltpu.VMEM((members, piece, width), bf16)] * 4 + [
             pltpu.VMEM(sizes + (own, columns), bf16),
-            pltpu.VMEM((members, piece, width), bf16),
-            pltpu.VMEM((members, piece, width), bf16),
-            dma((5, slots)), dma((5, slots)), dma((4, members)), dma((4, members)), dma((10,)),
-        ] + layer_scratch(rows, width, hidden),
+            pltpu.VMEM(sizes + (own, SMALL), bf16),
+            pltpu.VMEM((rows, 1), f32),
+            pltpu.VMEM((8, width), f32), pltpu.VMEM((1, hidden), f32),
+            pltpu.VMEM((8, width), f32), pltpu.VMEM((1, hidden), f32),
+            dma((5, slots)), dma((5, slots)), dma((8, members)), dma((8, members)),
+            dma((4, high + 2)), dma((4, high + 2)), dma((21,)),
+        ] + pools + layer_scratch(rows, width, hidden),
         compiler_params=pltpu.CompilerParams(
             collective_id=2, has_side_effects=True, vmem_limit_bytes=67_043_328),
-        name="first_sequence",
-    )(shard, live, tokens, grads)
-
-
-def second_call(x, g, live, weights, vec, upb, previous, vprev, uprev, final0, tg0, members, others):
-    _, piece, width = x.shape
-    rows, hidden = members * piece, upb.shape[1]
-    sizes = (members // 2, 2, others // 2, 2)
-    own = width // (members * others)
-    dma = pltpu.SemaphoreType.DMA
-    block = jax.ShapeDtypeStruct((members, piece, width), bf16)
-    pools = []
-    for columns in (hidden, hidden + width, 3 * width, SMALL):
-        pools += reduce_scratch(sizes[0], own, columns)
-    shapes = [(own, 3 * width), (own, width), (own, hidden), (own, hidden), (own, SMALL)]
-    return pl.pallas_call(
-        functools.partial(second_kernel, sizes, members, others),
-        out_shape=tuple(jax.ShapeDtypeStruct(shape, f32) for shape in shapes) + (block,) * 4,
-        in_specs=[VMEM] * 6 + [ANY] + [VMEM] * 2 + [ANY] * 2,
-        out_specs=(VMEM,) * 5 + (ANY,) * 4,
-        scratch_shapes=[
-            pltpu.VMEM((members, piece, width), bf16),
-            pltpu.VMEM((members, piece, width), bf16),
-            pltpu.VMEM(sizes + (own, 2 * hidden + 4 * width), bf16),
-            pltpu.VMEM(sizes + (own, SMALL), bf16),
-            pltpu.VMEM((8, width), f32),
-            pltpu.VMEM((1, hidden), f32),
-            pltpu.VMEM((2, width, 512), f32),
-            dma((4, sizes[0] + 2)), dma((4, sizes[0] + 2)), dma((4, members)), dma((4, members)), dma((4,)), dma((2,)),
-        ] + pools + layer_scratch(rows, width, hidden),
-        compiler_params=pltpu.CompilerParams(
-            collective_id=3, has_side_effects=True, vmem_limit_bytes=67_043_328),
-        name="second_sequence",
-    )(x, g, live, weights, vec, upb, previous, vprev, uprev, final0, tg0)
+        name="layer",
+    )(*tables, *shards, tokens, grads)
 
 
 def fused_body(
@@ -1344,25 +1443,17 @@
 ):
     members, others = lax.axis_size("dp"), lax.axis_size("fsdp")
     micro, rows, width = tokens.shape
-    piece = rows // members
     own = first_gain.shape[0]
-    hidden = down_weight.shape[0]
-    vectors = (first_gain, first_shift, query_bias, value_bias, mix_bias, second_gain, second_shift, down_bias)
-    twice = jnp.broadcast_to(jnp.concatenate([up_bias, up_bias])[None], (own, 128))
-    small = jnp.concatenate([jnp.stack(vectors, axis=1), jnp.zeros((own, 120), bf16), twice], axis=1)
-    shard = jnp.concatenate([joint_weight, small, mix_weight, up_weight, down_weight.T], axis=1)
-    table = send_to[:, 0]
-    pieces = (micro, members, piece, width)
-    sent, sent_grad = reorder(True, table, tokens.reshape(pieces), out_grad.reshape(pieces))
-    spots = slot_of[:, 0, :, None] * piece + jnp.arange(piece, dtype=jnp.int32)
-    live = (spots.reshape(micro, rows) < seq_lengths).astype(f32)[:, :, None]
-    weights, final0, tg0, total, vsum, usum, x, g, vec, upb = first_call(
-        shard, live[0], sent, sent_grad, members, others, hidden)
-    whole = weights.reshape(width, shard.shape[1])
-    joint, mix, up, down, tail, *returned = second_call(
-        x, g, live[1], whole, vec, upb, total, vsum, usum, final0, tg0, members, others)
-    layer_output, input_grad = reorder(
-        False, table, jnp.stack([returned[0], returned[2]]), jnp.stack([returned[1], returned[3]]))
+    parts = (first_gain, first_shift, query_bias, value_bias, mix_bias, second_gain, second_shift, down_bias,
+             up_bias, up_bias)
+    small = jnp.broadcast_to(jnp.concatenate(parts)[None], (own, SMALL))
+    goes_to = send_to[:, 0]
+    order = jnp.arange(members, dtype=jnp.int32)
+    came_from = jnp.sum(jnp.where(goes_to[:, :, None] == order, order[None, :, None], 0), axis=1).astype(jnp.int32)
+    pieces = (micro, members, rows // members, width)
+    joint, mix, up, down, tail, layer_output, input_grad = layer_call(
+        (came_from, goes_to, slot_of[:, 0], seq_lengths), (joint_weight, small, mix_weight, up_weight, down_weight.T),
+        tokens.reshape(pieces), out_grad.reshape(pieces), members, others)
     vec_grad = [tail[:, n] for n in range(8)]
     odd = lax.rem(lax.axis_index("fsdp"), 2) == 1
     up_bias_grad = jnp.where(odd, tail[0, 192:256], tail[0, 128:192])

time: 331 us -> 307 us (0.927)
  Pallas kernels: 315 us -> 285 us
  local copies, waits for them, and re-layouts: 8.43 us -> 17.6 us
    pallas_call x4 -> x1, Pallas kernels: 315 us -> 285 us  [layer_call(): pl.pallas_call(functools.partial(layer_kernel, sizes, members, others), o...]
    concatenate x1, local copies, waits for them, and re-layouts: 0.79 us -> 6.77 us  [fused_body(): small = jnp.broadcast_to(jnp.concatenate(parts)[None], (own, SMALL))]
    unnamed x45 -> x17, local copies, waits for them, and re-layouts: 2.73 us -> 8.4 us
    another operation x1 -> x0, other arithmetic: 4.5 us -> none  [fused_body(): jnp.stack([returned[0], returned[2]])]
    squeeze x3 -> x0, local copies, waits for them, and re-layouts: 3.33 us -> none  [the longest x2 2.31 us: fused_body(): live[1]]
where the time goes in v3:
time: 307 us; the launch traced here: 306 us
  Pallas kernels  285 us (93%)
  local copies, waits for them, and re-layouts  17.6 us (6%)
    pallas_call x1, Pallas kernels, layer_call(): pl.pallas_call(functools.partial(layer_kernel, sizes, members, others), o...  285 us
    unnamed x17, local copies, waits for them, and re-layouts  8.4 us
    concatenate x1, local copies, waits for them, and re-layouts, fused_body(): small = jnp.broadcast_to(jnp.concatenate(parts)[None], (own, SMALL))  6.77 us

profile of v3, /device:TPU:0, one launch (start us, length us, event | category | flops | bytes accessed | tf_op | source)
XLA Modules:
  0.0 305.8 jit_solution(14626535031855201155)
XLA Ops:
  0.6 1.3 select_reduce_fusion.refs_0_
  2.0 6.8 %concatenate.3 = bf16[256]{0:T(256)(128)(2,1)S(1)} concatenate(bf16[16]{0:T(256)(128)(2,1)} %param.23, bf16[16]{0:T(256)(128)(2,1)} %param.24, bf16[16]{0:T(256)(128)(2,1)} %param.26, bf16[16]{0:T(256)(128)(2,1)} %param.27, bf16[16]{0:T(256)(128)(2,1)} %param.29, bf16[16]{0:T(256)(128)(2,1)} %param.30, bf16[16]{0:T(256)(128)(2,1)} %param.31, bf16[16]{0:T(256)(128)(2,1)} %param.35, ...), dimensions={0} | concatenate | bytes 1024 | tf_op jit(solution)/shard_map/concatenate | solution.py:1449
  8.7 0.6 broadcast_in_dim.22.refs_5_
  9.3 1.3 copy.35.refs_3_
  10.6 284.9 %layer.1 = (f32[16,1536]{1,0:T(8,128)}, f32[16,512]{1,0:T(8,128)}, f32[16,2048]{1,0:T(8,128)}, f32[16,2048]{1,0:T(8,128)}, f32[16,256]{1,0:T(8,128)}, /*index=5*...) custom-call(s32[2,8]{1,0:T(2,128)} %select_reduce_fusion.refs_0_, s32[2,8]{1,0:T(2,128)} %bitcast.17, ...), custom_call_target="tpu_custom_call" | custom-call | tf_op jit(solution)/shard_map/layer/pallas_call | solution.py:1415
  295.5 1.3 fusion
  296.9 1.8 slice_reduce_fusion
  298.7 0.0 copy-start
  298.7 3.2 %copy.42 = bf16[2,1024,512]{2,1,0:T(8,128)(2,1)} copy(bf16[2,1024,512]{2,1,0:T(8,128)(2,1)} %bitcast.13) | data formatting | bytes 4194304
  301.9 0.0 copy-done
  301.9 0.0 copy-start.3
  301.9 0.0 copy-start.4
  301.9 0.0 copy-start.2
  301.9 0.0 copy-start.1
  301.9 1.3 copy.43
  303.2 0.0 copy-done.3
  303.2 0.6 copy.44
  303.9 0.0 copy-done.4
  303.9 0.6 copy.45
  304.5 0.0 copy-done.2
  304.5 0.7 copy.46
  305.1 0.0 copy-done.1
  305.1 0.7 copy.47
Async XLA Ops:
  298.7 3.2 %copy-start = (bf16[2,8,128,512]{3,2,1,0:T(8,128)(2,1)S(1)}, bf16[2,8,128,512]{3,2,1,0:T(8,128)(2,1)}, u32[]{:S(2)}) copy-start(bf16[2,8,128,512]{3,2,1,0:T(8,128)(2,1)} %get-tuple-element.23) | copy-start | bytes 6291460
  301.9 1.3 copy-start.3
  301.9 2.0 copy-start.4
  301.9 2.6 copy-start.2
  301.9 3.3 %copy-start.1 = (f32[16,2048]{1,0:T(8,128)S(1)}, f32[16,2048]{1,0:T(8,128)}, u32[]{:S(2)}) copy-start(f32[16,2048]{1,0:T(8,128)} %get-tuple-element.28) | copy-start | bytes 393220

commit v4 on v3

--- a/solution.py
+++ b/solution.py
@@ -824,7 +824,7 @@
 
         lax.fori_loop(0, self.pairs, pair, 0)
 
-    def feed(self, turn, arrive):
+    def feed(self, turn, arrive, ready):
         chunk = 512
         mix_at, up_at, down_at = self.offsets
 
@@ -848,6 +848,7 @@
             self.acc_b[...] = jnp.zeros_like(self.acc_b)
 
             def part(c, carry):
+                ready(s, c)
                 cs = self.at(c, chunk)
                 up = self.weight(pl.multiple_of(up_at + c * chunk, 128), chunk)
                 down = self.weight(pl.multiple_of(down_at + c * chunk, 128), chunk)
@@ -1019,15 +1020,23 @@
         return 2 * block, 2 * block + 1
 
     def start(self):
-        for s in range(1, self.members):
-            self.outgoing(lax.rem(self.me + s, self.members)).start()
+        self.start_direct()
+        self.start_others()
+
+    def start_direct(self):
+        for s in range(1, self.members // 2):
+            self.outgoing(lax.rem(self.me + 2 * s, self.members)).start()
+        self.outgoing(self.beside()).start()
         self.own.start()
+
+    def start_others(self):
+        for s in range(1, self.members // 2):
+            self.outgoing(lax.rem(self.beside() + 2 * s, self.members)).start()
 
     def give(self, s):
         @pl.when(s > 0)
         def _():
-            for to in self.pair(s):
-                self.outgoing(to).start()
+            self.outgoing(lax.rem(self.me + 2 * s, self.members)).start()
 
         @pl.when(s == 0)
         def _():
@@ -1157,22 +1166,30 @@
             action()
 
 
-def permute(target, source, table, m):
+def permute(target, source, table, m, inverse=False):
+    count = target.shape[0]
+
     def one(n, carry):
-        target[n] = source[table[m, n]]
+        if inverse:
+            spot = jnp.int32(0)
+            for k in range(1, count):
+                spot = jnp.where(table[m, k] == n, k, spot)
+        else:
+            spot = table[m, n]
+        target[n] = source[spot]
         return carry
 
-    lax.fori_loop(0, target.shape[0], one, 0)
+    lax.fori_loop(0, count, one, 0)
 
 
 def layer_kernel(sizes, members, others, *refs):
-    came_from, goes_to, slot, length, joint, small, mix, up, down, tokens, grads = refs[:11]
-    joint_out, mix_out, up_out, down_out, tail_out, layer_out, input_out = refs[11:18]
+    goes_to, slot, length, joint, mix, up, down, *vectors, tokens, grads = refs[:18]
+    joint_out, mix_out, up_out, down_out, tail_out, bias_out, layer_out, input_out = refs[18:26]
     (shard, weights, held, taken, back_0, back_1, back_2, back_3, total, extra, live, vec, upb, vsum, usum,
-     wsend, wrecv, tsend, trecv, rsend, rrecv, local) = refs[18:40]
+     wsend, wrecv, tsend, trecv, rsend, rrecv, local) = refs[26:48]
     back = (back_0, back_1, back_2, back_3)
-    pools = [refs[40 + 4 * n : 44 + 4 * n] for n in range(4)]
-    scratch = refs[56:]
+    pools = [refs[48 + 4 * n : 52 + 4 * n] for n in range(4)]
+    scratch = refs[64:]
     high = sizes[0]
     own, hidden = up.shape
     width = mix.shape[1]
@@ -1189,12 +1206,13 @@
     up_at = mix_at + width
     down_at = up_at + hidden
     shard[:, : 3 * width] = joint[...]
-    shard[:, 3 * width : mix_at] = small[...]
+    spread = [jnp.broadcast_to(vector[...].astype(f32), (own, vector.shape[1])) for vector in vectors]
+    shard[:, 3 * width : mix_at] = jnp.concatenate(spread + spread[-1:], axis=1).astype(bf16)
     shard[:, mix_at:up_at] = mix[...]
     shard[:, up_at:down_at] = up[...]
     shard[:, down_at:] = down[...]
     loads[0].wait()
-    permute(held.at[0], back[0], came_from, 0)
+    permute(held.at[0], back[0], goes_to, 0, inverse=True)
     greet(members, others)
 
     into = [
@@ -1211,8 +1229,10 @@
         (pl.ds(0, 1024), (0, 1, 2, 3)),
         (pl.ds(1024, mix_at - 1024), (0, 2, 1, 3)),
         (pl.ds(mix_at, width), (0, 1, 2, 3)),
-        (pl.ds(up_at, hidden), (0, 1, 2, 3)),
-        (pl.ds(down_at, hidden), (0, 2, 1, 3)),
+        (pl.ds(up_at, hidden // 2), (0, 1, 2, 3)),
+        (pl.ds(down_at, hidden // 2), (0, 2, 1, 3)),
+        (pl.ds(up_at + hidden // 2, hidden // 2), (0, 1, 2, 3)),
+        (pl.ds(down_at + hidden // 2, hidden // 2), (0, 2, 1, 3)),
     )
     gathers = [
         Gather(shard, weights, cs, order, local.at[16 + n], wsend.at[n], wrecv.at[n], sizes)
@@ -1221,14 +1241,16 @@
     early, late = gathers[:2], gathers[2:]
     for gather in early:
         gather.start(0)
-    into[0].start()
+    into[0].start_direct()
     for n in range(1, 4):
         loads[n].wait()
-        permute(held.at[n], back[n], came_from, n // 2)
+        permute(held.at[n], back[n], goes_to, n // 2, inverse=True)
     for number in range(1, 4):
         for gather in early:
             gather.wait(number - 1)
             gather.start(number)
+        if number == 2:
+            into[0].start_others()
     vsum[...] = jnp.zeros_like(vsum)
     usum[...] = jnp.zeros_like(usum)
 
@@ -1236,7 +1258,7 @@
         places = lax.broadcasted_iota(jnp.int32, (piece, 1), 0)
         for n in range(members):
             live[n * piece : (n + 1) * piece, :] = jnp.where(
-                places + slot[m, n] * piece < length[m, 0], 1.0, 0.0)
+                places + slot[m, n] * piece < length[0, m], 1.0, 0.0)
 
     def weight(start, size):
         return weights[:, :, :, :, :, pl.ds(start, size)].reshape(width, size)
@@ -1277,7 +1299,7 @@
         def _():
             for gather in late:
                 gather.start(0)
-            into[1].start()
+            into[1].start_direct()
 
         into[0].take(s)
 
@@ -1289,16 +1311,27 @@
             gather.start(number)
         return action
 
-    points = ((0, 2, 4), (4, 8, 13), (8, 12, 15))
+    mixed, up_0, down_0, up_1, down_1 = late
     plan = [
-        (point, relay(gather, number + 1))
-        for gather, when in zip(late, points) for number, point in enumerate(when)
+        (0, relay(mixed, 1)), (1, relay(up_0, 1)), (2, relay(mixed, 2)), (3, relay(down_0, 1)), (4, relay(up_0, 2)),
+        (5, relay(mixed, 3)), (6, relay(up_1, 1)), (6, relay(down_0, 2)), (8, relay(down_1, 1)), (11, relay(up_1, 2)),
+        (12, relay(up_0, 3)), (13, relay(down_1, 2)), (13, into[1].start_others), (14, relay(down_0, 3)),
     ]
-    plan.sort(key=lambda item: item[0])
     first.attend(lambda h: at_points(h, plan))
-    for gather in late:
+    for gather in late[:3]:
         gather.wait(3)
     into[0].wait_sent()
+
+    def ready(s, c):
+        @pl.when((s == 0) & (c == 1))
+        def _():
+            relay(up_1, 3)()
+            relay(down_1, 3)()
+
+        @pl.when((s == 0) & (c == 2))
+        def _():
+            up_1.wait(3)
+            down_1.wait(3)
 
     def arrive_grads(s):
         into[1].take(s)
@@ -1308,7 +1341,7 @@
             into[2].start()
             into[3].start()
 
-    first.feed(turn, arrive_grads)
+    first.feed(turn, arrive_grads, ready)
     returns[0].start()
     into[1].wait_sent()
     first.down_grad()
@@ -1324,6 +1357,11 @@
             ref[...] = value
         return emit
 
+    def emit_tail(value):
+        tail_out[...] = value[:, :128].T[:8]
+        odd = lax.rem(lax.axis_index("fsdp"), 2) == 1
+        bias_out[...] = jnp.where(odd, value[:1, 192:256], value[:1, 128:192])
+
     def emit_pair(value):
         up_out[...] = value[:, :hidden]
         mix_out[...] = value[:, hidden:]
@@ -1333,8 +1371,8 @@
         for n, (source, cs, wide_first, emit) in enumerate((
             (total, pl.ds(0, hidden), True, emit_to(down_out)),
             (total, pl.ds(hidden, hidden + width), False, emit_pair),
-            (total, pl.ds(2 * hidden + width, 3 * width), True, emit_to(joint_out)),
-            (extra, pl.ds(0, SMALL), False, emit_to(tail_out)),
+            (total, pl.ds(2 * hidden + width, 3 * width), False, emit_to(joint_out)),
+            (extra, pl.ds(0, SMALL), False, emit_tail),
         ))
     )
     mark(1)
@@ -1344,7 +1382,7 @@
     second.attend(nothing)
     into[2].wait_sent()
     into[3].wait()
-    second.feed(turn, nothing)
+    second.feed(turn, nothing, lambda s, c: None)
     returns[2].start()
     into[3].wait_sent()
     second.down_grad()
@@ -1382,9 +1420,10 @@
         part = usum[:, 128 * (n // 2) : 128 * (n // 2) + 128]
         extra[a, b, c, e, :, 128:] = jnp.broadcast_to(part, (own, 128)).astype(bf16)
     last.start()
-    ups.step(3)
     rest.step(0)
     last.step(0)
+    returns[3].start_others()
+    ups.step(3)
     result(2)()
     for number in range(1, 4):
         rest.step(number)
@@ -1397,7 +1436,7 @@
 
 
 def layer_call(tables, shards, tokens, grads, members, others):
-    joint, small, mix, up, down = shards
+    joint, mix, up, down, *vectors = shards
     own, hidden = up.shape
     _, _, piece, width = tokens.shape
     rows = members * piece
@@ -1410,14 +1449,14 @@
     pools = []
     for count in (hidden, hidden + width, 3 * width, SMALL):
         pools += exchange_scratch(high, own, count)
-    shapes = [(own, 3 * width), (own, width), (own, hidden), (own, hidden), (own, SMALL)]
+    shapes = [(own, 3 * width), (own, width), (own, hidden), (own, hidden), (8, own), (1, 2 * SMALL // 8)]
     blocks = pltpu.VMEM((4, members, piece, width), bf16)
     return pl.pallas_call(
         functools.partial(layer_kernel, sizes, members, others),
         out_shape=tuple(jax.ShapeDtypeStruct(shape, f32) for shape in shapes)
         + (jax.ShapeDtypeStruct(tokens.shape, bf16),) * 2,
-        in_specs=[smem] * 4 + [VMEM] * 5 + [ANY] * 2,
-        out_specs=(VMEM,) * 5 + (ANY,) * 2,
+        in_specs=[smem] * 3 + [VMEM] * (4 + len(vectors)) + [ANY] * 2,
+        out_specs=(VMEM,) * 6 + (ANY,) * 2,
         scratch_shapes=[
             pltpu.VMEM((own, columns + SMALL), bf16),
             pltpu.VMEM(sizes + (own, columns + SMALL), bf16),
@@ -1428,8 +1467,8 @@
             pltpu.VMEM((rows, 1), f32),
             pltpu.VMEM((8, width), f32), pltpu.VMEM((1, hidden), f32),
             pltpu.VMEM((8, width), f32), pltpu.VMEM((1, hidden), f32),
-            dma((5, slots)), dma((5, slots)), dma((8, members)), dma((8, members)),
-            dma((4, high + 2)), dma((4, high + 2)), dma((21,)),
+            dma((7, slots)), dma((7, slots)), dma((8, members)), dma((8, members)),
+            dma((4, high + 2)), dma((4, high + 2)), dma((23,)),
         ] + pools + layer_scratch(rows, width, hidden),
         compiler_params=pltpu.CompilerParams(
             collective_id=2, has_side_effects=True, vmem_limit_bytes=67_043_328),
@@ -1443,24 +1482,17 @@
 ):
     members, others = lax.axis_size("dp"), lax.axis_size("fsdp")
     micro, rows, width = tokens.shape
-    own = first_gain.shape[0]
-    parts = (first_gain, first_shift, query_bias, value_bias, mix_bias, second_gain, second_shift, down_bias,
-             up_bias, up_bias)
-    small = jnp.broadcast_to(jnp.concatenate(parts)[None], (own, SMALL))
-    goes_to = send_to[:, 0]
-    order = jnp.arange(members, dtype=jnp.int32)
-    came_from = jnp.sum(jnp.where(goes_to[:, :, None] == order, order[None, :, None], 0), axis=1).astype(jnp.int32)
+    vectors = (first_gain, first_shift, query_bias, value_bias, mix_bias, second_gain, second_shift, down_bias, up_bias)
     pieces = (micro, members, rows // members, width)
-    joint, mix, up, down, tail, layer_output, input_grad = layer_call(
-        (came_from, goes_to, slot_of[:, 0], seq_lengths), (joint_weight, small, mix_weight, up_weight, down_weight.T),
+    joint, mix, up, down, tail, bias, layer_output, input_grad = layer_call(
+        (send_to[:, 0], slot_of[:, 0], seq_lengths.reshape(1, micro)),
+        (joint_weight, mix_weight, up_weight, down_weight.T) + tuple(vector[None] for vector in vectors),
         tokens.reshape(pieces), out_grad.reshape(pieces), members, others)
-    vec_grad = [tail[:, n] for n in range(8)]
-    odd = lax.rem(lax.axis_index("fsdp"), 2) == 1
-    up_bias_grad = jnp.where(odd, tail[0, 192:256], tail[0, 128:192])
+    vec_grad = [tail[n] for n in range(8)]
     return (
         layer_output.reshape(tokens.shape), input_grad.reshape(tokens.shape),
         vec_grad[0], vec_grad[1], joint, vec_grad[2], vec_grad[3], mix, vec_grad[4], vec_grad[5], vec_grad[6],
-        up, up_bias_grad, down.T, vec_grad[7],
+        up, bias[0], down.T, vec_grad[7],
     )
 
 

time: 307 us -> 285 us (0.928)
  Pallas kernels: 285 us -> 275 us
  local copies, waits for them, and re-layouts: 17.6 us -> 9.13 us
    pallas_call x1, Pallas kernels: 285 us -> 275 us  [layer_call(): pl.pallas_call(functools.partial(layer_kernel, sizes, members, others), o...]
    concatenate x1 -> x0, local copies, waits for them, and re-layouts: 6.77 us -> none  [fused_body(): small = jnp.broadcast_to(jnp.concatenate(parts)[None], (own, SMALL))]
    unnamed x17 -> x19, local copies, waits for them, and re-layouts: 8.4 us -> 7.62 us
where the time goes in v4:
time: 285 us
  Pallas kernels  275 us (96%)
  local copies, waits for them, and re-layouts  9.13 us (3%)
    pallas_call x1, Pallas kernels, layer_call(): pl.pallas_call(functools.partial(layer_kernel, sizes, members, others), o...  275 us
    unnamed x19, local copies, waits for them, and re-layouts  7.62 us

profile of v4, /device:TPU:0, one launch (start us, length us, event | category | flops | bytes accessed | tf_op | source)
XLA Modules:
  0.0 284.5 jit_solution(18090489994567599710)
XLA Ops:
  0.7 274.7 %layer.1 = (f32[16,1536]{1,0:T(8,128)}, f32[16,512]{1,0:T(8,128)}, f32[16,2048]{1,0:T(8,128)}, f32[16,2048]{1,0:T(8,128)}, f32[8,16]{1,0:T(8,128)}, /*index=5*/f...) custom-call(s32[2,8]{1,0:T(2,128)} %bitcast.41, s32[2,8]{1,0:T(2,128)} %bitcast.42, ...), custom_call_target="tpu_custom_call" | custom-call | tf_op jit(solution)/shard_map/layer/pallas_call | solution.py:1454
  275.4 1.5 slice_bitcast_fusion
  276.9 0.0 copy-start
  276.9 3.2 %copy.40 = bf16[2,1024,512]{2,1,0:T(8,128)(2,1)} copy(bf16[2,1024,512]{2,1,0:T(8,128)(2,1)} %bitcast.36) | data formatting | bytes 4194304
  280.1 0.0 copy-done
  280.1 0.0 copy-start.3
  280.1 0.0 copy-start.4
  280.1 0.0 copy-start.2
  280.1 0.0 copy-start.5
  280.1 0.0 copy-start.1
  280.1 1.3 copy.41
  281.4 0.0 copy-done.3
  281.4 0.6 copy.42
  282.1 0.0 copy-done.4
  282.1 0.6 copy.43
  282.7 0.0 copy-done.2
  282.7 0.7 copy.44
  283.3 0.0 copy-done.5
  283.3 0.5 copy.45
  283.9 0.0 copy-done.1
  283.9 0.7 copy.46
Async XLA Ops:
  276.9 3.2 %copy-start = (bf16[2,8,128,512]{3,2,1,0:T(8,128)(2,1)S(1)}, bf16[2,8,128,512]{3,2,1,0:T(8,128)(2,1)}, u32[]{:S(2)}) copy-start(bf16[2,8,128,512]{3,2,1,0:T(8,128)(2,1)} %get-tuple-element.24) | copy-start | bytes 6291460
  280.1 1.4 copy-start.3
  280.1 2.0 copy-start.4
  280.1 2.6 copy-start.2
  280.1 3.3 %copy-start.5 = (f32[1,64]{1,0:T(1,128)S(1)}, f32[1,64]{1,0:T(1,128)}, u32[]{:S(2)}) copy-start(f32[1,64]{1,0:T(1,128)} %get-tuple-element.29) | copy-start | bytes 772
  280.1 3.8 %copy-start.1 = (f32[16,2048]{1,0:T(8,128)S(1)}, f32[16,2048]{1,0:T(8,128)}, u32[]{:S(2)}) copy-start(f32[16,2048]{1,0:T(8,128)} %get-tuple-element.30) | copy-start | bytes 393220

commit v5 on v4

--- a/solution.py
+++ b/solution.py
@@ -881,7 +881,7 @@
 
     def wide(self, lhs_t, rhs, base, count):
         def one(c, carry):
-            self.put(base + c, nn(lhs_t[...], rhs[c]))
+            self.put((base + c) * 512, nn(lhs_t[...], rhs[c]))
             return carry
 
         lax.fori_loop(0, count, one, 0)
@@ -893,12 +893,9 @@
         self.wide(self.second_t, self.pre, self.hidden // 512, self.hidden // 512)
 
     def mix_grad(self):
-        self.put(2 * self.hidden // 512, nn(self.att_t[...], self.mixin[...]))
-
-    def joint_grad(self):
-        self.wide(self.first_t, self.hid, (2 * self.hidden + self.width) // 512, 3 * self.width // 512)
-
-    def attend_back(self, hook):
+        self.put(2 * self.hidden, nn(self.att_t[...], self.mixin[...]))
+
+    def attend_back(self, hook, done):
         lane, low = self.lane, self.low
         joint = self.hid
 
@@ -943,6 +940,9 @@
             lax.fori_loop(0, self.blocks, one, 0)
             joint[1, :, ls] = self.dk[...].astype(bf16)
             joint[2, :, ls] = self.dv[...].astype(bf16)
+            grads = jnp.concatenate([joint[0, :, ls], joint[1, :, ls], joint[2, :, ls]], axis=1)
+            self.put(2 * self.hidden + self.width + p * 384, nn(self.first_t[...], grads))
+            done(p)
             return carry
 
         lax.fori_loop(0, self.pairs, pair, 0)
@@ -1182,20 +1182,31 @@
     lax.fori_loop(0, count, one, 0)
 
 
+def hail(members, others):
+    d, f = lax.axis_index("dp"), lax.axis_index("fsdp")
+    barrier = pltpu.get_barrier_semaphore()
+    for s in range(1, members):
+        pl.semaphore_signal(barrier, inc=1, device_id={"dp": lax.rem(d + s, members)}, device_id_type=MESH)
+    for s in range(1, others):
+        pl.semaphore_signal(barrier, inc=1, device_id={"fsdp": lax.rem(f + s, others)}, device_id_type=MESH)
+
+
 def layer_kernel(sizes, members, others, *refs):
     goes_to, slot, length, joint, mix, up, down, *vectors, tokens, grads = refs[:18]
     joint_out, mix_out, up_out, down_out, tail_out, bias_out, layer_out, input_out = refs[18:26]
     (shard, weights, held, taken, back_0, back_1, back_2, back_3, total, extra, live, vec, upb, vsum, usum,
      wsend, wrecv, tsend, trecv, rsend, rrecv, local) = refs[26:48]
     back = (back_0, back_1, back_2, back_3)
-    pools = [refs[48 + 4 * n : 52 + 4 * n] for n in range(4)]
-    scratch = refs[64:]
+    pools = [refs[48 + 4 * n : 52 + 4 * n] for n in range(5)]
+    scratch = refs[68:]
     high = sizes[0]
     own, hidden = up.shape
     width = mix.shape[1]
     piece = tokens.shape[2]
     devices = members * others
     z = lax.axis_index("dp") // 2
+
+    hail(members, others)
 
     loads = [
         pltpu.make_async_copy((grads if n % 2 else tokens).at[n // 2], back[n], local.at[n]) for n in range(4)
@@ -1213,7 +1224,7 @@
     shard[:, down_at:] = down[...]
     loads[0].wait()
     permute(held.at[0], back[0], goes_to, 0, inverse=True)
-    greet(members, others)
+    pl.semaphore_wait(pltpu.get_barrier_semaphore(), members + others - 2)
 
     into = [
         Route(held.at[n], taken.at[n], local.at[4 + n], tsend.at[n], trecv.at[n], members) for n in range(4)
@@ -1251,6 +1262,9 @@
             gather.start(number)
         if number == 2:
             into[0].start_others()
+            for gather in late:
+                gather.start(0)
+    into[1].start_direct()
     vsum[...] = jnp.zeros_like(vsum)
     usum[...] = jnp.zeros_like(usum)
 
@@ -1263,15 +1277,14 @@
     def weight(start, size):
         return weights[:, :, :, :, :, pl.ds(start, size)].reshape(width, size)
 
-    def columns(k):
-        return pl.ds(pl.multiple_of(k * 512, 512), 512)
-
-    def put_first(k, value):
-        total[:, :, :, :, :, columns(k)] = value.astype(bf16).reshape(sizes + (own, 512))
-
-    def put_second(k, value):
-        value = value + total[:, :, :, :, :, columns(k)].reshape(width, 512).astype(f32)
-        total[:, :, :, :, :, columns(k)] = value.astype(bf16).reshape(sizes + (own, 512))
+    def put_first(start, value):
+        cs = pl.ds(pl.multiple_of(start, 128), value.shape[1])
+        total[:, :, :, :, :, cs] = value.astype(bf16).reshape(sizes + (own, value.shape[1]))
+
+    def put_second(start, value):
+        cs = pl.ds(pl.multiple_of(start, 128), value.shape[1])
+        value = value + total[:, :, :, :, :, cs].reshape(value.shape).astype(f32)
+        total[:, :, :, :, :, cs] = value.astype(bf16).reshape(sizes + (own, value.shape[1]))
 
     def turn(s):
         return lax.rem(z + s, high)
@@ -1295,12 +1308,6 @@
     fill_vectors(weights[:, :, :, :, :, 3 * width : mix_at].reshape(devices, own, SMALL), vec, upb)
 
     def arrive_tokens(s):
-        @pl.when(s == high - 1)
-        def _():
-            for gather in late:
-                gather.start(0)
-            into[1].start_direct()
-
         into[0].take(s)
 
     first.project(turn, arrive_tokens)
@@ -1347,8 +1354,7 @@
     first.down_grad()
     first.up_grad()
     first.mix_grad()
-    first.attend_back(nothing)
-    first.joint_grad()
+    first.attend_back(nothing, nothing)
     first.first_back(turn, nothing)
     returns[1].start()
 
@@ -1366,12 +1372,22 @@
         up_out[...] = value[:, :hidden]
         mix_out[...] = value[:, hidden:]
 
-    downs, ups, rest, last = (
+    def emit_joint(start, count):
+        def emit(value):
+            for p in range(count):
+                for j in range(3):
+                    spot = j * width + (start + p) * 128
+                    joint_out[:, spot : spot + 128] = value[:, p * 384 + j * 128 : p * 384 + j * 128 + 128]
+        return emit
+
+    joint_at, pairs = 2 * hidden + width, width // 128
+    downs, ups, rest, rest_last, last = (
         Exchange(source, cs, wide_first, emit, pools[n], rsend.at[n], rrecv.at[n], high)
         for n, (source, cs, wide_first, emit) in enumerate((
             (total, pl.ds(0, hidden), True, emit_to(down_out)),
             (total, pl.ds(hidden, hidden + width), False, emit_pair),
-            (total, pl.ds(2 * hidden + width, 3 * width), False, emit_to(joint_out)),
+            (total, pl.ds(joint_at, 384 * (pairs - 1)), False, emit_joint(0, pairs - 1)),
+            (total, pl.ds(joint_at + 384 * (pairs - 1), 384), False, emit_joint(pairs - 1, 1)),
             (extra, pl.ds(0, SMALL), False, emit_tail),
         ))
     )
@@ -1403,16 +1419,16 @@
 
     plan_back = [
         (0, step(downs, 0)), (1, step(ups, 0)), (3, result(0)), (6, step(downs, 1)), (8, step(ups, 1)),
-        (9, result(1)), (10, step(downs, 2)), (12, step(ups, 2)), (15, step(downs, 3)),
+        (9, result(1)), (10, step(downs, 2)), (12, step(ups, 2)), (14, step(rest, 0)), (15, step(downs, 3)),
     ]
-    second.attend_back(lambda h: at_points(h, plan_back))
+    second.attend_back(
+        lambda h: at_points(h, plan_back), lambda p: at_points(p, [(pairs - 2, rest.start), (pairs - 1, rest_last.start)]))
 
     def send_grads(s):
         returns[3].give(lax.rem(s + 1, high))
+        at_points(s, [(0, step(rest_last, 0)), (high - 1, step(rest, 1))])
 
     second.first_back(turn_last, send_grads)
-    second.joint_grad()
-    rest.start()
     turned = jnp.concatenate([vsum[...], jnp.zeros((120, width), f32)], axis=0).T
     extra[:, :, :, :, :, :128] = turned.astype(bf16).reshape(sizes + (own, 128))
     for n in range(devices):
@@ -1420,16 +1436,19 @@
         part = usum[:, 128 * (n // 2) : 128 * (n // 2) + 128]
         extra[a, b, c, e, :, 128:] = jnp.broadcast_to(part, (own, 128)).astype(bf16)
     last.start()
-    rest.step(0)
+    rest_last.step(1)
     last.step(0)
     returns[3].start_others()
+    rest.step(2)
     ups.step(3)
+    rest_last.step(2)
+    last.step(1)
+    last.step(2)
     result(2)()
-    for number in range(1, 4):
-        rest.step(number)
-        last.step(number)
+    for item in (rest, rest_last, last):
+        item.step(3)
     result(3)()
-    for item in gathers + returns + [downs, ups, rest, last]:
+    for item in gathers + returns + [downs, ups, rest, rest_last, last]:
         item.wait_sent()
     for item in results:
         item.wait()
@@ -1447,7 +1466,7 @@
     dma = pltpu.SemaphoreType.DMA
     smem = pl.BlockSpec(memory_space=pltpu.SMEM)
     pools = []
-    for count in (hidden, hidden + width, 3 * width, SMALL):
+    for count in (hidden, hidden + width, 3 * width - 384, 384, SMALL):
         pools += exchange_scratch(high, own, count)
     shapes = [(own, 3 * width), (own, width), (own, hidden), (own, hidden), (8, own), (1, 2 * SMALL // 8)]
     blocks = pltpu.VMEM((4, members, piece, width), bf16)
@@ -1468,7 +1487,7 @@
             pltpu.VMEM((8, width), f32), pltpu.VMEM((1, hidden), f32),
             pltpu.VMEM((8, width), f32), pltpu.VMEM((1, hidden), f32),
             dma((7, slots)), dma((7, slots)), dma((8, members)), dma((8, members)),
-            dma((4, high + 2)), dma((4, high + 2)), dma((23,)),
+            dma((5, high + 2)), dma((5, high + 2)), dma((23,)),
         ] + pools + layer_scratch(rows, width, hidden),
         compiler_params=pltpu.CompilerParams(
             collective_id=2, has_side_effects=True, vmem_limit_bytes=67_043_328),

time: 285 us -> 284 us (level)
  no operation moved by 1% of the time
where the time goes in v5:
time: 284 us
  Pallas kernels  274 us (96%)
  local copies, waits for them, and re-layouts  9.13 us (3%)
    pallas_call x1, Pallas kernels, layer_call(): pl.pallas_call(functools.partial(layer_kernel, sizes, members, others), o...  274 us
    unnamed x19, local copies, waits for them, and re-layouts  7.62 us

profile of v5, /device:TPU:0, one launch (start us, length us, event | category | flops | bytes accessed | tf_op | source)
XLA Modules:
  0.0 283.6 jit_solution(11418166871999891881)
XLA Ops:
  0.7 273.8 %layer.1 = (f32[16,1536]{1,0:T(8,128)}, f32[16,512]{1,0:T(8,128)}, f32[16,2048]{1,0:T(8,128)}, f32[16,2048]{1,0:T(8,128)}, f32[8,16]{1,0:T(8,128)}, /*index=5*/f...) custom-call(s32[2,8]{1,0:T(2,128)} %bitcast.41, s32[2,8]{1,0:T(2,128)} %bitcast.42, ...), custom_call_target="tpu_custom_call" | custom-call | tf_op jit(solution)/shard_map/layer/pallas_call | solution.py:1473
  274.4 1.5 slice_bitcast_fusion
  276.0 0.0 copy-start
  276.0 3.2 %copy.40 = bf16[2,1024,512]{2,1,0:T(8,128)(2,1)} copy(bf16[2,1024,512]{2,1,0:T(8,128)(2,1)} %bitcast.36) | data formatting | bytes 4194304
  279.1 0.0 copy-done
  279.2 0.0 copy-start.3
  279.2 0.0 copy-start.4
  279.2 0.0 copy-start.2
  279.2 0.0 copy-start.5
  279.2 0.0 copy-start.1
  279.2 1.3 copy.41
  280.5 0.0 copy-done.3
  280.5 0.6 copy.42
  281.1 0.0 copy-done.4
  281.1 0.6 copy.43
  281.8 0.0 copy-done.2
  281.8 0.7 copy.44
  282.4 0.0 copy-done.5
  282.4 0.5 copy.45
  282.9 0.0 copy-done.1
  282.9 0.7 copy.46
Async XLA Ops:
  276.0 3.2 %copy-start = (bf16[2,8,128,512]{3,2,1,0:T(8,128)(2,1)S(1)}, bf16[2,8,128,512]{3,2,1,0:T(8,128)(2,1)}, u32[]{:S(2)}) copy-start(bf16[2,8,128,512]{3,2,1,0:T(8,128)(2,1)} %get-tuple-element.24) | copy-start | bytes 6291460
  279.2 1.4 copy-start.3
  279.2 2.0 copy-start.4
  279.2 2.6 copy-start.2
  279.2 3.3 %copy-start.5 = (f32[1,64]{1,0:T(1,128)S(1)}, f32[1,64]{1,0:T(1,128)}, u32[]{:S(2)}) copy-start(f32[1,64]{1,0:T(1,128)} %get-tuple-element.29) | copy-start | bytes 772
  279.2 3.8 %copy-start.1 = (f32[16,2048]{1,0:T(8,128)S(1)}, f32[16,2048]{1,0:T(8,128)}, u32[]{:S(2)}) copy-start(f32[16,2048]{1,0:T(8,128)} %get-tuple-element.30) | copy-start | bytes 393220
